TPU v7x, 32 devices: a whole 2x2x4 slice. The times are simulated.
32 devices in a mesh: boxes: 32 (over z, y, x, core).
Axes of the slice: x: 2, y: 2, z: 4, core: 2. Of those that a mesh axis runs over, the one named last changes fastest.
Arguments:
- conserved: float32 [32, 5, 16, 32, 128], P('boxes'), may hold values from -6 to 6
- volume_fraction: float32 [32, 16, 32, 128], P('boxes'), may hold values from 0.05 to 1
- cut_mask: int32 [32, 16, 32, 128], P('boxes'), may hold values 0 or 1
- merge_code: int32 [32, 16, 32, 128], P('boxes'), may hold values from 0 to 26
Outputs:
- redistributed: float32 [32, 5, 16, 32, 128], P('boxes')
All inputs are finite; a program needn't handle non-finite values. No bound on the sum of `cut_mask` on one device may be relied on, other than what follows from the above.
Results may differ from a plain program's by a relative error of at most 0.0003.
Values sent between devices are 32-bit elements; how exact they have to be, the bound alone decides.
No kernel may reach another device: no remote copies, remote signals or barrier semaphores. Data moves between devices by JAX's collectives and lax.ppermute only.
A program may use at most 64 MiB of HBM per device.

v0:
```python
import jax
import jax.numpy as jnp
from jax import lax
from jax.sharding import PartitionSpec as P

NBY = 4
NBZ = 4


OFFSETS = [
    (first, second, third)
    for first in (-1, 0, 1)
    for second in (-1, 0, 1)
    for third in (-1, 0, 1)
    if (first, second, third) != (0, 0, 0)
]


def shifted(shard, axis, by):
    devices = lax.axis_size(axis)
    pairs = [(i, i + by) for i in range(devices) if 0 <= i + by < devices]
    return lax.ppermute(shard, axis, pairs)


def decode(code_field):
    sign_parts = (code_field // 9 - 1, code_field // 3 % 3 - 1, code_field % 3 - 1)
    members = []
    for offset in OFFSETS:
        inside = jnp.ones(code_field.shape, jnp.bool_)
        for direction, component in zip(sign_parts, offset):
            if component != 0:
                inside = inside & (direction == component)
        members.append(inside)
    return members


def placed(values, offset):
    spread = [(0, 0)] * (values.ndim - 3) + [(1 + component, 1 - component) for component in offset]
    return jnp.pad(values, spread)


def count_members(members):
    running = placed(jnp.ones(members[0].shape, jnp.float32), (0, 0, 0))
    for offset, inside in zip(OFFSETS, members):
        running = running + placed(inside.astype(jnp.float32), offset)
    return running


def window(weighted, offset, interior):
    starts = [0] + [1 + component for component in offset]
    limits = [weighted.shape[0]] + [anchor + extent for anchor, extent in zip(starts[1:], interior)]
    return lax.slice(weighted, starts, limits)


def neighbour_average(weighted, members):
    interior = [extent - 2 for extent in weighted.shape[1:]]
    running = window(weighted, (0, 0, 0), interior)
    for offset, inside in zip(OFFSETS, members):
        running = running + jnp.where(inside[None], window(weighted, offset, interior), 0.0)
    return running[1:] / running[0:1]


def spread_back(average, members):
    running = placed(average, (0, 0, 0))
    for offset, inside in zip(OFFSETS, members):
        running = running + placed(jnp.where(inside[None], average, 0.0), offset)
    return running


def exchange_rims(values, spatial_dim, stride, layers, low_edge, high_edge):
    extent = values.shape[spatial_dim]
    lower_rim = lax.slice_in_dim(values, 0, layers, axis=spatial_dim)
    upper_rim = lax.slice_in_dim(values, extent - layers, extent, axis=spatial_dim)
    from_below = shifted(upper_rim, "boxes", stride)
    from_above = shifted(lower_rim, "boxes", -stride)
    from_below = jnp.where(low_edge, 0.0, from_below)
    from_above = jnp.where(high_edge, 0.0, from_above)
    return jnp.concatenate([from_below, values, from_above], axis=spatial_dim)


def fill_ghosts(values, layers, edges):
    strides = (NBY * NBZ, NBZ, 1)
    for spatial_dim in (3, 2, 1):
        low_edge, high_edge = edges[spatial_dim - 1]
        values = exchange_rims(
            values, spatial_dim, strides[spatial_dim - 1], layers, low_edge, high_edge
        )
    return values


def return_rims(values, spatial_dim, stride, low_edge, high_edge):
    extent = values.shape[spatial_dim]
    lower_ghost = lax.slice_in_dim(values, 0, 1, axis=spatial_dim)
    upper_ghost = lax.slice_in_dim(values, extent - 1, extent, axis=spatial_dim)
    from_below = shifted(upper_ghost, "boxes", stride)
    from_above = shifted(lower_ghost, "boxes", -stride)
    from_below = jnp.where(low_edge, 0.0, from_below)
    from_above = jnp.where(high_edge, 0.0, from_above)
    leading = lax.slice_in_dim(values, 1, 2, axis=spatial_dim) + from_below
    middle = lax.slice_in_dim(values, 2, extent - 2, axis=spatial_dim)
    trailing = lax.slice_in_dim(values, extent - 2, extent - 1, axis=spatial_dim) + from_above
    return jnp.concatenate([leading, middle, trailing], axis=spatial_dim)


def sum_ghosts(values, edges):
    strides = (NBY * NBZ, NBZ, 1)
    for spatial_dim in (1, 2, 3):
        low_edge, high_edge = edges[spatial_dim - 1]
        values = return_rims(values, spatial_dim, strides[spatial_dim - 1], low_edge, high_edge)
    return values


def per_device(conserved, volume_fraction, cut_mask, merge_code):
    fields = conserved[0]
    fraction = volume_fraction[0]
    code_field = jnp.where(cut_mask[0] == 1, merge_code[0], 13)
    position = lax.axis_index("boxes")
    box_x = position // (NBY * NBZ)
    box_y = position // NBZ % NBY
    box_z = position % NBZ
    edges = (
        (box_x == 0, box_x == lax.axis_size("boxes") // (NBY * NBZ) - 1),
        (box_y == 0, box_y == NBY - 1),
        (box_z == 0, box_z == NBZ - 1),
    )
    members = decode(code_field)
    counts_ghost = count_members(members)[None]
    counts = sum_ghosts(counts_ghost, edges)[0]
    weight = fraction / counts
    packed = jnp.concatenate([weight[None], weight[None] * fields], axis=0)
    weighted = fill_ghosts(packed, 1, edges)
    average = neighbour_average(weighted, members)
    deposits = spread_back(average, members)
    gathered = sum_ghosts(deposits, edges)
    return (gathered / counts[None])[None]


def solution(mesh):
    return jax.shard_map(
        per_device,
        mesh=mesh,
        in_specs=(
            P("boxes", None, None, None, None),
            P("boxes", None, None, None),
            P("boxes", None, None, None),
            P("boxes", None, None, None),
        ),
        out_specs=P("boxes", None, None, None, None),
        check_vma=False,
    )
```

profile of v0, /device:TPU:5, one launch (start us, length us, event | category | flops | bytes accessed | tf_op | source)
XLA Modules:
  0.0 217.8 jit_solution(16279148314739238653)
XLA Ops:
  0.0 2.5 %and_bitcast_fusion.15 = (pred[16,32,128]{2,0,1:T(8,128)(4,1)}, pred[1,16,32,128]{3,1,2,0:T(8,128)(4,1)S(1)}, pred[1,16,32,128]{3,1,2,0:T(8,128)(4,1)S(1)}, pred...) fusion(s32[1,16,32,128]{3,2,1,0:T(8,128)} %param.7, ...), kind=kLoop, calls=%fused_computation.153 | loop fusion | flops 2228224 | bytes 1441792 | tf_op jit(solution)/shard_map/jit(_where)/broadcast_in_dim | solution.py:59
  4.2 3.8 %add_bitcast_fusion = f32[1,18,34,130]{3,1,2,0:T(8,128)S(1)} fusion(f32[16,32,128]{2,0,1:T(8,128)S(1)} %broadcast_in_dim.486, pred[16,32,128]{2,0,1:T(8,128)(4,1)S(1)} %and.272, pred[16,32,128]{2,0,1:T(8,128)(4,1)S(1)} %get-tuple-element.36, pred[16,32,128]{2,0,1:T(8,128)(4,1)S(1)} %get-tuple-element.35, pred[16,32,128]{2,0,1:T(8,128)(4,1)S(1)} %get-tuple-element.113, ...), kind=kLoop, calls=%fused_computation.74 | loop fusion | flops 4137120 | bytes 2284320 | tf_op jit(solution)/shard_map/broadcast_in_dim | solution.py:127
  8.0 4.2 %collective-permute-start = (f32[1,1,34,130]{3,1,2,0:T(1,128)S(1)}, f32[1,1,34,130]{3,1,2,0:T(1,128)S(1)}, u32[]{:S(2)}, u32[]{:S(2)}) collective-permute-start(f32[1,1,34,130]{3,1,2,0:T(1,128)S(1)} %slice.283), channel_id=1, source_target_pairs={{0,16},{1,17},{2,18},{3,19},{4,20},{5,21},{6,22},{7,23},{8,24},{9,... | collective-permute-start | bytes 53048 | tf_op jit(solution)/shard_map/ppermute | solution.py:22
  14.7 4.2 %collective-permute-done.1 = f32[1,1,34,130]{3,1,2,0:T(1,128)S(1)} collective-permute-done((f32[1,1,34,130]{3,1,2,0:T(1,128)S(1)}, f32[1,1,34,130]{3,1,2,0:T(1,128)S(1)}, u32[]{:S(2)}, u32[]{:S(2)}) %collective-permute-start.1) | collective-permute-done | bytes 17712 | tf_op jit(solution)/shard_map/ppermute | solution.py:22
  19.0 3.2 %collective-permute-start.2 = (f32[1,16,1,130]{3,1,2,0:T(8,128)S(1)}, f32[1,16,1,130]{3,1,2,0:T(8,128)S(1)}, u32[]{:S(2)}, u32[]{:S(2)}) collective-permute-start(f32[1,16,1,130]{3,1,2,0:T(8,128)S(1)} %pad_maximum_fusion.21), channel_id=1, source_target_pairs={{0,4},{1,5},{2,6},{3,7},{4,8},{5,9},{6,10},{7,11},{8,12},{9,13},{1... | collective-permute-start | bytes 24968 | tf_op jit(solution)/shard_map/ppermute | solution.py:22
  25.9 3.0 %collective-permute-done.3 = f32[1,16,1,130]{3,1,2,0:T(8,128)S(1)} collective-permute-done((f32[1,16,1,130]{3,1,2,0:T(8,128)S(1)}, f32[1,16,1,130]{3,1,2,0:T(8,128)S(1)}, u32[]{:S(2)}, u32[]{:S(2)}) %collective-permute-start.3) | collective-permute-done | bytes 8352 | tf_op jit(solution)/shard_map/ppermute | solution.py:22
  29.2 8.0 %collective-permute-start.4 = (f32[1,16,32,1]{3,2,1,0:T(8,128)S(1)}, f32[1,16,32,1]{3,2,1,0:T(8,128)S(1)}, u32[]{:S(2)}, u32[]{:S(2)}) collective-permute-start(f32[1,16,32,1]{3,2,1,0:T(8,128)S(1)} %slice.289), channel_id=1, source_target_pairs={{0,1},{1,2},{2,3},{3,4},{4,5},{5,6},{6,7},{7,8},{8,9},{9,10},{10,1... | collective-permute-start | bytes 6152 | tf_op jit(solution)/shard_map/ppermute | solution.py:22
  37.2 3.3 %collective-permute-done.4 = f32[1,16,32,1]{3,2,1,0:T(8,128)S(1)} collective-permute-done((f32[1,16,32,1]{3,2,1,0:T(8,128)S(1)}, f32[1,16,32,1]{3,2,1,0:T(8,128)S(1)}, u32[]{:S(2)}, u32[]{:S(2)}) %collective-permute-start.4) | collective-permute-done | bytes 2080 | tf_op jit(solution)/shard_map/ppermute | solution.py:22
  40.6 4.2 %collective-permute-start.5 = (f32[1,16,32,1]{3,2,1,0:T(8,128)S(1)}, f32[1,16,32,1]{3,2,1,0:T(8,128)S(1)}, u32[]{:S(2)}, u32[]{:S(2)}) collective-permute-start(f32[1,16,32,1]{3,2,1,0:T(8,128)S(1)} %get-tuple-element.85), channel_id=1, source_target_pairs={{1,0},{2,1},{3,2},{4,3},{5,4},{6,5},{7,6},{8,7},{9,8},{10,9},{11,1... | collective-permute-start | bytes 6152 | tf_op jit(solution)/shard_map/ppermute | solution.py:22
  46.2 2.8 %collective-permute-done.5 = f32[1,16,32,1]{3,2,1,0:T(8,128)S(1)} collective-permute-done((f32[1,16,32,1]{3,2,1,0:T(8,128)S(1)}, f32[1,16,32,1]{3,2,1,0:T(8,128)S(1)}, u32[]{:S(2)}, u32[]{:S(2)}) %collective-permute-start.5) | collective-permute-done | bytes 2080 | tf_op jit(solution)/shard_map/ppermute | solution.py:22
  52.9 2.6 %copy.352 = f32[6,16,32,1]{2,1,3,0:T(8,128)} copy(f32[6,16,32,1]{3,2,1,0:T(8,128)} %get-tuple-element.51) | data formatting | bytes 24576
  59.8 2.4 %collective-permute-start.7 = (f32[6,16,32,1]{2,1,3,0:T(8,128)}, f32[6,16,32,1]{2,1,3,0:T(8,128)}, u32[]{:S(2)}, u32[]{:S(2)}) collective-permute-start(f32[6,16,32,1]{2,1,3,0:T(8,128)} %copy.353), channel_id=1, source_target_pairs={{1,0},{2,1},{3,2},{4,3},{5,4},{6,5},{7,6},{8,7},{9,8},{10,9},{11,1... | collective-permute-start | bytes 36872 | tf_op jit(solution)/shard_map/ppermute | solution.py:22
  62.2 2.6 %copy.332 = f32[6,16,32,1]{3,1,2,0:T(8,128)} copy(f32[6,16,32,1]{2,1,3,0:T(8,128)} %collective-permute-done.6) | data formatting | bytes 24576 | tf_op jit(solution)/shard_map/ppermute | solution.py:22
  67.3 2.6 %copy.334 = f32[6,16,32,1]{3,1,2,0:T(8,128)} copy(f32[6,16,32,1]{2,1,3,0:T(8,128)} %collective-permute-done.7) | data formatting | bytes 24576 | tf_op jit(solution)/shard_map/ppermute | solution.py:22
  71.6 2.5 %collective-permute-start.8 = (f32[6,16,1,130]{3,1,2,0:T(8,128)S(1)}, f32[6,16,1,130]{3,1,2,0:T(8,128)S(1)}, u32[]{:S(2)}, u32[]{:S(2)}) collective-permute-start(f32[6,16,1,130]{3,1,2,0:T(8,128)S(1)} %get-tuple-element.43), channel_id=1, source_target_pairs={{0,4},{1,5},{2,6},{3,7},{4,8},{5,9},{6,10},{7,11},{8,12},{9,13},{1... | collective-permute-start | bytes 149768 | tf_op jit(solution)/shard_map/ppermute | solution.py:22
  75.5 3.0 %collective-permute-start.9 = (f32[6,16,1,130]{3,1,2,0:T(8,128)S(1)}, f32[6,16,1,130]{3,1,2,0:T(8,128)S(1)}, u32[]{:S(2)}, u32[]{:S(2)}) collective-permute-start(f32[6,16,1,130]{3,1,2,0:T(8,128)S(1)} %get-tuple-element.44), channel_id=1, source_target_pairs={{4,0},{5,1},{6,2},{7,3},{8,4},{9,5},{10,6},{11,7},{12,8},{13,9},{1... | collective-permute-start | bytes 149768 | tf_op jit(solution)/shard_map/ppermute | solution.py:22
  78.5 3.2 %collective-permute-done.9 = f32[6,16,1,130]{3,1,2,0:T(8,128)S(1)} collective-permute-done((f32[6,16,1,130]{3,1,2,0:T(8,128)S(1)}, f32[6,16,1,130]{3,1,2,0:T(8,128)S(1)}, u32[]{:S(2)}, u32[]{:S(2)}) %collective-permute-start.9) | collective-permute-done | bytes 49952 | tf_op jit(solution)/shard_map/ppermute | solution.py:22
  84.4 4.7 %maximum_maximum_fusion.1 = (f32[6,16,33,130]{3,1,2,0:T(8,128)}, f32[6,16,33,130]{3,1,2,0:T(8,128)}) fusion(f32[6,16,32,1]{3,1,2,0:T(8,128)S(1)} %broadcast_select_fusion, f32[6,16,32,128]{3,1,2,0:T(8,128)S(1)} %copy.336, f32[6,16,32,1]{3,1,2,0:T(8,128)S(1)} %broadcast_select_fusion.1, f32[6,16,1,130]{3,1,2,0:T(8,128)S(1)} %broadcast_select_fusion.35, ...), kind=kLoop, calls=%fused_computation.3 | loop fusion | flops 2471040 | bytes 4992000 | tf_op jit(solution)/shard_map/concatenate | solution.py:78
  90.6 10.8 %collective-permute-done.11 = f32[6,1,34,130]{3,1,2,0:T(1,128)S(1)} collective-permute-done((f32[6,1,34,130]{3,1,2,0:T(1,128)S(1)}, f32[6,1,34,130]{3,1,2,0:T(1,128)S(1)}, u32[]{:S(2)}, u32[]{:S(2)}) %collective-permute-start.11) | collective-permute-done | bytes 106112 | tf_op jit(solution)/shard_map/ppermute | solution.py:22
  101.7 6.3 %maximum_maximum_fusion = (f32[6,17,34,130]{3,1,2,0:T(8,128)S(1)}, f32[6,17,34,130]{3,1,2,0:T(8,128)S(1)}) fusion(f32[6,16,1,130]{3,1,2,0:T(8,128)S(1)} %broadcast_select_fusion.34, f32[6,16,32,1]{3,1,2,0:T(8,128)S(1)} %broadcast_select_fusion, f32[6,16,32,128]{3,1,2,0:T(8,128)} %copy-done, f32[6,16,32,1]{3,1,2,0:T(8,128)} %copy-done.1, ...), kind=kLoop, calls=%fused_computation | loop fusion | flops 4508400 | bytes 5516160 | tf_op jit(solution)/shard_map/concatenate | solution.py:78
  108.2 13.5 %fusion.2 = f32[6,16,32,128]{3,1,2,0:T(8,128)} fusion(f32[6,17,34,130]{3,1,2,0:T(8,128)S(1)} %get-tuple-element.38, f32[6,16,33,130]{3,1,2,0:T(8,128)} %get-tuple-element.42, f32[6,16,32,1]{3,1,2,0:T(8,128)} %copy-done.2, f32[6,16,32,128]{3,1,2,0:T(8,128)} %copy-done, f32[6,16,32,1]{3,1,2,0:T(8,128)} %copy-done.1, f32[6,16,33,130]{3,1,2,0:T(8,128)} %get-tuple-element.41, ...), kind=kLoop, calls=%fused_computation.15 | loop fusion | flops 21233664 | bytes 42622976 | tf_op jit(solution)/shard_map/add | solution.py:59
  124.5 2.9 %broadcast_select_fusion.25 = (f32[5,16,32,128]{3,1,2,0:T(8,128)S(1)}, f32[5,16,32,128]{3,1,2,0:T(8,128)S(1)}, f32[5,16,32,128]{3,1,2,0:T(8,128)}, f32[5,16,32,1...) fusion(f32[5,16,32,128]{3,1,2,0:T(8,128)S(1)} %get-tuple-element.6, ...), kind=kLoop, calls=%fused_computation.100 | loop fusion | flops 2293760 | bytes 10944512 | tf_op jit(solution)/shard_map/jit(_where)/select_n | solution.py:66
  127.4 4.1 %broadcast_select_fusion.26 = (f32[5,16,32,128]{3,1,2,0:T(8,128)S(1)}, f32[5,16,32,128]{3,1,2,0:T(8,128)S(1)}, f32[5,16,32,128]{3,1,2,0:T(8,128)S(1)}, f32[5,16,...) fusion(f32[5,16,32,128]{3,1,2,0:T(8,128)S(1)} %get-tuple-elemen, ...), kind=kLoop, calls=%fused_computation.101 | loop fusion | flops 5898240 | bytes 26083328 | tf_op jit(solution)/shard_map/jit(_where)/select_n | solution.py:66
  131.6 18.6 %pad_add_fusion = f32[5,18,34,130]{3,1,2,0:T(8,128)S(1)} fusion(f32[5,16,32,128]{3,1,2,0:T(8,128)} %get-tuple-element.77, f32[5,16,32,128]{3,1,2,0:T(8,128)S(1)} %get-tuple-element.54, f32[5,16,32,128]{3,1,2,0:T(8,128)S(1)} %get-tuple-element.55, f32[5,16,32,128]{3,1,2,0:T(8,128)S(1)} %get-tuple-element.56, f32[5,16,32,128]{3,1,2,0:T(8,128)S(1)} %get-tuple-element.57, ...), kind=kLoop, calls=%fused_computation.2 | loop fusion | flops 10342800 | bytes 36980640 | tf_op jit(solution)/shard_map/add | solution.py:66
  151.6 2.4 %collective-permute-done.12 = f32[5,1,34,130]{3,1,2,0:T(1,128)S(1)} collective-permute-done((f32[5,1,34,130]{3,1,2,0:T(1,128)S(1)}, f32[5,1,34,130]{3,1,2,0:T(1,128)S(1)}, u32[]{:S(2)}, u32[]{:S(2)}) %collective-permute-start.12) | collective-permute-done | bytes 88432 | tf_op jit(solution)/shard_map/ppermute | solution.py:22
  156.1 5.3 %collective-permute-done.13 = f32[5,1,34,130]{3,1,2,0:T(1,128)S(1)} collective-permute-done((f32[5,1,34,130]{3,1,2,0:T(1,128)S(1)}, f32[5,1,34,130]{3,1,2,0:T(1,128)S(1)}, u32[]{:S(2)}, u32[]{:S(2)}) %collective-permute-start.13) | collective-permute-done | bytes 88432 | tf_op jit(solution)/shard_map/ppermute | solution.py:22
  163.6 4.5 %collective-permute-done.14 = f32[5,16,1,130]{3,1,2,0:T(8,128)S(1)} collective-permute-done((f32[5,16,1,130]{3,1,2,0:T(8,128)S(1)}, f32[5,16,1,130]{3,1,2,0:T(8,128)S(1)}, u32[]{:S(2)}, u32[]{:S(2)}) %collective-permute-start.14) | collective-permute-done | bytes 41632 | tf_op jit(solution)/shard_map/ppermute | solution.py:22
  179.5 9.5 %collective-permute-start.16 = (f32[5,16,32,1]{2,1,3,0:T(8,128)S(1)}, f32[5,16,32,1]{2,1,3,0:T(8,128)S(1)}, u32[]{:S(2)}, u32[]{:S(2)}) collective-permute-start(f32[5,16,32,1]{2,1,3,0:T(8,128)S(1)} %copy.339), channel_id=1, source_target_pairs={{0,1},{1,2},{2,3},{3,4},{4,5},{5,6},{6,7},{7,8},{8,9},{9,10},{10,1... | collective-permute-start | bytes 30728 | tf_op jit(solution)/shard_map/ppermute | solution.py:22
  191.7 3.3 %slice_add_fusion.1 = (f32[5,16,32,1]{3,1,2,0:T(8,128)}, f32[5,16,32,1]{3,1,2,0:T(8,128)}) fusion(f32[5,16,32,1]{3,1,2,0:T(8,128)} %copy.342, f32[5,16,32,130]{3,1,2,0:T(8,128)S(1)} %pad_maximum_fusion.4), kind=kLoop, calls=%fused_computation.70 | loop fusion | flops 2560 | bytes 51200 | tf_op jit(solution)/shard_map/add | solution.py:99
  196.8 4.6 %collective-permute-start.17 = (f32[5,16,32,1]{2,1,3,0:T(8,128)S(1)}, f32[5,16,32,1]{2,1,3,0:T(8,128)S(1)}, u32[]{:S(2)}, u32[]{:S(2)}) collective-permute-start(f32[5,16,32,1]{2,1,3,0:T(8,128)S(1)} %copy.344), channel_id=1, source_target_pairs={{1,0},{2,1},{3,2},{4,3},{5,4},{6,5},{7,6},{8,7},{9,8},{10,9},{11,1... | collective-permute-start | bytes 30728 | tf_op jit(solution)/shard_map/ppermute | solution.py:22
  208.4 2.6 %slice_add_fusion = f32[5,16,32,1]{3,1,2,0:T(8,128)} fusion(f32[5,16,32,1]{3,1,2,0:T(8,128)} %copy.347, f32[5,16,32,130]{3,1,2,0:T(8,128)S(1)} %pad_maximum_fusion.4), kind=kLoop, calls=%fused_computation.68 | loop fusion | flops 2560 | bytes 30720 | tf_op jit(solution)/shard_map/add | solution.py:101
  214.7 3.1 %maximum_divide_fusion = f32[1,5,16,32,128]{4,3,2,1,0:T(8,128)} fusion(f32[1,5,16,32,1]{4,3,2,1,0:T(8,128)} %copy.351, f32[1,5,16,32,126]{4,3,2,1,0:T(8,128)S(1)} %copy-done.4, f32[1,5,16,32,1]{4,3,2,1,0:T(8,128)S(1)} %copy-done.5, f32[16,32,128]{2,1,0:T(8,128)S(1)} %copy-done.15), kind=kLoop, calls=%fused_computation.72 | loop fusion | flops 983040 | bytes 2883584 | tf_op jit(solution)/shard_map/div | solution.py:135
  (140 shorter events, 62.4 us)
Async XLA Ops:
  2.5 105.6 %copy-start.6 = (pred[1,16,32,128]{3,1,2,0:T(8,128)(4,1)}, pred[1,16,32,128]{3,1,2,0:T(8,128)(4,1)S(1)}, u32[]{:S(2)}) copy-start(pred[1,16,32,128]{3,1,2,0:T(8,128)(4,1)S(1)} %get-tuple-element.10) | copy-start | bytes 196612
  2.5 105.6 %copy-start.7 = (pred[1,16,32,128]{3,1,2,0:T(8,128)(4,1)}, pred[1,16,32,128]{3,1,2,0:T(8,128)(4,1)S(1)}, u32[]{:S(2)}) copy-start(pred[1,16,32,128]{3,1,2,0:T(8,128)(4,1)S(1)} %get-tuple-element.8) | copy-start | bytes 196612
  8.0 5.2 %collective-permute-start = (f32[1,1,34,130]{3,1,2,0:T(1,128)S(1)}, f32[1,1,34,130]{3,1,2,0:T(1,128)S(1)}, u32[]{:S(2)}, u32[]{:S(2)}) collective-permute-start(f32[1,1,34,130]{3,1,2,0:T(1,128)S(1)} %slice.283), channel_id=1, source_target_pairs={{0,16},{1,17},{2,18},{3,19},{4,20},{5,21},{6,22},{7,23},{8,24},{9,... | collective-permute-start | bytes 53048 | tf_op jit(solution)/shard_map/ppermute | solution.py:22
  13.4 5.6 %collective-permute-start.1 = (f32[1,1,34,130]{3,1,2,0:T(1,128)S(1)}, f32[1,1,34,130]{3,1,2,0:T(1,128)S(1)}, u32[]{:S(2)}, u32[]{:S(2)}) collective-permute-start(f32[1,1,34,130]{3,1,2,0:T(1,128)S(1)} %get-tuple-element.79), channel_id=1, source_target_pairs={{16,0},{17,1},{18,2},{19,3},{20,4},{21,5},{22,6},{23,7},{24,8},{25... | collective-permute-start | bytes 53048 | tf_op jit(solution)/shard_map/ppermute | solution.py:22
  19.0 4.5 %collective-permute-start.2 = (f32[1,16,1,130]{3,1,2,0:T(8,128)S(1)}, f32[1,16,1,130]{3,1,2,0:T(8,128)S(1)}, u32[]{:S(2)}, u32[]{:S(2)}) collective-permute-start(f32[1,16,1,130]{3,1,2,0:T(8,128)S(1)} %pad_maximum_fusion.21), channel_id=1, source_target_pairs={{0,4},{1,5},{2,6},{3,7},{4,8},{5,9},{6,10},{7,11},{8,12},{9,13},{1... | collective-permute-start | bytes 24968 | tf_op jit(solution)/shard_map/ppermute | solution.py:22
  23.5 5.4 %collective-permute-start.3 = (f32[1,16,1,130]{3,1,2,0:T(8,128)S(1)}, f32[1,16,1,130]{3,1,2,0:T(8,128)S(1)}, u32[]{:S(2)}, u32[]{:S(2)}) collective-permute-start(f32[1,16,1,130]{3,1,2,0:T(8,128)S(1)} %get-tuple-element.83), channel_id=1, source_target_pairs={{4,0},{5,1},{6,2},{7,3},{8,4},{9,5},{10,6},{11,7},{12,8},{13,9},{1... | collective-permute-start | bytes 24968 | tf_op jit(solution)/shard_map/ppermute | solution.py:22
  29.2 11.3 %collective-permute-start.4 = (f32[1,16,32,1]{3,2,1,0:T(8,128)S(1)}, f32[1,16,32,1]{3,2,1,0:T(8,128)S(1)}, u32[]{:S(2)}, u32[]{:S(2)}) collective-permute-start(f32[1,16,32,1]{3,2,1,0:T(8,128)S(1)} %slice.289), channel_id=1, source_target_pairs={{0,1},{1,2},{2,3},{3,4},{4,5},{5,6},{6,7},{7,8},{8,9},{9,10},{10,1... | collective-permute-start | bytes 6152 | tf_op jit(solution)/shard_map/ppermute | solution.py:22
  40.6 8.4 %collective-permute-start.5 = (f32[1,16,32,1]{3,2,1,0:T(8,128)S(1)}, f32[1,16,32,1]{3,2,1,0:T(8,128)S(1)}, u32[]{:S(2)}, u32[]{:S(2)}) collective-permute-start(f32[1,16,32,1]{3,2,1,0:T(8,128)S(1)} %get-tuple-element.85), channel_id=1, source_target_pairs={{1,0},{2,1},{3,2},{4,3},{5,4},{6,5},{7,6},{8,7},{9,8},{10,9},{11,1... | collective-permute-start | bytes 6152 | tf_op jit(solution)/shard_map/ppermute | solution.py:22
  46.0 28.1 %copy-start.11 = (pred[1,16,32,128]{3,1,2,0:T(8,128)(4,1)}, pred[1,16,32,128]{3,1,2,0:T(8,128)(4,1)S(1)}, u32[]{:S(2)}) copy-start(pred[1,16,32,128]{3,1,2,0:T(8,128)(4,1)S(1)} %get-tuple-element.87) | copy-start | bytes 196612
  46.0 62.1 %copy-start.10 = (pred[1,16,32,128]{3,1,2,0:T(8,128)(4,1)}, pred[1,16,32,128]{3,1,2,0:T(8,128)(4,1)S(1)}, u32[]{:S(2)}) copy-start(pred[1,16,32,128]{3,1,2,0:T(8,128)(4,1)S(1)} %get-tuple-element.20) | copy-start | bytes 196612
  55.5 6.7 %collective-permute-start.6 = (f32[6,16,32,1]{2,1,3,0:T(8,128)}, f32[6,16,32,1]{2,1,3,0:T(8,128)}, u32[]{:S(2)}, u32[]{:S(2)}) collective-permute-start(f32[6,16,32,1]{2,1,3,0:T(8,128)} %copy.352), channel_id=1, source_target_pairs={{0,1},{1,2},{2,3},{3,4},{4,5},{5,6},{6,7},{7,8},{8,9},{9,10},{10,1... | collective-permute-start | bytes 36872 | tf_op jit(solution)/shard_map/ppermute | solution.py:22
  58.5 25.9 %copy-start = (f32[6,16,32,128]{3,1,2,0:T(8,128)}, f32[6,16,32,128]{3,1,2,0:T(8,128)S(1)}, u32[]{:S(2)}) copy-start(f32[6,16,32,128]{3,1,2,0:T(8,128)S(1)} %copy.336) | copy-start | bytes 4718596
  59.8 7.5 %collective-permute-start.7 = (f32[6,16,32,1]{2,1,3,0:T(8,128)}, f32[6,16,32,1]{2,1,3,0:T(8,128)}, u32[]{:S(2)}, u32[]{:S(2)}) collective-permute-start(f32[6,16,32,1]{2,1,3,0:T(8,128)} %copy.353), channel_id=1, source_target_pairs={{1,0},{2,1},{3,2},{4,3},{5,4},{6,5},{7,6},{8,7},{9,8},{10,9},{11,1... | collective-permute-start | bytes 36872 | tf_op jit(solution)/shard_map/ppermute | solution.py:22
  66.3 18.0 %copy-start.1 = (f32[6,16,32,1]{3,1,2,0:T(8,128)}, f32[6,16,32,1]{3,1,2,0:T(8,128)S(1)}, u32[]{:S(2)}) copy-start(f32[6,16,32,1]{3,1,2,0:T(8,128)S(1)} %broadcast_select_fusion.1) | copy-start | bytes 36868
  71.5 30.2 %copy-start.2 = (f32[6,16,32,1]{3,1,2,0:T(8,128)}, f32[6,16,32,1]{3,1,2,0:T(8,128)S(1)}, u32[]{:S(2)}) copy-start(f32[6,16,32,1]{3,1,2,0:T(8,128)S(1)} %broadcast_select_fusion) | copy-start | bytes 36868
  71.6 6.8 %collective-permute-start.8 = (f32[6,16,1,130]{3,1,2,0:T(8,128)S(1)}, f32[6,16,1,130]{3,1,2,0:T(8,128)S(1)}, u32[]{:S(2)}, u32[]{:S(2)}) collective-permute-start(f32[6,16,1,130]{3,1,2,0:T(8,128)S(1)} %get-tuple-element.43), channel_id=1, source_target_pairs={{0,4},{1,5},{2,6},{3,7},{4,8},{5,9},{6,10},{7,11},{8,12},{9,13},{1... | collective-permute-start | bytes 149768 | tf_op jit(solution)/shard_map/ppermute | solution.py:22
  75.5 6.2 %collective-permute-start.9 = (f32[6,16,1,130]{3,1,2,0:T(8,128)S(1)}, f32[6,16,1,130]{3,1,2,0:T(8,128)S(1)}, u32[]{:S(2)}, u32[]{:S(2)}) collective-permute-start(f32[6,16,1,130]{3,1,2,0:T(8,128)S(1)} %get-tuple-element.44), channel_id=1, source_target_pairs={{4,0},{5,1},{6,2},{7,3},{8,4},{9,5},{10,6},{11,7},{12,8},{13,9},{1... | collective-permute-start | bytes 149768 | tf_op jit(solution)/shard_map/ppermute | solution.py:22
  83.0 7.4 %collective-permute-start.10 = (f32[6,1,34,130]{3,1,2,0:T(1,128)S(1)}, f32[6,1,34,130]{3,1,2,0:T(1,128)S(1)}, u32[]{:S(2)}, u32[]{:S(2)}) collective-permute-start(f32[6,1,34,130]{3,1,2,0:T(1,128)S(1)} %get-tuple-element.39), channel_id=1, source_target_pairs={{0,16},{1,17},{2,18},{3,19},{4,20},{5,21},{6,22},{7,23},{8,24},{9,... | collective-permute-start | bytes 318248 | tf_op jit(solution)/shard_map/ppermute | solution.py:22
  89.1 12.3 %collective-permute-start.11 = (f32[6,1,34,130]{3,1,2,0:T(1,128)S(1)}, f32[6,1,34,130]{3,1,2,0:T(1,128)S(1)}, u32[]{:S(2)}, u32[]{:S(2)}) collective-permute-start(f32[6,1,34,130]{3,1,2,0:T(1,128)S(1)} %get-tuple-element.40), channel_id=1, source_target_pairs={{16,0},{17,1},{18,2},{19,3},{20,4},{21,5},{22,6},{23,7},{24,8},{25... | collective-permute-start | bytes 318248 | tf_op jit(solution)/shard_map/ppermute | solution.py:22
  101.6 6.5 %copy-start.12 = (pred[1,16,32,128]{3,1,2,0:T(8,128)(4,1)S(1)}, pred[1,16,32,128]{3,1,2,0:T(8,128)(4,1)}, u32[]{:S(2)}) copy-start(pred[1,16,32,128]{3,1,2,0:T(8,128)(4,1)} %copy-done.11) | copy-start | bytes 196612
  101.6 6.5 %copy-start.14 = (pred[1,16,32,128]{3,1,2,0:T(8,128)(4,1)S(1)}, pred[1,16,32,128]{3,1,2,0:T(8,128)(4,1)}, u32[]{:S(2)}) copy-start(pred[1,16,32,128]{3,1,2,0:T(8,128)(4,1)} %get-tuple-element.95) | copy-start | bytes 196612
  101.7 6.5 %copy-start.16 = (pred[16,32,128]{2,0,1:T(8,128)(4,1)S(1)}, pred[16,32,128]{2,0,1:T(8,128)(4,1)}, u32[]{:S(2)}) copy-start(pred[16,32,128]{2,0,1:T(8,128)(4,1)} %get-tuple-element.7) | copy-start | bytes 196612
  101.7 6.5 %copy-start.17 = (pred[16,32,128]{2,0,1:T(8,128)(4,1)S(1)}, pred[16,32,128]{2,0,1:T(8,128)(4,1)}, u32[]{:S(2)}) copy-start(pred[16,32,128]{2,0,1:T(8,128)(4,1)} %get-tuple-element.97) | copy-start | bytes 196612
  101.7 6.5 %copy-start.18 = (pred[16,32,128]{2,0,1:T(8,128)(4,1)S(1)}, pred[16,32,128]{2,0,1:T(8,128)(4,1)}, u32[]{:S(2)}) copy-start(pred[16,32,128]{2,0,1:T(8,128)(4,1)} %get-tuple-element.98) | copy-start | bytes 196612
  101.7 6.5 %copy-start.19 = (pred[16,32,128]{2,0,1:T(8,128)(4,1)S(1)}, pred[16,32,128]{2,0,1:T(8,128)(4,1)}, u32[]{:S(2)}) copy-start(pred[16,32,128]{2,0,1:T(8,128)(4,1)} %get-tuple-element.100) | copy-start | bytes 196612
  101.7 6.5 %copy-start.20 = (pred[16,32,128]{2,0,1:T(8,128)(4,1)S(1)}, pred[16,32,128]{2,0,1:T(8,128)(4,1)}, u32[]{:S(2)}) copy-start(pred[16,32,128]{2,0,1:T(8,128)(4,1)} %get-tuple-element.101) | copy-start | bytes 196612
  150.3 3.7 %collective-permute-start.12 = (f32[5,1,34,130]{3,1,2,0:T(1,128)S(1)}, f32[5,1,34,130]{3,1,2,0:T(1,128)S(1)}, u32[]{:S(2)}, u32[]{:S(2)}) collective-permute-start(f32[5,1,34,130]{3,1,2,0:T(1,128)S(1)} %slice.324), channel_id=1, source_target_pairs={{0,16},{1,17},{2,18},{3,19},{4,20},{5,21},{6,22},{7,23},{8,24},{9,... | collective-permute-start | bytes 265208 | tf_op jit(solution)/shard_map/ppermute | solution.py:22
  154.3 7.1 %collective-permute-start.13 = (f32[5,1,34,130]{3,1,2,0:T(1,128)S(1)}, f32[5,1,34,130]{3,1,2,0:T(1,128)S(1)}, u32[]{:S(2)}, u32[]{:S(2)}) collective-permute-start(f32[5,1,34,130]{3,1,2,0:T(1,128)S(1)} %get-tuple-element.46), channel_id=1, source_target_pairs={{16,0},{17,1},{18,2},{19,3},{20,4},{21,5},{22,6},{23,7},{24,8},{25... | collective-permute-start | bytes 265208 | tf_op jit(solution)/shard_map/ppermute | solution.py:22
  161.6 6.4 %collective-permute-start.14 = (f32[5,16,1,130]{3,1,2,0:T(8,128)S(1)}, f32[5,16,1,130]{3,1,2,0:T(8,128)S(1)}, u32[]{:S(2)}, u32[]{:S(2)}) collective-permute-start(f32[5,16,1,130]{3,1,2,0:T(8,128)S(1)} %pad_maximum_fusion.19), channel_id=1, source_target_pairs={{0,4},{1,5},{2,6},{3,7},{4,8},{5,9},{6,10},{7,11},{8,12},{9,13},{1... | collective-permute-start | bytes 124808 | tf_op jit(solution)/shard_map/ppermute | solution.py:22
  168.1 6.1 %collective-permute-start.15 = (f32[5,16,1,130]{3,1,2,0:T(8,128)S(1)}, f32[5,16,1,130]{3,1,2,0:T(8,128)S(1)}, u32[]{:S(2)}, u32[]{:S(2)}) collective-permute-start(f32[5,16,1,130]{3,1,2,0:T(8,128)S(1)} %get-tuple-element.48), channel_id=1, source_target_pairs={{4,0},{5,1},{6,2},{7,3},{8,4},{9,5},{10,6},{11,7},{12,8},{13,9},{1... | collective-permute-start | bytes 124808 | tf_op jit(solution)/shard_map/ppermute | solution.py:22
  179.5 10.6 %collective-permute-start.16 = (f32[5,16,32,1]{2,1,3,0:T(8,128)S(1)}, f32[5,16,32,1]{2,1,3,0:T(8,128)S(1)}, u32[]{:S(2)}, u32[]{:S(2)}) collective-permute-start(f32[5,16,32,1]{2,1,3,0:T(8,128)S(1)} %copy.339), channel_id=1, source_target_pairs={{0,1},{1,2},{2,3},{3,4},{4,5},{5,6},{6,7},{7,8},{8,9},{9,10},{10,1... | collective-permute-start | bytes 30728 | tf_op jit(solution)/shard_map/ppermute | solution.py:22
  196.8 10.0 %collective-permute-start.17 = (f32[5,16,32,1]{2,1,3,0:T(8,128)S(1)}, f32[5,16,32,1]{2,1,3,0:T(8,128)S(1)}, u32[]{:S(2)}, u32[]{:S(2)}) collective-permute-start(f32[5,16,32,1]{2,1,3,0:T(8,128)S(1)} %copy.344), channel_id=1, source_target_pairs={{1,0},{2,1},{3,2},{4,3},{5,4},{6,5},{7,6},{8,7},{9,8},{10,9},{11,1... | collective-permute-start | bytes 30728 | tf_op jit(solution)/shard_map/ppermute | solution.py:22
  (16 other events, 49.4 us)
where the time goes:
time: 219 us; the launch traced here: 218 us
  other arithmetic  82.3 us (38%)
  starting transfers between devices  55.9 us (26%)
  waiting for transfers between devices  45.4 us (21%)
  local copies, waits for them, and re-layouts  33.2 us (15%)
    ppermute x18, starting transfers between devices, shifted(): return lax.ppermute(shard, axis, pairs)  55.9 us
    ppermute x18, waiting for transfers between devices, shifted(): return lax.ppermute(shard, axis, pairs)  45.4 us
    add x1, other arithmetic, spread_back(): running = running + placed(jnp.where(inside[None], average, 0.0), offset)  18.6 us
    add x1, other arithmetic, neighbour_average(): running + jnp.where(inside[None], window(weighted, offset, interior), 0.0)  13.5 us
    concatenate x2, other arithmetic, exchange_rims(): return jnp.concatenate([from_below, values, from_above], axis=spatial_dim)  11.1 us
    select_n x3, other arithmetic, spread_back(): running = running + placed(jnp.where(inside[None], average, 0.0), offset)  8.69 us
    unnamed x60, local copies, waits for them, and re-layouts  5.53 us
    ppermute x2, local copies, waits for them, and re-layouts, shifted(): return lax.ppermute(shard, axis, pairs)  5.25 us
  transfers between devices with their start and end apart: 18, of which 14 were waited for; matrix products, arithmetic and copies ran while one was open for 10% of the time, Pallas kernels for 0%

commit v1 on v0

v1 whole, which is shorter than its diff:
```python
import functools

import jax
import jax.numpy as jnp
from jax import lax
from jax.experimental import pallas as pl
from jax.experimental.pallas import tpu as pltpu
from jax.sharding import PartitionSpec as P

NBY = 4
NBZ = 4
AXIS = "boxes"

NFIELD = 5
VF = 5
C1 = 6
C2 = 7
NF = 8
ZU, ZD, YU, YD, XU, XD = 16, 256, 4, 4096, 1 << 28, 1 << 29
LOW = (1 << 24) - 1
EDGE = 13.0


def pairing(stride, extent, devices, odd):
    pairs = []
    for i in range(devices):
        c = i // stride % extent
        partner = ((c + 1) ^ 1) - 1 if odd else c ^ 1
        pairs.append((i, i + (partner % extent - c) * stride))
    return pairs


def lanes_of(shape):
    return lax.broadcasted_iota(jnp.int32, shape, len(shape) - 1)


def roll(value, shift, axis=1):
    if isinstance(shift, int):
        shift %= value.shape[axis]
        if shift == 0:
            return value
    return pltpu.roll(value, shift, axis)


def place():
    me = lax.axis_index(AXIS)
    return me // (NBY * NBZ), me // NBZ % NBY, me % NBZ


def pack_kernel(cx, cy, two_x, u, vf, mask, code, zp, y_a, y_b, *xs):
    bx, by, bz = place()
    lane = lanes_of((cy, 128))
    slot = ((lane + 1) & 127) >> 1
    low_lane = (lane & 1) == 0

    def codes(rows):
        return jnp.where(mask[rows, :] == 1, code[rows, :], 13).astype(jnp.float32)

    for g in range(2):
        acc = jnp.zeros((cy, 128), jnp.float32)
        for k in range(4):
            f = 4 * g + k
            for x in range(cx):
                m = cx * k + x
                rows = pl.ds(x * cy, cy)
                if f < NFIELD:
                    part = roll(u[pl.ds((f * cx + x) * cy, cy), :], 2 * m)
                elif f == VF:
                    part = roll(vf[rows, :], 2 * m)
                elif f == C1:
                    part = roll(codes(rows), 2 * m)
                else:
                    c = codes(rows)
                    part = jnp.where(low_lane, roll(c, 2 * m - 1), roll(c, 2 * m + 1))
                acc = jnp.where(slot == m, part, acc)
        zp[g * cy : (g + 1) * cy, :] = acc

    def y_face(out, high):
        rim = jnp.where(high, cy - 1, 0)
        second = jnp.where(high, cy - 2, 1)

        def column(ref, base, row):
            return ref[pl.ds(base + row, cx, stride=cy), :]

        def code_column(row):
            return jnp.where(column(mask, 0, row) == 1, column(code, 0, row), 13).astype(jnp.float32)

        for f in range(NFIELD):
            out[f * cx : (f + 1) * cx, :] = column(u, f * cx * cy, rim)
        out[VF * cx : (VF + 1) * cx, :] = column(vf, 0, rim)
        out[C1 * cx : (C1 + 1) * cx, :] = code_column(rim)
        out[C2 * cx : (C2 + 1) * cx, :] = code_column(second)

    y_face(y_a, by % 2 == 0)
    y_face(y_b, by % 2 == 1)

    def x_face(out, high):
        rim = jnp.where(high, cx - 1, 0) * cy
        second = jnp.where(high, cx - 2, 1) * cy

        def rows(base, start):
            return pl.ds(pl.multiple_of(base + start, 8), cy)

        for f in range(NFIELD):
            out[f * cy : (f + 1) * cy, :] = u[rows(f * cx * cy, rim), :]
        out[VF * cy : (VF + 1) * cy, :] = vf[rows(0, rim), :]
        out[C1 * cy : (C1 + 1) * cy, :] = codes(rows(0, rim))
        out[C2 * cy : (C2 + 1) * cy, :] = codes(rows(0, second))

    x_face(xs[0], bx % 2 == 0)
    if two_x:
        x_face(xs[1], bx % 2 == 1)


def z_merge_kernel(cx, cy, r_a, r_b, ya_in, yb_in, zh, y_a, y_b):
    bx, by, bz = place()
    odd = bz % 2 == 1
    lane = lanes_of((cy, 128))
    low_lane = (lane & 1) == 0
    codes = (lane >= 63) & (lane <= 126)
    for g in range(2):
        rows = slice(g * cy, (g + 1) * cy)
        a, b = r_a[rows, :], r_b[rows, :]
        edge = jnp.where(codes, EDGE, 0.0) if g else jnp.zeros((cy, 128), jnp.float32)
        low = jnp.where(bz > 0, roll(jnp.where(odd, a, b), 1), edge)
        high = jnp.where(bz < NBZ - 1, roll(jnp.where(odd, b, a), -1), edge)
        zh[rows, :] = jnp.where(low_lane, low, high)
    n = NF * cx

    def finish(out, main, high):
        out[:n, :] = main[...]
        rim = jnp.where(high, cy - 1, 0)
        second = jnp.where(high, cy - 2, 1)
        for g in range(2):
            out[n + 2 * g : n + 2 * g + 1, :] = zh[pl.ds(g * cy + rim, 1), :]
            out[n + 2 * g + 1 : n + 2 * g + 2, :] = zh[pl.ds(g * cy + second, 1), :]
        out[n + 4 : n + 8, :] = jnp.zeros((4, 128), jnp.float32)

    finish(y_a, ya_in, by % 2 == 0)
    finish(y_b, yb_in, by % 2 == 1)


def z_edge_rows(cx):
    n = NF * cx
    row = lax.broadcasted_iota(jnp.int32, (n + 8, 128), 0)
    lane = lanes_of((n + 8, 128))
    codes = ((row >= C1 * cx) & (row < n)) | ((row >= n + 2) & (lane >= 63) & (lane <= 126))
    return jnp.where(codes, EDGE, 0.0)


def y_merge_kernel(cx, cy, two_x, r_a, r_b, zh, y_lo, y_hi, *xs):
    bx, by, bz = place()
    odd = by % 2 == 1
    edge = z_edge_rows(cx)
    a, b = r_a[...], r_b[...]
    y_lo[...] = jnp.where(by > 0, jnp.where(odd, a, b), edge)
    y_hi[...] = jnp.where(by < NBY - 1, jnp.where(odd, b, a), edge)
    n = NF * cx

    def x_rim(out, high):
        rim = jnp.where(high, cx - 1, 0)
        second = jnp.where(high, cx - 2, 1)
        out[: 2 * cy, :] = zh[...]
        at = 2 * cy
        for y in (y_lo, y_hi):
            out[at : at + 4, :] = y[n : n + 4, :]
            at += 4
        for y in (y_lo, y_hi):
            for f in range(NF):
                out[at : at + 1, :] = y[pl.ds(f * cx + rim, 1), :]
                at += 1
            for f in (C1, C2):
                out[at : at + 1, :] = y[pl.ds(f * cx + second, 1), :]
                at += 1
        out[at:, :] = jnp.zeros((out.shape[0] - at, 128), jnp.float32)

    x_rim(xs[0], bx % 2 == 0)
    if two_x:
        x_rim(xs[1], bx % 2 == 1)


def decode(code):
    qx = (code * 57) >> 9
    rest = code - 9 * qx
    qy = (rest * 11) >> 5
    qz = rest - 3 * qy
    word = 1 + jnp.where(qz == 2, ZU, 0) + jnp.where(qz == 0, ZD, 0)
    word = word * jnp.where(qy == 2, 1 + YU, jnp.where(qy == 0, 1 + YD, 1))
    return word | jnp.where(qx == 2, XU, jnp.where(qx == 0, XD, 0))


def on(word, bits):
    return (word & bits) == bits


def ring_store(ref, lead, value):
    n = value.shape[0]
    ref[(*lead, slice(8, 8 + n), slice(None))] = value
    ref[(*lead, slice(0, 8), slice(None))] = value[n - 8 :]
    ref[(*lead, slice(8 + n, 16 + n), slice(None))] = value[:8]


def main_kernel(
    cx, cy, nbx, u, vf, mask, code, zh, y_lo, y_hi, xa, xb, sa, sb, out,
    cw, ht, hz, zf, ow, tmp_i, tmp_f, i1, zw, zi, h0, hm, hp, rc, av, dz,
):
    bx, by, bz = place()
    x_odd = bx % 2 == 1
    has_lo, has_hi = bx > 0, bx < nbx - 1
    n = NF * cx
    rows = cy + 8
    tiles = rows // 8
    tile_lane = lanes_of((8, 128))
    lane = lanes_of((rows, 128))
    first_lane, last_lane = lane == 0, lane == 127
    even = (lane & 1) == 0

    def lower(a, b):
        return jnp.where(x_odd, a, b)

    def upper(a, b):
        return jnp.where(x_odd, b, a)

    def x_raw(f, side):
        part = slice(f * cy, (f + 1) * cy)
        edge = EDGE if f >= C1 else 0.0
        if side == 0:
            return jnp.where(has_lo, lower(xa[part, :], xb[part, :]), edge)
        return jnp.where(has_hi, upper(xa[part, :], xb[part, :]), edge)

    ht[...] = jnp.zeros(ht.shape, jnp.float32)
    at = 2 * cy + 8
    for f in range(C2):
        for x in range(cx):
            ht[f, x + 2, 0:1, :] = y_hi[f * cx + x : f * cx + x + 1, :]
            ht[f, x + 2, 7:8, :] = y_lo[f * cx + x : f * cx + x + 1, :]
    for x in range(cx):
        ht[C1, x + 2, 1:2, :] = y_hi[C2 * cx + x : C2 * cx + x + 1, :]
        ht[C1, x + 2, 6:7, :] = y_lo[C2 * cx + x : C2 * cx + x + 1, :]
    for side, layer, second in ((0, 1, 0), (1, cx + 2, cx + 3)):
        present = has_lo if side == 0 else has_hi
        pick = lower if side == 0 else upper
        for y, row1, row2 in ((0, 7, 6), (1, 0, 1)):

            def rim(i, base=at + 10 * y, pick=pick, present=present, edge=0.0):
                return jnp.where(present, pick(sa[base + i : base + i + 1, :], sb[base + i : base + i + 1, :]), edge)

            for f in range(C1):
                ht[f, layer, row1 : row1 + 1, :] = rim(f)
            ht[C1, layer, row1 : row1 + 1, :] = rim(C1, edge=EDGE)
            ht[C1, layer, row2 : row2 + 1, :] = rim(C2, edge=EDGE)
            ht[C1, second, row1 : row1 + 1, :] = rim(NF, edge=EDGE)
            ht[C1, second, row2 : row2 + 1, :] = rim(NF + 1, edge=EDGE)

    def words(own, layer):
        both = jnp.concatenate([own, ht[C1, layer].astype(jnp.int32)], axis=0)
        ring_store(cw, (layer,), decode(both))

    def own_words(x, _):
        part = pl.ds(pl.multiple_of(x * cy, 8), cy)
        words(jnp.where(mask[part, :] == 1, code[part, :], 13), x + 2)
        return 0

    lax.fori_loop(0, cx, own_words, 0)
    words(x_raw(C2, 0).astype(jnp.int32), 0)
    words(x_raw(C1, 0).astype(jnp.int32), 1)
    words(x_raw(C1, 1).astype(jnp.int32), cx + 2)
    words(x_raw(C2, 1).astype(jnp.int32), cx + 3)

    zrow = 2 * cy
    for g in range(2):
        for i, row in enumerate((0, 1)):
            hz[0, g, row : row + 1, :] = y_hi[n + 2 * g + i : n + 2 * g + i + 1, :]
            hz[0, g, 7 - row : 8 - row, :] = y_lo[n + 2 * g + i : n + 2 * g + i + 1, :]
            for side, pick in ((1, lower), (2, upper)):
                hi, lo = zrow + 4 + 2 * g + i, zrow + 2 * g + i
                hz[side, g, row : row + 1, :] = pick(sa[hi : hi + 1, :], sb[hi : hi + 1, :])
                hz[side, g, 7 - row : 8 - row, :] = pick(sa[lo : lo + 1, :], sb[lo : lo + 1, :])
    below = (lane == 127) | (lane <= 2)
    above = (lane >= 2 * cx + 3) & (lane <= 2 * cx + 6)
    for f in range(NF):
        g, k = f // 4, f % 4
        part = slice(g * cy, (g + 1) * cy)
        edge = EDGE if f >= C1 else 0.0
        own = jnp.concatenate([zh[part, :], hz[0, g]], axis=0)
        lo = jnp.concatenate([lower(sa[part, :], sb[part, :]), hz[1, g]], axis=0)
        hi = jnp.concatenate([upper(sa[part, :], sb[part, :]), hz[2, g]], axis=0)
        base = 4 - 2 * cx * k
        lo = jnp.where(has_lo, roll(lo, base - 2 * cx), edge)
        hi = jnp.where(has_hi, roll(hi, base + 2 * cx), edge)
        zf[f] = jnp.where(below, lo, jnp.where(above, hi, roll(own, base)))

    def lane_pair(layer):
        return (lane == 2 * layer) | (lane == 2 * layer - 1) | ((lane == 127) & (layer == 0))

    def collect(layer, acc):
        return jnp.where(lane_pair(layer), roll(cw[layer, 8 : 8 + rows, :], 2 * layer), acc)

    inner = lax.fori_loop(0, cx + 4, collect, jnp.ones((rows, 128), jnp.int32))
    outer1 = decode(zf[C1].astype(jnp.int32))
    outer2 = decode(zf[C2].astype(jnp.int32))
    ring_store(ow, (), outer1)
    inward = jnp.where(even, ZU, ZD)
    outward = jnp.where(even, ZD, ZU)

    def spread_counts(planes):
        mid = up = down = jnp.zeros((rows, 128), jnp.int32)
        for word, bits in planes:
            v = 1 + ((word & YU) << 6) + ((word & YD) << 4)
            if bits is not None:
                v = jnp.where((word & bits) != 0, v, 0)
            mid = mid + v
            up = up + jnp.where((word & XU) != 0, v, 0)
            down = down + jnp.where((word & XD) != 0, v, 0)
        total = mid + roll(up, 2) + roll(down, -2)
        ring_store(tmp_i, (), total)
        before, after = tmp_i[7 : 7 + rows, :], tmp_i[9 : 9 + rows, :]
        return (total & 255) + ((before >> 8) & 255) + ((after >> 16) & 255)

    z_count = spread_counts(((outer1, None), (outer2, inward), (inner, outward)))
    i1[...] = spread_counts(((outer1, inward),))
    z_weight = zf[VF] / z_count.astype(jnp.float32)
    zw[0] = z_weight
    for f in range(NFIELD):
        zw[f + 1] = z_weight * zf[f]

    zi[...] = jnp.zeros(zi.shape, jnp.float32)

    def weigh(layer, field):
        mid, left, right = (cw[layer + d, 8 : 8 + rows, :] for d in (0, -1, 1))
        total = (mid & LOW) + jnp.where((left & XU) != 0, left & LOW, 0) + jnp.where((right & XD) != 0, right & LOW, 0)
        ring_store(tmp_i, (), total)
        before, after = tmp_i[7 : 7 + rows, :], tmp_i[9 : 9 + rows, :]
        total = (total & 0x333) + ((before >> 2) & 0x333) + ((after >> 12) & 0x333)
        back = 128 - 2 * layer
        extra = roll(i1[...], back)
        count = (total & 15) + jnp.where(first_lane, extra, (roll(total, 1) >> 4) & 15)
        count = count + jnp.where(last_lane, extra, (roll(total, -1) >> 8) & 15)
        inverse = 1.0 / count.astype(jnp.float32)
        rc[layer] = inverse[:cy]
        weight = field(VF) * inverse
        pair = lane_pair(layer)
        for f in range(NFIELD + 1):
            w = weight * field(f - 1) if f else weight
            halo = roll(zw[f], back)
            ring_store(h0, (f, layer), w)
            ring_store(hm, (f, layer), w + jnp.where(first_lane, halo, roll(w, 1)))
            ring_store(hp, (f, layer), w + jnp.where(last_lane, halo, roll(w, -1)))
            zi[f] = jnp.where(pair, roll(w, 2 * layer), zi[f])

    def own_field(x, f):
        base = (f * cx + x if f < NFIELD else x) * cy
        ref = u if f < NFIELD else vf
        return jnp.concatenate([ref[pl.ds(pl.multiple_of(base, 8), cy), :], ht[f, x + 2]], axis=0)

    def own_weigh(x, _):
        weigh(x + 2, functools.partial(own_field, x))
        return 0

    lax.fori_loop(0, cx, own_weigh, 0)
    weigh(1, lambda f: jnp.concatenate([x_raw(f, 0), ht[f, 1]], axis=0))
    weigh(cx + 2, lambda f: jnp.concatenate([x_raw(f, 1), ht[f, cx + 2]], axis=0))

    word = ow[8 : 8 + rows, :]
    sums = []
    for f in range(NFIELD + 1):
        ring_store(tmp_f, (), zw[f] + zi[f])
        mid, before, after = (tmp_f[s : s + rows, :] for s in (8, 7, 9))
        parts = []
        for d in (0, 1, -1):
            m, b, a = (roll(v, -2 * d) for v in (mid, before, after))
            parts.append(m + jnp.where((word & YU) != 0, a, jnp.where((word & YD) != 0, b, 0.0)))
        sums.append(parts[0] + jnp.where((word & XU) != 0, parts[1], jnp.where((word & XD) != 0, parts[2], 0.0)))
    inverse = 1.0 / sums[0]
    for f in range(NFIELD):
        v = jnp.where((word & inward) != 0, sums[f + 1] * inverse, 0.0)
        spread = []
        for bits in (0, YU, YD):
            w = jnp.where((word & bits) != 0, v, 0.0) if bits else v
            up, down = jnp.where((word & XU) != 0, w, 0.0), jnp.where((word & XD) != 0, w, 0.0)
            spread.append(w + roll(up, 2) + roll(down, -2))
        ring_store(tmp_f, (), spread[1])
        total = spread[0] + tmp_f[7 : 7 + rows, :]
        ring_store(tmp_f, (), spread[2])
        dz[f] = total + tmp_f[9 : 9 + rows, :]

    def average(layer, _):
        for t in range(tiles):
            at = 8 + 8 * t
            word = cw[layer, at : at + 8, :]
            zu, zd = (word & ZU) != 0, (word & ZD) != 0
            yu, yd = (word & YU) != 0, (word & YD) != 0
            xu, xd = (word & XU) != 0, (word & XD) != 0
            sums = []
            for f in range(NFIELD + 1):
                parts = []
                for d in (0, 1, -1):
                    line = []
                    for e in (0, 1, -1):
                        at_e = slice(at + e, at + e + 8)
                        v0, vm, vp = (r[f, layer + d, at_e, :] for r in (h0, hm, hp))
                        line.append(jnp.where(zu, vp, jnp.where(zd, vm, v0)))
                    parts.append(line[0] + jnp.where(yu, line[1], jnp.where(yd, line[2], 0.0)))
                sums.append(parts[0] + jnp.where(xu, parts[1], jnp.where(xd, parts[2], 0.0)))
            inverse = 1.0 / sums[0]
            for f in range(NFIELD):
                a = sums[f + 1] * inverse
                av[f, layer, at : at + 8, :] = a
                if t == 0:
                    av[f, layer, 8 + rows : 16 + rows, :] = a
                if t == tiles - 1:
                    av[f, layer, 0:8, :] = a
        return 0

    lax.fori_loop(1, cx + 3, average, 0)

    tile_first, tile_last = tile_lane == 0, tile_lane == 127

    def spread(x, _):
        layer = x + 2
        back = 128 - 2 * layer
        for t in range(tiles - 1):
            at = 8 + 8 * t
            base = [av[f, layer, at : at + 8, :] for f in range(NFIELD)]
            word = cw[layer, at : at + 8, :]
            up = [jnp.where((word & ZU) != 0, a, 0.0) for a in base]
            down = [jnp.where((word & ZD) != 0, a, 0.0) for a in base]
            for d in (0, 1, -1):
                for e in (0, 1, -1):
                    if d == 0 and e == 0:
                        continue
                    at_e = slice(at - e, at - e + 8)
                    word = cw[layer - d, at_e, :]
                    bits = (0, XU, XD)[d] | (0, YU, YD)[e]
                    here = on(word, bits)
                    here_up, here_down = on(word, bits | ZU), on(word, bits | ZD)
                    for f in range(NFIELD):
                        a = av[f, layer - d, at_e, :]
                        base[f] = base[f] + jnp.where(here, a, 0.0)
                        up[f] = up[f] + jnp.where(here_up, a, 0.0)
                        down[f] = down[f] + jnp.where(here_down, a, 0.0)
            inverse = rc[layer, 8 * t : 8 * t + 8, :]
            for f in range(NFIELD):
                halo = roll(dz[f, 8 * t : 8 * t + 8, :], back)
                total = base[f] + jnp.where(tile_first, halo, roll(up[f], 1))
                total = total + jnp.where(tile_last, halo, roll(down[f], -1))
                out[pl.ds(pl.multiple_of((f * cx + x) * cy + 8 * t, 8), 8), :] = total * inverse
        return 0

    lax.fori_loop(0, cx, spread, 0)


def call(kernel, outs, scratch=(), name=None):
    return pl.pallas_call(
        kernel,
        out_shape=tuple(jax.ShapeDtypeStruct(s, jnp.float32) for s in outs),
        scratch_shapes=scratch,
        name=name,
    )


def per_device(conserved, volume_fraction, cut_mask, merge_code):
    _, cx, cy, cz = cut_mask.shape
    devices = lax.axis_size(AXIS)
    nbx = devices // (NBY * NBZ)
    two_x = nbx > 2
    u = conserved.reshape(NFIELD * cx * cy, cz)
    vf, mask, code = (a.reshape(cx * cy, cz) for a in (volume_fraction, cut_mask, merge_code))

    def swap(value, stride, extent, odd):
        return lax.ppermute(value, AXIS, pairing(stride, extent, devices, odd))

    def x_swap(parts):
        got = [swap(p, NBY * NBZ, nbx, odd) for odd, p in enumerate(parts)]
        return got if two_x else got * 2

    n = NF * cx
    face, z_shape, y_shape, x_shape = (n, cz), (2 * cy, cz), (n + 8, cz), (NF * cy, cz)
    rim_shape = (2 * cy + 32, cz)
    copies = 2 if two_x else 1
    zp, ya, yb, *xs = call(
        functools.partial(pack_kernel, cx, cy, two_x), [z_shape, face, face] + [x_shape] * copies, name="pack"
    )(u, vf, mask, code)
    xa, xb = x_swap(xs)
    zh, ya, yb = call(functools.partial(z_merge_kernel, cx, cy), [z_shape, y_shape, y_shape], name="z_merge")(
        swap(zp, 1, NBZ, False), swap(zp, 1, NBZ, True), ya, yb
    )
    y_lo, y_hi, *rims = call(
        functools.partial(y_merge_kernel, cx, cy, two_x), [y_shape, y_shape] + [rim_shape] * copies, name="y_merge"
    )(swap(ya, NBZ, NBY, False), swap(yb, NBZ, NBY, True), zh)
    sa, sb = x_swap(rims)

    rows, ring = cy + 8, cy + 24
    layers = cx + 4
    f32, i32 = jnp.float32, jnp.int32
    scratch = [
        pltpu.VMEM((layers, ring, cz), i32),
        pltpu.VMEM((C2, layers, 8, cz), f32),
        pltpu.VMEM((3, 2, 8, cz), f32),
        pltpu.VMEM((NF, rows, cz), f32),
        pltpu.VMEM((ring, cz), i32),
        pltpu.VMEM((ring, cz), i32),
        pltpu.VMEM((ring, cz), f32),
        pltpu.VMEM((rows, cz), i32),
        pltpu.VMEM((NFIELD + 1, rows, cz), f32),
        pltpu.VMEM((NFIELD + 1, rows, cz), f32),
        pltpu.VMEM((NFIELD + 1, layers, ring, cz), f32),
        pltpu.VMEM((NFIELD + 1, layers, ring, cz), f32),
        pltpu.VMEM((NFIELD + 1, layers, ring, cz), f32),
        pltpu.VMEM((layers, cy, cz), f32),
        pltpu.VMEM((NFIELD, layers, ring, cz), f32),
        pltpu.VMEM((NFIELD, rows, cz), f32),
    ]
    (out,) = call(functools.partial(main_kernel, cx, cy, nbx), [(NFIELD * cx * cy, cz)], scratch, name="redistribute")(
        u, vf, mask, code, zh, y_lo, y_hi, xa, xb, sa, sb
    )
    return out.reshape(conserved.shape)


def solution(mesh):
    return jax.shard_map(
        per_device,
        mesh=mesh,
        in_specs=(
            P(AXIS, None, None, None, None),
            P(AXIS, None, None, None),
            P(AXIS, None, None, None),
            P(AXIS, None, None, None),
        ),
        out_specs=P(AXIS, None, None, None, None),
        check_vma=False,
    )
```

time: 219 us -> 42.6 us (0.19)
  the two profiles are of different devices: /device:TPU:5 before, /device:TPU:0 now
where the time goes in v1:
time: 42.6 us; the launch traced here: 42.4 us
  Pallas kernels  22.7 us (53%)
  starting transfers between devices  11 us (26%)
  waiting for transfers between devices  6.85 us (16%)
  local copies, waits for them, and re-layouts  1.85 us (4%)
    pallas_call x1, Pallas kernels, per_device(): call(functools.partial(main_kernel, cx, cy, nbx), [(NFIELD * cx * cy, cz)...  16.5 us
    ppermute x6, starting transfers between devices, swap(): return lax.ppermute(value, AXIS, pairing(stride, extent, devices, odd))  11 us
    ppermute x6, waiting for transfers between devices, swap(): return lax.ppermute(value, AXIS, pairing(stride, extent, devices, odd))  6.85 us
    pallas_call x1, Pallas kernels, per_device(): call(functools.partial(pack_kernel, cx, cy, two_x), [z_shape, face, face]...  2.94 us
    unnamed x12, local copies, waits for them, and re-layouts  1.85 us
    pallas_call x1, Pallas kernels, per_device(): call(functools.partial(z_merge_kernel, cx, cy), [z_shape, y_shape, y_shap...  1.69 us
    pallas_call x1, Pallas kernels, per_device(): call(functools.partial(y_merge_kernel, cx, cy, two_x), [y_shape, y_shape]...  1.62 us
  transfers between devices with their start and end apart: 6, of which 3 were waited for; matrix products, arithmetic and copies ran while one was open for 0% of the time, Pallas kernels for 8%

profile of v1, /device:TPU:0, one launch (start us, length us, event | category | flops | bytes accessed | tf_op | source)
XLA Modules:
  0.0 42.4 jit_solution(16420948686044157360)
XLA Ops:
  0.0 2.9 %pack.1 = (f32[64,128]{1,0:T(8,128)}, f32[128,128]{1,0:T(8,128)}, f32[128,128]{1,0:T(8,128)}, f32[256,128]{1,0:T(8,128)}) custom-call(f32[2560,128]{1,0:T(8,128)} %bitcast.5, f32[512,128]{1,0:T(8,128)} %bitcast.7, s32[512,128]{1,0:T(8,128)} %bitcast.9, s32[512,128]{1,0:T(8,128)} %bitcast.11), custom_call_target="tpu_custom_call" | custom-call | tf_op jit(solution)/shard_map/pack/pallas_call | solution.py:481
  2.9 2.4 %collective-permute-start.1 = (f32[64,128]{1,0:T(8,128)}, f32[64,128]{1,0:T(8,128)S(1)}, u32[]{:S(2)}, u32[]{:S(2)}) collective-permute-start(f32[64,128]{1,0:T(8,128)} %get-tuple-element.15), channel_id=1, source_target_pairs={{0,3},{1,2},{2,1},{3,0},{4,7},{5,6},{6,5},{7,4},{8,11},{9,10},{10,... | collective-permute-start | bytes 98312 | tf_op jit(solution)/shard_map/ppermute | solution.py:471
  5.3 0.7 %collective-permute-start = (f32[64,128]{1,0:T(8,128)}, f32[64,128]{1,0:T(8,128)S(1)}, u32[]{:S(2)}, u32[]{:S(2)}) collective-permute-start(f32[64,128]{1,0:T(8,128)} %get-tuple-element.15), channel_id=1, source_target_pairs={{0,1},{1,0},{2,3},{3,2},{4,5},{5,4},{6,7},{7,6},{8,9},{9,8},{10,11... | collective-permute-start | bytes 98312 | tf_op jit(solution)/shard_map/ppermute | solution.py:471
  6.0 2.6 %collective-permute-start.4 = (f32[256,128]{1,0:T(8,128)}, f32[256,128]{1,0:T(8,128)S(1)}, u32[]{:S(2)}, u32[]{:S(2)}) collective-permute-start(f32[256,128]{1,0:T(8,128)} %get-tuple-element.23), channel_id=1, source_target_pairs={{0,16},{1,17},{2,18},{3,19},{4,20},{5,21},{6,22},{7,23},{8,24},{9,... | collective-permute-start | bytes 393224 | tf_op jit(solution)/shard_map/ppermute | solution.py:471
  8.6 0.0 collective-permute-done.1.r_b
  8.6 0.0 copy-start.4
  8.6 0.0 collective-permute-done.r_a
  8.6 0.0 copy-start.5
  8.6 0.6 %copy-done.4 = f32[64,128]{1,0:T(8,128)} copy-done((f32[64,128]{1,0:T(8,128)}, f32[64,128]{1,0:T(8,128)S(1)}, u32[]{:S(2)}) %copy-start.4) | copy-done | bytes 32792
  9.2 0.0 copy-done.5
  9.2 1.7 %z_merge.1 = (f32[64,128]{1,0:T(8,128)}, f32[136,128]{1,0:T(8,128)}, f32[136,128]{1,0:T(8,128)}) custom-call(f32[64,128]{1,0:T(8,128)} %copy-done.5, f32[64,128]{1,0:T(8,128)} %copy-done.4, f32[128,128]{1,0:T(8,128)} %get-tuple-element.16.ya_in, f32[128,128]{1,0:T(8,128)} %get-tuple-element.17.yb_in), custom_call_target="tpu_custom_call" | custom-call | tf_op jit(solution)/shard_map/z_merge/pallas_call | solution.py:485
  10.9 1.5 %collective-permute-start.2 = (f32[136,128]{1,0:T(8,128)}, f32[136,128]{1,0:T(8,128)S(1)}, u32[]{:S(2)}, u32[]{:S(2)}) collective-permute-start(f32[136,128]{1,0:T(8,128)} %get-tuple-element.19), channel_id=1, source_target_pairs={{0,4},{1,5},{2,6},{3,7},{4,0},{5,1},{6,2},{7,3},{8,12},{9,13},{10,... | collective-permute-start | bytes 208904 | tf_op jit(solution)/shard_map/ppermute | solution.py:471
  12.4 1.5 %collective-permute-start.3 = (f32[136,128]{1,0:T(8,128)}, f32[136,128]{1,0:T(8,128)S(1)}, u32[]{:S(2)}, u32[]{:S(2)}) collective-permute-start(f32[136,128]{1,0:T(8,128)} %get-tuple-element.20), channel_id=1, source_target_pairs={{0,12},{1,13},{2,14},{3,15},{4,8},{5,9},{6,10},{7,11},{8,4},{9,5},... | collective-permute-start | bytes 208904 | tf_op jit(solution)/shard_map/ppermute | solution.py:471
  14.0 1.5 %collective-permute-done.2.r_a = f32[136,128]{1,0:T(8,128)S(1)} collective-permute-done((f32[136,128]{1,0:T(8,128)}, f32[136,128]{1,0:T(8,128)S(1)}, u32[]{:S(2)}, u32[]{:S(2)}) %collective-permute-start.2) | collective-permute-done | bytes 69664 | tf_op jit(solution)/shard_map/ppermute | solution.py:471
  15.4 0.0 copy-start.2
  15.5 2.4 %collective-permute-done.3.r_b = f32[136,128]{1,0:T(8,128)S(1)} collective-permute-done((f32[136,128]{1,0:T(8,128)}, f32[136,128]{1,0:T(8,128)S(1)}, u32[]{:S(2)}, u32[]{:S(2)}) %collective-permute-start.3) | collective-permute-done | bytes 69664 | tf_op jit(solution)/shard_map/ppermute | solution.py:471
  17.9 0.0 copy-start.3
  17.9 0.0 copy-done.2
  17.9 0.6 %copy-done.3 = f32[136,128]{1,0:T(8,128)} copy-done((f32[136,128]{1,0:T(8,128)}, f32[136,128]{1,0:T(8,128)S(1)}, u32[]{:S(2)}) %copy-start.3) | copy-done | bytes 69656
  18.5 1.6 %y_merge.1 = (f32[136,128]{1,0:T(8,128)}, f32[136,128]{1,0:T(8,128)}, f32[96,128]{1,0:T(8,128)}) custom-call(f32[136,128]{1,0:T(8,128)} %copy-done.2, f32[136,128]{1,0:T(8,128)} %copy-done.3, f32[64,128]{1,0:T(8,128)} %get-tuple-element.18.zh), custom_call_target="tpu_custom_call" | custom-call | tf_op jit(solution)/shard_map/y_merge/pallas_call | solution.py:488
  20.1 2.2 %collective-permute-start.5 = (f32[96,128]{1,0:T(8,128)}, f32[96,128]{1,0:T(8,128)S(1)}, u32[]{:S(2)}, u32[]{:S(2)}) collective-permute-start(f32[96,128]{1,0:T(8,128)} %get-tuple-element.24), channel_id=1, source_target_pairs={{0,16},{1,17},{2,18},{3,19},{4,20},{5,21},{6,22},{7,23},{8,24},{9,... | collective-permute-start | bytes 147464 | tf_op jit(solution)/shard_map/ppermute | solution.py:471
  22.4 0.0 collective-permute-done.4.xa.xb
  22.4 0.0 copy-start
  22.4 2.9 %collective-permute-done.5.sa.sb = f32[96,128]{1,0:T(8,128)S(1)} collective-permute-done((f32[96,128]{1,0:T(8,128)}, f32[96,128]{1,0:T(8,128)S(1)}, u32[]{:S(2)}, u32[]{:S(2)}) %collective-permute-start.5) | collective-permute-done | bytes 49184 | tf_op jit(solution)/shard_map/ppermute | solution.py:471
  25.3 0.0 copy-start.1
  25.3 0.0 copy-done
  25.3 0.6 %copy-done.1 = f32[96,128]{1,0:T(8,128)} copy-done((f32[96,128]{1,0:T(8,128)}, f32[96,128]{1,0:T(8,128)S(1)}, u32[]{:S(2)}) %copy-start.1) | copy-done | bytes 49176
  25.9 16.5 %redistribute.1 = f32[2560,128]{1,0:T(8,128)} custom-call(f32[2560,128]{1,0:T(8,128)} %bitcast.6, f32[512,128]{1,0:T(8,128)} %bitcast.8, s32[512,128]{1,0:T(8,128)} %bitcast.10, s32[512,128]{1,0:T(8,128)} %bitcast.12, f32[64,128]{1,0:T(8,128)} %get-tuple-element.18.zh, f32[136,128]{1,0:T(8,128)} %get-tuple-element.21.y_lo, ...), custom_call_target="tpu_custom_call" | custom-call | tf_op jit(solution)/shard_map/redistribute/pallas_call | solution.py:514
Async XLA Ops:
  2.9 5.7 %collective-permute-start.1 = (f32[64,128]{1,0:T(8,128)}, f32[64,128]{1,0:T(8,128)S(1)}, u32[]{:S(2)}, u32[]{:S(2)}) collective-permute-start(f32[64,128]{1,0:T(8,128)} %get-tuple-element.15), channel_id=1, source_target_pairs={{0,3},{1,2},{2,1},{3,0},{4,7},{5,6},{6,5},{7,4},{8,11},{9,10},{10,... | collective-permute-start | bytes 98312 | tf_op jit(solution)/shard_map/ppermute | solution.py:471
  5.3 3.3 %collective-permute-start = (f32[64,128]{1,0:T(8,128)}, f32[64,128]{1,0:T(8,128)S(1)}, u32[]{:S(2)}, u32[]{:S(2)}) collective-permute-start(f32[64,128]{1,0:T(8,128)} %get-tuple-element.15), channel_id=1, source_target_pairs={{0,1},{1,0},{2,3},{3,2},{4,5},{5,4},{6,7},{7,6},{8,9},{9,8},{10,11... | collective-permute-start | bytes 98312 | tf_op jit(solution)/shard_map/ppermute | solution.py:471
  6.0 16.3 %collective-permute-start.4 = (f32[256,128]{1,0:T(8,128)}, f32[256,128]{1,0:T(8,128)S(1)}, u32[]{:S(2)}, u32[]{:S(2)}) collective-permute-start(f32[256,128]{1,0:T(8,128)} %get-tuple-element.23), channel_id=1, source_target_pairs={{0,16},{1,17},{2,18},{3,19},{4,20},{5,21},{6,22},{7,23},{8,24},{9,... | collective-permute-start | bytes 393224 | tf_op jit(solution)/shard_map/ppermute | solution.py:471
  8.6 0.6 %copy-start.4 = (f32[64,128]{1,0:T(8,128)}, f32[64,128]{1,0:T(8,128)S(1)}, u32[]{:S(2)}) copy-start(f32[64,128]{1,0:T(8,128)S(1)} %collective-permute-done.1.r_b) | copy-start | bytes 98308
  8.6 0.6 %copy-start.5 = (f32[64,128]{1,0:T(8,128)}, f32[64,128]{1,0:T(8,128)S(1)}, u32[]{:S(2)}) copy-start(f32[64,128]{1,0:T(8,128)S(1)} %collective-permute-done.r_a) | copy-start | bytes 98308
  10.9 4.5 %collective-permute-start.2 = (f32[136,128]{1,0:T(8,128)}, f32[136,128]{1,0:T(8,128)S(1)}, u32[]{:S(2)}, u32[]{:S(2)}) collective-permute-start(f32[136,128]{1,0:T(8,128)} %get-tuple-element.19), channel_id=1, source_target_pairs={{0,4},{1,5},{2,6},{3,7},{4,0},{5,1},{6,2},{7,3},{8,12},{9,13},{10,... | collective-permute-start | bytes 208904 | tf_op jit(solution)/shard_map/ppermute | solution.py:471
  12.4 5.4 %collective-permute-start.3 = (f32[136,128]{1,0:T(8,128)}, f32[136,128]{1,0:T(8,128)S(1)}, u32[]{:S(2)}, u32[]{:S(2)}) collective-permute-start(f32[136,128]{1,0:T(8,128)} %get-tuple-element.20), channel_id=1, source_target_pairs={{0,12},{1,13},{2,14},{3,15},{4,8},{5,9},{6,10},{7,11},{8,4},{9,5},... | collective-permute-start | bytes 208904 | tf_op jit(solution)/shard_map/ppermute | solution.py:471
  15.4 2.4 %copy-start.2 = (f32[136,128]{1,0:T(8,128)}, f32[136,128]{1,0:T(8,128)S(1)}, u32[]{:S(2)}) copy-start(f32[136,128]{1,0:T(8,128)S(1)} %collective-permute-done.2.r_a) | copy-start | bytes 208900
  17.9 0.6 %copy-start.3 = (f32[136,128]{1,0:T(8,128)}, f32[136,128]{1,0:T(8,128)S(1)}, u32[]{:S(2)}) copy-start(f32[136,128]{1,0:T(8,128)S(1)} %collective-permute-done.3.r_b) | copy-start | bytes 208900
  20.1 5.2 %collective-permute-start.5 = (f32[96,128]{1,0:T(8,128)}, f32[96,128]{1,0:T(8,128)S(1)}, u32[]{:S(2)}, u32[]{:S(2)}) collective-permute-start(f32[96,128]{1,0:T(8,128)} %get-tuple-element.24), channel_id=1, source_target_pairs={{0,16},{1,17},{2,18},{3,19},{4,20},{5,21},{6,22},{7,23},{8,24},{9,... | collective-permute-start | bytes 147464 | tf_op jit(solution)/shard_map/ppermute | solution.py:471
  22.4 3.0 %copy-start = (f32[256,128]{1,0:T(8,128)}, f32[256,128]{1,0:T(8,128)S(1)}, u32[]{:S(2)}) copy-start(f32[256,128]{1,0:T(8,128)S(1)} %collective-permute-done.4.xa.xb) | copy-start | bytes 393220
  25.3 0.6 %copy-start.1 = (f32[96,128]{1,0:T(8,128)}, f32[96,128]{1,0:T(8,128)S(1)}, u32[]{:S(2)}) copy-start(f32[96,128]{1,0:T(8,128)S(1)} %collective-permute-done.5.sa.sb) | copy-start | bytes 147460

commit v2 on v1

--- a/solution.py
+++ b/solution.py
@@ -450,12 +450,18 @@
     lax.fori_loop(0, cx, spread, 0)
 
 
-def call(kernel, outs, scratch=(), name=None):
+def call(kernel, ins, outs, scratch=(), name=None, grant=8, last=False):
+    vmem = pl.BlockSpec(memory_space=pltpu.VMEM)
     return pl.pallas_call(
         kernel,
-        out_shape=tuple(jax.ShapeDtypeStruct(s, jnp.float32) for s in outs),
+        in_specs=[vmem] * ins,
+        out_specs=tuple([pl.BlockSpec() if last else vmem] * len(outs)),
+        out_shape=tuple(
+            jax.ShapeDtypeStruct(s, jnp.float32) if last else pltpu.VMEM(s, jnp.float32) for s in outs
+        ),
         scratch_shapes=scratch,
         name=name,
+        compiler_params=pltpu.CompilerParams(vmem_limit_bytes=grant << 20),
     )
 
 
@@ -479,14 +485,14 @@
     rim_shape = (2 * cy + 32, cz)
     copies = 2 if two_x else 1
     zp, ya, yb, *xs = call(
-        functools.partial(pack_kernel, cx, cy, two_x), [z_shape, face, face] + [x_shape] * copies, name="pack"
+        functools.partial(pack_kernel, cx, cy, two_x), 4, [z_shape, face, face] + [x_shape] * copies, name="pack"
     )(u, vf, mask, code)
     xa, xb = x_swap(xs)
-    zh, ya, yb = call(functools.partial(z_merge_kernel, cx, cy), [z_shape, y_shape, y_shape], name="z_merge")(
+    zh, ya, yb = call(functools.partial(z_merge_kernel, cx, cy), 4, [z_shape, y_shape, y_shape], name="z_merge")(
         swap(zp, 1, NBZ, False), swap(zp, 1, NBZ, True), ya, yb
     )
     y_lo, y_hi, *rims = call(
-        functools.partial(y_merge_kernel, cx, cy, two_x), [y_shape, y_shape] + [rim_shape] * copies, name="y_merge"
+        functools.partial(y_merge_kernel, cx, cy, two_x), 3, [y_shape, y_shape] + [rim_shape] * copies, name="y_merge"
     )(swap(ya, NBZ, NBY, False), swap(yb, NBZ, NBY, True), zh)
     sa, sb = x_swap(rims)
 
@@ -511,7 +517,7 @@
         pltpu.VMEM((NFIELD, layers, ring, cz), f32),
         pltpu.VMEM((NFIELD, rows, cz), f32),
     ]
-    (out,) = call(functools.partial(main_kernel, cx, cy, nbx), [(NFIELD * cx * cy, cz)], scratch, name="redistribute")(
+    (out,) = call(functools.partial(main_kernel, cx, cy, nbx), 11, [(NFIELD * cx * cy, cz)], scratch, "redistribute", 28, True)(
         u, vf, mask, code, zh, y_lo, y_hi, xa, xb, sa, sb
     )
     return out.reshape(conserved.shape)

time: 42.6 us -> 39.6 us (0.930)
  Pallas kernels: 22.7 us -> 15.7 us
  waiting for transfers between devices: 6.85 us -> 9.37 us
  local copies, waits for them, and re-layouts: 1.85 us -> 4.18 us
  starting transfers between devices: 11 us -> 10.1 us
    pallas_call x4, Pallas kernels: 22.7 us -> 15.7 us  [the longest x1 14.8 us: per_device(): call(functools.partial(main_kernel, cx, cy, nbx), 11, [(NFIELD * cx * cy,...]
    ppermute x6, waiting for transfers between devices: 6.85 us -> 9.37 us  [swap(): return lax.ppermute(value, AXIS, pairing(stride, extent, devices, odd))]
    unnamed x12 -> x16, local copies, waits for them, and re-layouts: 1.85 us -> 4.18 us
    ppermute x6, starting transfers between devices: 11 us -> 10.1 us  [swap(): return lax.ppermute(value, AXIS, pairing(stride, extent, devices, odd))]
  transfers between devices with their start and end apart: 6 -> 6, of which waited for: 3 -> 3; matrix products, arithmetic and copies ran while one was open for 0% -> 0% of each run, Pallas kernels for 8% -> 0%
where the time goes in v2:
time: 39.6 us; the launch traced here: 39.4 us
  Pallas kernels  15.7 us (40%)
  starting transfers between devices  10.1 us (26%)
  waiting for transfers between devices  9.37 us (24%)
  local copies, waits for them, and re-layouts  4.18 us (11%)
    pallas_call x1, Pallas kernels, per_device(): call(functools.partial(main_kernel, cx, cy, nbx), 11, [(NFIELD * cx * cy,...  14.8 us
    ppermute x6, starting transfers between devices, swap(): return lax.ppermute(value, AXIS, pairing(stride, extent, devices, odd))  10.1 us
    ppermute x6, waiting for transfers between devices, swap(): return lax.ppermute(value, AXIS, pairing(stride, extent, devices, odd))  9.37 us
    unnamed x16, local copies, waits for them, and re-layouts  4.18 us
  transfers between devices with their start and end apart: 6, of which 3 were waited for; matrix products, arithmetic and copies ran while one was open for 0% of the time, Pallas kernels for 0%

profile of v2, /device:TPU:0, one launch (start us, length us, event | category | flops | bytes accessed | tf_op | source)
XLA Modules:
  0.0 39.4 jit_solution(14284925554274583054)
XLA Ops:
  0.0 0.0 copy-start
  0.0 1.3 %copy-done = f32[1,5,16,32,128]{4,3,2,1,0:T(8,128)S(1)} copy-done((f32[1,5,16,32,128]{4,3,2,1,0:T(8,128)S(1)}, f32[1,5,16,32,128]{4,3,2,1,0:T(8,128)}, u32[]{:S(2)}) %copy-start) | copy-done | bytes 1310744
  1.3 0.0 copy-start.2
  1.3 0.9 %copy-done.2 = f32[1,16,32,128]{3,2,1,0:T(8,128)S(1)} copy-done((f32[1,16,32,128]{3,2,1,0:T(8,128)S(1)}, f32[1,16,32,128]{3,2,1,0:T(8,128)}, u32[]{:S(2)}) %copy-start.2) | copy-done | bytes 262168
  2.3 0.0 copy-start.4
  2.3 0.9 %copy-done.4 = s32[1,16,32,128]{3,2,1,0:T(8,128)S(1)} copy-done((s32[1,16,32,128]{3,2,1,0:T(8,128)S(1)}, s32[1,16,32,128]{3,2,1,0:T(8,128)}, u32[]{:S(2)}) %copy-start.4) | copy-done | bytes 262168
  3.2 0.0 copy-start.6
  3.2 0.9 %copy-done.6 = s32[1,16,32,128]{3,2,1,0:T(8,128)S(1)} copy-done((s32[1,16,32,128]{3,2,1,0:T(8,128)S(1)}, s32[1,16,32,128]{3,2,1,0:T(8,128)}, u32[]{:S(2)}) %copy-start.6) | copy-done | bytes 262168
  4.2 0.0 copy-start.1
  4.2 0.0 copy-start.3
  4.2 0.0 copy-start.5
  4.2 0.0 copy-start.7
  4.2 0.8 %pack.1 = (f32[64,128]{1,0:T(8,128)S(1)}, f32[128,128]{1,0:T(8,128)S(1)}, f32[128,128]{1,0:T(8,128)S(1)}, f32[256,128]{1,0:T(8,128)S(1)}) custom-call(f32[2560,128]{1,0:T(8,128)S(1)} %bitcast.5, f32[512,128]{1,0:T(8,128)S(1)} %bitcast.7, s32[512,128]{1,0:T(8,128)S(1)} %bitcast.9, s32[512,128]{1,0:T(8,128)S(1)} %bitcast.11), custom_call_target="tpu_custom_call" | custom-call | tf_op jit(solution)/shard_map/pack/pallas_call | solution.py:487
  5.0 2.5 %collective-permute-start.1 = (f32[64,128]{1,0:T(8,128)S(1)}, f32[64,128]{1,0:T(8,128)S(1)}, u32[]{:S(2)}, u32[]{:S(2)}) collective-permute-start(f32[64,128]{1,0:T(8,128)S(1)} %get-tuple-element.15), channel_id=1, source_target_pairs={{0,3},{1,2},{2,1},{3,0},{4,7},{5,6},{6,5},{7,4},{8,11},{9,10},{10,... | collective-permute-start | bytes 98312 | tf_op jit(solution)/shard_map/ppermute | solution.py:477
  7.4 0.7 %collective-permute-start = (f32[64,128]{1,0:T(8,128)S(1)}, f32[64,128]{1,0:T(8,128)S(1)}, u32[]{:S(2)}, u32[]{:S(2)}) collective-permute-start(f32[64,128]{1,0:T(8,128)S(1)} %get-tuple-element.15), channel_id=1, source_target_pairs={{0,1},{1,0},{2,3},{3,2},{4,5},{5,4},{6,7},{7,6},{8,9},{9,8},{10,11... | collective-permute-start | bytes 98312 | tf_op jit(solution)/shard_map/ppermute | solution.py:477
  8.1 2.6 %collective-permute-start.4 = (f32[256,128]{1,0:T(8,128)S(1)}, f32[256,128]{1,0:T(8,128)S(1)}, u32[]{:S(2)}, u32[]{:S(2)}) collective-permute-start(f32[256,128]{1,0:T(8,128)S(1)} %get-tuple-element.23), channel_id=1, source_target_pairs={{0,16},{1,17},{2,18},{3,19},{4,20},{5,21},{6,22},{7,23},{8,24},{9,... | collective-permute-start | bytes 393224 | tf_op jit(solution)/shard_map/ppermute | solution.py:477
  10.7 0.0 collective-permute-done.1.r_b
  10.7 0.0 collective-permute-done.r_a
  10.7 0.1 z_merge.1
  10.8 1.6 %collective-permute-start.2 = (f32[136,128]{1,0:T(8,128)S(1)}, f32[136,128]{1,0:T(8,128)S(1)}, u32[]{:S(2)}, u32[]{:S(2)}) collective-permute-start(f32[136,128]{1,0:T(8,128)S(1)} %get-tuple-element.19), channel_id=1, source_target_pairs={{0,4},{1,5},{2,6},{3,7},{4,0},{5,1},{6,2},{7,3},{8,12},{9,13},{10,... | collective-permute-start | bytes 208904 | tf_op jit(solution)/shard_map/ppermute | solution.py:477
  12.4 1.5 %collective-permute-start.3 = (f32[136,128]{1,0:T(8,128)S(1)}, f32[136,128]{1,0:T(8,128)S(1)}, u32[]{:S(2)}, u32[]{:S(2)}) collective-permute-start(f32[136,128]{1,0:T(8,128)S(1)} %get-tuple-element.20), channel_id=1, source_target_pairs={{0,12},{1,13},{2,14},{3,15},{4,8},{5,9},{6,10},{7,11},{8,4},{9,5},... | collective-permute-start | bytes 208904 | tf_op jit(solution)/shard_map/ppermute | solution.py:477
  13.9 1.3 %collective-permute-done.2.r_a = f32[136,128]{1,0:T(8,128)S(1)} collective-permute-done((f32[136,128]{1,0:T(8,128)S(1)}, f32[136,128]{1,0:T(8,128)S(1)}, u32[]{:S(2)}, u32[]{:S(2)}) %collective-permute-start.2) | collective-permute-done | bytes 69664 | tf_op jit(solution)/shard_map/ppermute | solution.py:477
  15.2 3.7 %collective-permute-done.3.r_b = f32[136,128]{1,0:T(8,128)S(1)} collective-permute-done((f32[136,128]{1,0:T(8,128)S(1)}, f32[136,128]{1,0:T(8,128)S(1)}, u32[]{:S(2)}, u32[]{:S(2)}) %collective-permute-start.3) | collective-permute-done | bytes 69664 | tf_op jit(solution)/shard_map/ppermute | solution.py:477
  19.0 1.2 %collective-permute-start.5 = (f32[96,128]{1,0:T(8,128)S(1)}, f32[96,128]{1,0:T(8,128)S(1)}, u32[]{:S(2)}, u32[]{:S(2)}) collective-permute-start(f32[96,128]{1,0:T(8,128)S(1)} %get-tuple-element.24), channel_id=1, source_target_pairs={{0,16},{1,17},{2,18},{3,19},{4,20},{5,21},{6,22},{7,23},{8,24},{9,... | collective-permute-start | bytes 147464 | tf_op jit(solution)/shard_map/ppermute | solution.py:477
  20.2 0.0 collective-permute-done.4.xa.xb
  20.2 4.3 %collective-permute-done.5.sa.sb = f32[96,128]{1,0:T(8,128)S(1)} collective-permute-done((f32[96,128]{1,0:T(8,128)S(1)}, f32[96,128]{1,0:T(8,128)S(1)}, u32[]{:S(2)}, u32[]{:S(2)}) %collective-permute-start.5) | collective-permute-done | bytes 49184 | tf_op jit(solution)/shard_map/ppermute | solution.py:477
  24.6 0.0 copy-done.1
  24.6 0.0 copy-done.3
  24.6 0.0 copy-done.5
  24.6 0.0 copy-done.7
  24.6 14.8 %redistribute.1 = f32[2560,128]{1,0:T(8,128)} custom-call(f32[2560,128]{1,0:T(8,128)S(1)} %bitcast.6, f32[512,128]{1,0:T(8,128)S(1)} %bitcast.8, s32[512,128]{1,0:T(8,128)S(1)} %bitcast.10, s32[512,128]{1,0:T(8,128)S(1)} %bitcast.12, f32[64,128]{1,0:T(8,128)S(1)} %get-tuple-element.18.zh, f32[136,128]{1,0:T(8,128)S(1)} %get-tuple-element.21.y_lo, ...), custom_call_target="tpu_custom_call" | custom-call | tf_op jit(solution)/shard_map/redistribute/pallas_call | solution.py:520
  (1 shorter events, 0.0 us)
Async XLA Ops:
  0.0 1.3 %copy-start = (f32[1,5,16,32,128]{4,3,2,1,0:T(8,128)S(1)}, f32[1,5,16,32,128]{4,3,2,1,0:T(8,128)}, u32[]{:S(2)}) copy-start(f32[1,5,16,32,128]{4,3,2,1,0:T(8,128)} %param.4) | copy-start | bytes 3932164
  1.3 0.9 %copy-start.2 = (f32[1,16,32,128]{3,2,1,0:T(8,128)S(1)}, f32[1,16,32,128]{3,2,1,0:T(8,128)}, u32[]{:S(2)}) copy-start(f32[1,16,32,128]{3,2,1,0:T(8,128)} %param.5) | copy-start | bytes 786436
  2.3 0.9 %copy-start.4 = (s32[1,16,32,128]{3,2,1,0:T(8,128)S(1)}, s32[1,16,32,128]{3,2,1,0:T(8,128)}, u32[]{:S(2)}) copy-start(s32[1,16,32,128]{3,2,1,0:T(8,128)} %param.6) | copy-start | bytes 786436
  3.2 0.9 %copy-start.6 = (s32[1,16,32,128]{3,2,1,0:T(8,128)S(1)}, s32[1,16,32,128]{3,2,1,0:T(8,128)}, u32[]{:S(2)}) copy-start(s32[1,16,32,128]{3,2,1,0:T(8,128)} %param.7) | copy-start | bytes 786436
  4.2 20.4 %copy-start.1 = (f32[1,5,16,32,128]{4,3,2,1,0:T(8,128)S(1)}, f32[1,5,16,32,128]{4,3,2,1,0:T(8,128)}, u32[]{:S(2)}) copy-start(f32[1,5,16,32,128]{4,3,2,1,0:T(8,128)} %param.4) | copy-start | bytes 3932164
  4.2 20.4 %copy-start.3 = (f32[1,16,32,128]{3,2,1,0:T(8,128)S(1)}, f32[1,16,32,128]{3,2,1,0:T(8,128)}, u32[]{:S(2)}) copy-start(f32[1,16,32,128]{3,2,1,0:T(8,128)} %param.5) | copy-start | bytes 786436
  4.2 20.4 %copy-start.5 = (s32[1,16,32,128]{3,2,1,0:T(8,128)S(1)}, s32[1,16,32,128]{3,2,1,0:T(8,128)}, u32[]{:S(2)}) copy-start(s32[1,16,32,128]{3,2,1,0:T(8,128)} %param.6) | copy-start | bytes 786436
  4.2 20.4 %copy-start.7 = (s32[1,16,32,128]{3,2,1,0:T(8,128)S(1)}, s32[1,16,32,128]{3,2,1,0:T(8,128)}, u32[]{:S(2)}) copy-start(s32[1,16,32,128]{3,2,1,0:T(8,128)} %param.7) | copy-start | bytes 786436
  5.0 5.7 %collective-permute-start.1 = (f32[64,128]{1,0:T(8,128)S(1)}, f32[64,128]{1,0:T(8,128)S(1)}, u32[]{:S(2)}, u32[]{:S(2)}) collective-permute-start(f32[64,128]{1,0:T(8,128)S(1)} %get-tuple-element.15), channel_id=1, source_target_pairs={{0,3},{1,2},{2,1},{3,0},{4,7},{5,6},{6,5},{7,4},{8,11},{9,10},{10,... | collective-permute-start | bytes 98312 | tf_op jit(solution)/shard_map/ppermute | solution.py:477
  7.4 3.3 %collective-permute-start = (f32[64,128]{1,0:T(8,128)S(1)}, f32[64,128]{1,0:T(8,128)S(1)}, u32[]{:S(2)}, u32[]{:S(2)}) collective-permute-start(f32[64,128]{1,0:T(8,128)S(1)} %get-tuple-element.15), channel_id=1, source_target_pairs={{0,1},{1,0},{2,3},{3,2},{4,5},{5,4},{6,7},{7,6},{8,9},{9,8},{10,11... | collective-permute-start | bytes 98312 | tf_op jit(solution)/shard_map/ppermute | solution.py:477
  8.1 12.1 %collective-permute-start.4 = (f32[256,128]{1,0:T(8,128)S(1)}, f32[256,128]{1,0:T(8,128)S(1)}, u32[]{:S(2)}, u32[]{:S(2)}) collective-permute-start(f32[256,128]{1,0:T(8,128)S(1)} %get-tuple-element.23), channel_id=1, source_target_pairs={{0,16},{1,17},{2,18},{3,19},{4,20},{5,21},{6,22},{7,23},{8,24},{9,... | collective-permute-start | bytes 393224 | tf_op jit(solution)/shard_map/ppermute | solution.py:477
  10.8 4.4 %collective-permute-start.2 = (f32[136,128]{1,0:T(8,128)S(1)}, f32[136,128]{1,0:T(8,128)S(1)}, u32[]{:S(2)}, u32[]{:S(2)}) collective-permute-start(f32[136,128]{1,0:T(8,128)S(1)} %get-tuple-element.19), channel_id=1, source_target_pairs={{0,4},{1,5},{2,6},{3,7},{4,0},{5,1},{6,2},{7,3},{8,12},{9,13},{10,... | collective-permute-start | bytes 208904 | tf_op jit(solution)/shard_map/ppermute | solution.py:477
  12.4 6.5 %collective-permute-start.3 = (f32[136,128]{1,0:T(8,128)S(1)}, f32[136,128]{1,0:T(8,128)S(1)}, u32[]{:S(2)}, u32[]{:S(2)}) collective-permute-start(f32[136,128]{1,0:T(8,128)S(1)} %get-tuple-element.20), channel_id=1, source_target_pairs={{0,12},{1,13},{2,14},{3,15},{4,8},{5,9},{6,10},{7,11},{8,4},{9,5},... | collective-permute-start | bytes 208904 | tf_op jit(solution)/shard_map/ppermute | solution.py:477
  19.0 5.6 %collective-permute-start.5 = (f32[96,128]{1,0:T(8,128)S(1)}, f32[96,128]{1,0:T(8,128)S(1)}, u32[]{:S(2)}, u32[]{:S(2)}) collective-permute-start(f32[96,128]{1,0:T(8,128)S(1)} %get-tuple-element.24), channel_id=1, source_target_pairs={{0,16},{1,17},{2,18},{3,19},{4,20},{5,21},{6,22},{7,23},{8,24},{9,... | collective-permute-start | bytes 147464 | tf_op jit(solution)/shard_map/ppermute | solution.py:477

commit v3 on v0

v3 whole, which is shorter than its diff:
```python
import functools
import types

import jax
import jax.numpy as jnp
from jax import lax
from jax.experimental import pallas as pl
from jax.experimental.pallas import tpu as pltpu
from jax.sharding import PartitionSpec as P

NBY = 4
NBZ = 4
AXIS = "boxes"

NFIELD = 5
VF = 5
C1 = 6
C2 = 7
NF = 8
ZU, ZD, YU, YD, XU, XD = 16, 256, 4, 4096, 1 << 28, 1 << 29
LOW = (1 << 24) - 1
EDGE = 13.0


def pairing(stride, extent, devices, odd):
    pairs = []
    for i in range(devices):
        c = i // stride % extent
        partner = ((c + 1) ^ 1) - 1 if odd else c ^ 1
        pairs.append((i, i + (partner % extent - c) * stride))
    return pairs


def lanes_of(shape):
    return lax.broadcasted_iota(jnp.int32, shape, len(shape) - 1)


def roll(value, shift, axis=1):
    if isinstance(shift, int):
        shift %= value.shape[axis]
        if shift == 0:
            return value
    return pltpu.roll(value, shift, axis)


def place():
    me = lax.axis_index(AXIS)
    return me // (NBY * NBZ), me // NBZ % NBY, me % NBZ


def pack_kernel(cx, cy, u_in, vf_in, mask_in, code_in, zp, u, vf, c, mask, code, sems):
    copies = [
        pltpu.make_async_copy(mask_in, mask, sems.at[0]),
        pltpu.make_async_copy(code_in, code, sems.at[1]),
        pltpu.make_async_copy(vf_in, vf, sems.at[2]),
    ]
    for f in range(NFIELD):
        rows = pl.ds(f * cx * cy, cx * cy)
        copies.append(pltpu.make_async_copy(u_in.at[rows, :], u.at[rows, :], sems.at[3 + f]))
    for copy in copies:
        copy.start()
    lane = lanes_of((cy, 128))
    slot = ((lane + 1) & 127) >> 1
    low_lane = (lane & 1) == 0
    copies[0].wait()
    copies[1].wait()
    for x in range(cx):
        rows = pl.ds(x * cy, cy)
        c[rows, :] = jnp.where(mask[rows, :] == 1, code[rows, :], 13).astype(jnp.float32)
    for g in (1, 0):
        acc = jnp.zeros((cy, 128), jnp.float32)
        for k in (3, 2, 1, 0):
            f = 4 * g + k
            if f <= VF:
                copies[3 + f if f < VF else 2].wait()
            for x in range(cx):
                m = cx * k + x
                rows = pl.ds(x * cy, cy)
                if f < NFIELD:
                    part = roll(u[pl.ds((f * cx + x) * cy, cy), :], 2 * m)
                elif f < C2:
                    part = roll((vf if f == VF else c)[rows, :], 2 * m)
                else:
                    part = jnp.where(low_lane, roll(c[rows, :], 2 * m - 1), roll(c[rows, :], 2 * m + 1))
                acc = jnp.where(slot == m, part, acc)
        zp[g * cy : (g + 1) * cy, :] = acc


def faces_kernel(cx, cy, two_x, u, vf, c, y_a, y_b, *xs):
    bx, by, bz = place()

    def y_face(out, high):
        rim = jnp.where(high, cy - 1, 0)
        second = jnp.where(high, cy - 2, 1)

        def column(ref, base, row):
            return ref[pl.ds(base + row, cx, stride=cy), :]

        for f in range(NFIELD):
            out[f * cx : (f + 1) * cx, :] = column(u, f * cx * cy, rim)
        out[VF * cx : (VF + 1) * cx, :] = column(vf, 0, rim)
        out[C1 * cx : (C1 + 1) * cx, :] = column(c, 0, rim)
        out[C2 * cx : (C2 + 1) * cx, :] = column(c, 0, second)

    y_face(y_a, by % 2 == 0)
    y_face(y_b, by % 2 == 1)

    def x_face(out, high):
        rim = jnp.where(high, cx - 1, 0) * cy
        second = jnp.where(high, cx - 2, 1) * cy

        def rows(base, start):
            return pl.ds(pl.multiple_of(base + start, 8), cy)

        for f in range(NFIELD):
            out[f * cy : (f + 1) * cy, :] = u[rows(f * cx * cy, rim), :]
        out[VF * cy : (VF + 1) * cy, :] = vf[rows(0, rim), :]
        out[C1 * cy : (C1 + 1) * cy, :] = c[rows(0, rim), :]
        out[C2 * cy : (C2 + 1) * cy, :] = c[rows(0, second), :]

    x_face(xs[0], bx % 2 == 0)
    if two_x:
        x_face(xs[1], bx % 2 == 1)


def z_merge_kernel(cx, cy, r_a, r_b, ya_in, yb_in, zh, y_a, y_b):
    bx, by, bz = place()
    odd = bz % 2 == 1
    lane = lanes_of((cy, 128))
    low_lane = (lane & 1) == 0
    codes = (lane >= 63) & (lane <= 126)
    for g in range(2):
        rows = slice(g * cy, (g + 1) * cy)
        a, b = r_a[rows, :], r_b[rows, :]
        edge = jnp.where(codes, EDGE, 0.0) if g else jnp.zeros((cy, 128), jnp.float32)
        low = jnp.where(bz > 0, roll(jnp.where(odd, a, b), 1), edge)
        high = jnp.where(bz < NBZ - 1, roll(jnp.where(odd, b, a), -1), edge)
        zh[rows, :] = jnp.where(low_lane, low, high)
    n = NF * cx

    def finish(out, main, high):
        out[:n, :] = main[...]
        rim = jnp.where(high, cy - 1, 0)
        second = jnp.where(high, cy - 2, 1)
        for g in range(2):
            out[n + 2 * g : n + 2 * g + 1, :] = zh[pl.ds(g * cy + rim, 1), :]
            out[n + 2 * g + 1 : n + 2 * g + 2, :] = zh[pl.ds(g * cy + second, 1), :]
        out[n + 4 : n + 8, :] = jnp.zeros((4, 128), jnp.float32)

    finish(y_a, ya_in, by % 2 == 0)
    finish(y_b, yb_in, by % 2 == 1)


def z_edge_rows(cx):
    n = NF * cx
    row = lax.broadcasted_iota(jnp.int32, (n + 8, 128), 0)
    lane = lanes_of((n + 8, 128))
    codes = ((row >= C1 * cx) & (row < n)) | ((row >= n + 2) & (lane >= 63) & (lane <= 126))
    return jnp.where(codes, EDGE, 0.0)


def y_merge_kernel(cx, cy, two_x, r_a, r_b, zh, *refs):
    copies = 2 if two_x else 1
    mains, (y_lo, y_hi), xs = refs[:copies], refs[copies : copies + 2], refs[copies + 2 :]
    bx, by, bz = place()
    odd = by % 2 == 1
    edge = z_edge_rows(cx)
    a, b = r_a[...], r_b[...]
    y_lo[...] = jnp.where(by > 0, jnp.where(odd, a, b), edge)
    y_hi[...] = jnp.where(by < NBY - 1, jnp.where(odd, b, a), edge)
    n = NF * cx

    def x_rim(out, main, high):
        rim = jnp.where(high, cx - 1, 0)
        second = jnp.where(high, cx - 2, 1)
        at = NF * cy
        out[:at, :] = main[...]
        out[at : at + 2 * cy, :] = zh[...]
        at += 2 * cy
        for y in (y_lo, y_hi):
            out[at : at + 4, :] = y[n : n + 4, :]
            at += 4
        for y in (y_lo, y_hi):
            for f in range(NF):
                out[at : at + 1, :] = y[pl.ds(f * cx + rim, 1), :]
                at += 1
            for f in (C1, C2):
                out[at : at + 1, :] = y[pl.ds(f * cx + second, 1), :]
                at += 1
        out[at:, :] = jnp.zeros((out.shape[0] - at, 128), jnp.float32)

    x_rim(xs[0], mains[0], bx % 2 == 0)
    if two_x:
        x_rim(xs[1], mains[1], bx % 2 == 1)


def decode(code):
    qx = (code * 57) >> 9
    rest = code - 9 * qx
    qy = (rest * 11) >> 5
    qz = rest - 3 * qy
    word = 1 + jnp.where(qz == 2, ZU, 0) + jnp.where(qz == 0, ZD, 0)
    word = word * jnp.where(qy == 2, 1 + YU, jnp.where(qy == 0, 1 + YD, 1))
    return word | jnp.where(qx == 2, XU, jnp.where(qx == 0, XD, 0))


def on(word, bits):
    return (word & bits) == bits


def ring_store(ref, lead, value):
    n = value.shape[0]
    ref[(*lead, slice(8, 8 + n), slice(None))] = value
    ref[(*lead, slice(0, 8), slice(None))] = value[n - 8 :]
    ref[(*lead, slice(8 + n, 16 + n), slice(None))] = value[:8]


def y_rows(r, x):
    cx = r.cx
    for f in range(C2):
        r.ht[f, x + 2, 0:1, :] = r.y_hi[f * cx + x : f * cx + x + 1, :]
        r.ht[f, x + 2, 7:8, :] = r.y_lo[f * cx + x : f * cx + x + 1, :]
    r.ht[C1, x + 2, 1:2, :] = r.y_hi[C2 * cx + x : C2 * cx + x + 1, :]
    r.ht[C1, x + 2, 6:7, :] = r.y_lo[C2 * cx + x : C2 * cx + x + 1, :]


def set_words(r, own, layer):
    both = jnp.concatenate([own, r.ht[C1, layer]], axis=0)
    ring_store(r.cw, (layer,), decode(both.astype(jnp.int32)))


def z_pair(r, layer):
    return (r.lane == 2 * layer) | (r.lane == 2 * layer - 1) | ((r.lane == 127) & (layer == 0))


def collect(r, layer, acc):
    return jnp.where(z_pair(r, layer), roll(r.cw[layer, 8 : 8 + r.rows, :], 2 * layer), acc)


def z_halo(r, f, rows_of, shift):
    g, k = f // 4, f % 4
    return roll(rows_of(g), 4 - 2 * r.cx * k + shift)


def spread_counts(r, planes):
    mid = up = down = jnp.zeros((r.rows, 128), jnp.int32)
    for word, bits in planes:
        v = 1 + ((word & YU) << 6) + ((word & YD) << 4)
        if bits is not None:
            v = jnp.where((word & bits) != 0, v, 0)
        mid = mid + v
        up = up + jnp.where((word & XU) != 0, v, 0)
        down = down + jnp.where((word & XD) != 0, v, 0)
    total = mid + roll(up, 2) + roll(down, -2)
    ring_store(r.tmp_i, (0,), total)
    before, after = r.tmp_i[0, 7 : 7 + r.rows, :], r.tmp_i[0, 9 : 9 + r.rows, :]
    return (total & 255) + ((before >> 8) & 255) + ((after >> 16) & 255)


def z_counts(r, inner):
    outer1, outer2 = (decode(r.zf[f].astype(jnp.int32)) for f in (C1, C2))
    r.ow[...] = outer1
    z_count = spread_counts(r, ((outer1, None), (outer2, r.inward), (inner, r.outward)))
    r.i1[...] = spread_counts(r, ((outer1, r.inward),))
    z_weight = r.zf[VF] / z_count.astype(jnp.float32)
    r.zw[0] = z_weight
    for f in range(NFIELD):
        r.zw[f + 1] = z_weight * r.zf[f]


def weigh(r, layer, field, slot=0):
    rows = r.rows
    mid, left, right = (r.cw[layer + d, 8 : 8 + rows, :] for d in (0, -1, 1))
    total = (mid & LOW) + jnp.where((left & XU) != 0, left & LOW, 0) + jnp.where((right & XD) != 0, right & LOW, 0)
    ring_store(r.tmp_i, (slot,), total)
    before, after = r.tmp_i[slot, 7 : 7 + rows, :], r.tmp_i[slot, 9 : 9 + rows, :]
    total = (total & 0x333) + ((before >> 2) & 0x333) + ((after >> 12) & 0x333)
    back = 128 - 2 * layer
    extra = roll(r.i1[...], back)
    first_lane, last_lane = r.lane == 0, r.lane == 127
    count = (total & 15) + jnp.where(first_lane, extra, (roll(total, 1) >> 4) & 15)
    count = count + jnp.where(last_lane, extra, (roll(total, -1) >> 8) & 15)
    inverse = 1.0 / count.astype(jnp.float32)
    r.rc[layer] = inverse[: r.cy]
    weight = field(VF) * inverse
    pair = z_pair(r, layer)
    for f in range(NFIELD + 1):
        w = weight * field(f - 1) if f else weight
        halo = roll(r.zw[f], back)
        ring_store(r.h0, (f, layer), w)
        ring_store(r.hm, (f, layer), w + jnp.where(first_lane, halo, roll(w, 1)))
        ring_store(r.hp, (f, layer), w + jnp.where(last_lane, halo, roll(w, -1)))
        r.zi[f] = jnp.where(pair, roll(w, 2 * layer), r.zi[f])


def own_field(r, x, f):
    base = (f * r.cx + x if f < NFIELD else x) * r.cy
    ref = r.u if f < NFIELD else r.vf
    if not isinstance(base, int):
        base = pl.multiple_of(base, 8)
    return jnp.concatenate([ref[pl.ds(base, r.cy), :], r.ht[f, x + 2]], axis=0)


def z_averages(r):
    rows, word, tmp = r.rows, r.ow[...], r.tmp_f
    sums = []
    for f in range(NFIELD + 1):
        ring_store(tmp, (f,), r.zw[f] + r.zi[f])
        mid, before, after = (tmp[f, s : s + rows, :] for s in (8, 7, 9))
        parts = []
        for d in (0, 1, -1):
            m, b, a = (roll(v, -2 * d) for v in (mid, before, after))
            parts.append(m + jnp.where((word & YU) != 0, a, jnp.where((word & YD) != 0, b, 0.0)))
        sums.append(parts[0] + jnp.where((word & XU) != 0, parts[1], jnp.where((word & XD) != 0, parts[2], 0.0)))
    inverse = 1.0 / sums[0]
    for f in range(NFIELD):
        v = jnp.where((word & r.inward) != 0, sums[f + 1] * inverse, 0.0)
        spread = []
        for bits in (0, YU, YD):
            w = jnp.where((word & bits) != 0, v, 0.0) if bits else v
            up, down = jnp.where((word & XU) != 0, w, 0.0), jnp.where((word & XD) != 0, w, 0.0)
            spread.append(w + roll(up, 2) + roll(down, -2))
        ring_store(tmp, (6 + 2 * f,), spread[1])
        ring_store(tmp, (7 + 2 * f,), spread[2])
        r.dz[f] = spread[0] + tmp[6 + 2 * f, 7 : 7 + rows, :] + tmp[7 + 2 * f, 9 : 9 + rows, :]


def average(r, layer):
    rows = r.rows
    tiles = rows // 8
    for t in range(tiles):
        at = 8 + 8 * t
        word = r.cw[layer, at : at + 8, :]
        zu, zd = (word & ZU) != 0, (word & ZD) != 0
        yu, yd = (word & YU) != 0, (word & YD) != 0
        xu, xd = (word & XU) != 0, (word & XD) != 0
        sums = []
        for f in range(NFIELD + 1):
            parts = []
            for d in (0, 1, -1):
                line = []
                for e in (0, 1, -1):
                    at_e = slice(at + e, at + e + 8)
                    v0, vm, vp = (h[f, layer + d, at_e, :] for h in (r.h0, r.hm, r.hp))
                    line.append(jnp.where(zu, vp, jnp.where(zd, vm, v0)))
                parts.append(line[0] + jnp.where(yu, line[1], jnp.where(yd, line[2], 0.0)))
            sums.append(parts[0] + jnp.where(xu, parts[1], jnp.where(xd, parts[2], 0.0)))
        inverse = 1.0 / sums[0]
        for f in range(NFIELD):
            a = sums[f + 1] * inverse
            r.av[f, layer, at : at + 8, :] = a
            if t == 0:
                r.av[f, layer, 8 + rows : 16 + rows, :] = a
            if t == tiles - 1:
                r.av[f, layer, 0:8, :] = a


def redistribute(r, x, out):
    cx, cy = r.cx, r.cy
    layer = x + 2
    back = 128 - 2 * layer
    lane = lanes_of((8, 128))
    first_lane, last_lane = lane == 0, lane == 127
    for t in range(cy // 8):
        at = 8 + 8 * t
        base = [r.av[f, layer, at : at + 8, :] for f in range(NFIELD)]
        word = r.cw[layer, at : at + 8, :]
        up = [jnp.where((word & ZU) != 0, a, 0.0) for a in base]
        down = [jnp.where((word & ZD) != 0, a, 0.0) for a in base]
        for d in (0, 1, -1):
            for e in (0, 1, -1):
                if d == 0 and e == 0:
                    continue
                at_e = slice(at - e, at - e + 8)
                word = r.cw[layer - d, at_e, :]
                bits = (0, XU, XD)[d] | (0, YU, YD)[e]
                here = on(word, bits)
                here_up, here_down = on(word, bits | ZU), on(word, bits | ZD)
                for f in range(NFIELD):
                    a = r.av[f, layer - d, at_e, :]
                    base[f] = base[f] + jnp.where(here, a, 0.0)
                    up[f] = up[f] + jnp.where(here_up, a, 0.0)
                    down[f] = down[f] + jnp.where(here_down, a, 0.0)
        inverse = r.rc[layer, 8 * t : 8 * t + 8, :]
        for f in range(NFIELD):
            halo = roll(r.dz[f, 8 * t : 8 * t + 8, :], back)
            total = base[f] + jnp.where(first_lane, halo, roll(up[f], 1))
            total = total + jnp.where(last_lane, halo, roll(down[f], -1))
            out[pl.ds(pl.multiple_of((f * cx + x) * cy + 8 * t, 8), 8), :] = total * inverse


def common(r):
    r.rows = r.cy + 8
    r.lane = lanes_of((r.rows, 128))
    even = (r.lane & 1) == 0
    r.inward = jnp.where(even, ZU, ZD)
    r.outward = jnp.where(even, ZD, ZU)
    n = NF * r.cx
    for g in range(2):
        for i, row in enumerate((0, 1)):
            r.hz[0, g, row : row + 1, :] = r.y_hi[n + 2 * g + i : n + 2 * g + i + 1, :]
            r.hz[0, g, 7 - row : 8 - row, :] = r.y_lo[n + 2 * g + i : n + 2 * g + i + 1, :]

    def own_z(g):
        return jnp.concatenate([r.zh[g * r.cy : (g + 1) * r.cy, :], r.hz[0, g]], axis=0)

    return own_z


KEPT = ("cw", "inner", "zi", "h0", "hm", "hp", "rc", "av")
SCRATCH = ("ht", "hz", "zf", "ow", "tmp_i", "tmp_f", "i1", "zw", "dz")


def inner_kernel(cx, cy, *refs):
    names = ("u", "vf", "c", "zh", "y_lo", "y_hi", *KEPT, "res", *SCRATCH)
    r = types.SimpleNamespace(cx=cx, cy=cy, **dict(zip(names, refs)))
    own_z = common(r)
    r.ht[...] = jnp.zeros(r.ht.shape, jnp.float32)
    for x in range(cx):
        y_rows(r, x)

    def words(x, acc):
        set_words(r, r.c[pl.ds(pl.multiple_of(x * cy, 8), cy), :], x + 2)
        return collect(r, x + 2, acc)

    inner = lax.fori_loop(0, cx, words, jnp.ones((r.rows, 128), jnp.int32), unroll=4)
    r.inner[...] = inner
    for f in range(NF):
        r.zf[f] = z_halo(r, f, own_z, 0)
    z_counts(r, inner)
    r.zi[...] = jnp.zeros(r.zi.shape, jnp.float32)

    def weigh_two(i, _):
        for j in range(2):
            x = 1 + 2 * i + j
            weigh(r, x + 2, functools.partial(own_field, r, x), j)
        return 0

    lax.fori_loop(0, (cx - 2) // 2, weigh_two, 0)
    z_averages(r)

    def average_one(layer, _):
        average(r, layer)
        return 0

    lax.fori_loop(4, cx, average_one, 0)

    def spread_one(x, _):
        redistribute(r, x, r.res)
        return 0

    lax.fori_loop(3, cx - 3, spread_one, 0)


def outer_kernel(cx, cy, nbx, *refs):
    kept_in = len(KEPT)
    names = ("u", "vf", "c", "zh", "y_lo", "y_hi", "res", "xa", "xb")
    ins = refs[: len(names)]
    rest = refs[len(names) + kept_in :]
    r = types.SimpleNamespace(cx=cx, cy=cy, **dict(zip(names, ins)))
    r.__dict__.update(zip(("out", *KEPT, *SCRATCH, "rim", "sems"), rest))
    size = cx * cy

    def send(src, first, last, base):
        copies = []
        for f in range(NFIELD):
            rows = pl.ds(f * size + first * cy, (last - first) * cy)
            copies.append(pltpu.make_async_copy(src.at[rows, :], r.out.at[rows, :], r.sems.at[base + f]))
        for copy in copies:
            copy.start()
        return copies

    copies = send(r.res, 3, cx - 3, 0)
    own_z = common(r)
    bx, by, bz = place()
    x_odd = bx % 2 == 1
    has_lo, has_hi = bx > 0, bx < nbx - 1

    def x_part(side, first, count):
        a, b = r.xa[first : first + count, :], r.xb[first : first + count, :]
        return jnp.where(x_odd, a, b) if side == 0 else jnp.where(x_odd, b, a)

    def x_raw(f, side):
        edge = EDGE if f >= C1 else 0.0
        return jnp.where(has_hi if side else has_lo, x_part(side, f * cy, cy), edge)

    zrow = NF * cy
    edges = zrow + 2 * cy
    for x in (0, cx - 1):
        y_rows(r, x)
    for side, layer, second in ((0, 1, 0), (1, cx + 2, cx + 3)):
        present = has_hi if side else has_lo
        for y, row1, row2 in ((0, 7, 6), (1, 0, 1)):
            base = edges + 8 + 10 * y

            def rim(i, edge, base=base, side=side, present=present):
                return jnp.where(present, x_part(side, base + i, 1), edge)

            for f in range(C1):
                r.ht[f, layer, row1 : row1 + 1, :] = rim(f, 0.0)
            r.ht[C1, layer, row1 : row1 + 1, :] = rim(C1, EDGE)
            r.ht[C1, layer, row2 : row2 + 1, :] = rim(C2, EDGE)
            r.ht[C1, second, row1 : row1 + 1, :] = rim(NF, EDGE)
            r.ht[C1, second, row2 : row2 + 1, :] = rim(NF + 1, EDGE)
    set_words(r, x_raw(C2, 0), 0)
    set_words(r, x_raw(C1, 0), 1)
    set_words(r, x_raw(C1, 1), cx + 2)
    set_words(r, x_raw(C2, 1), cx + 3)

    for side in (0, 1):
        for g in range(2):
            for i, row in enumerate((0, 1)):
                lo, hi = edges + 2 * g + i, edges + 4 + 2 * g + i
                r.hz[1 + side, g, row : row + 1, :] = x_part(side, hi, 1)
                r.hz[1 + side, g, 7 - row : 8 - row, :] = x_part(side, lo, 1)

    def x_z(side):
        return lambda g: jnp.concatenate([x_part(side, zrow + g * cy, cy), r.hz[1 + side, g]], axis=0)

    below = (r.lane == 127) | (r.lane <= 2)
    above = (r.lane >= 2 * cx + 3) & (r.lane <= 2 * cx + 6)
    for f in range(NF):
        edge = EDGE if f >= C1 else 0.0
        lo = jnp.where(has_lo, z_halo(r, f, x_z(0), -2 * cx), edge)
        hi = jnp.where(has_hi, z_halo(r, f, x_z(1), 2 * cx), edge)
        r.zf[f] = jnp.where(below, lo, jnp.where(above, hi, z_halo(r, f, own_z, 0)))
    inner = r.inner[...]
    for layer in (0, 1, cx + 2, cx + 3):
        inner = collect(r, layer, inner)
    z_counts(r, inner)
    weigh(r, 1, lambda f: jnp.concatenate([x_raw(f, 0), r.ht[f, 1]], axis=0), 0)
    weigh(r, 2, functools.partial(own_field, r, 0), 1)
    weigh(r, cx + 1, functools.partial(own_field, r, cx - 1), 2)
    weigh(r, cx + 2, lambda f: jnp.concatenate([x_raw(f, 1), r.ht[f, cx + 2]], axis=0), 3)
    z_averages(r)

    def average_one(i, _):
        average(r, 1 + i + jnp.where(i >= 3, cx - 4, 0))
        return 0

    lax.fori_loop(0, 6, average_one, 0)

    def spread_one(x, _):
        redistribute(r, x, r.rim)
        return 0

    lax.fori_loop(0, 3, spread_one, 0)
    copies += send(r.rim, 0, 3, NFIELD)
    lax.fori_loop(cx - 3, cx, spread_one, 0)
    copies += send(r.rim, cx - 3, cx, 2 * NFIELD)
    for copy in copies:
        copy.wait()


def call(kernel, ins, outs, scratch=(), name=None, grant=8, flops=0, **kwargs):
    return pl.pallas_call(
        kernel,
        in_specs=ins,
        out_specs=tuple(pl.BlockSpec(memory_space=o.memory_space) for o in outs),
        out_shape=tuple(outs),
        scratch_shapes=scratch,
        name=name,
        cost_estimate=pl.CostEstimate(flops=flops, transcendentals=0, bytes_accessed=0),
        compiler_params=pltpu.CompilerParams(vmem_limit_bytes=grant << 20),
        **kwargs,
    )


def per_device(conserved, volume_fraction, cut_mask, merge_code):
    _, cx, cy, cz = cut_mask.shape
    devices = lax.axis_size(AXIS)
    nbx = devices // (NBY * NBZ)
    two_x = nbx > 2
    cells = cx * cy
    u = conserved.reshape(NFIELD * cells, cz)
    vf, mask, code = (a.reshape(cells, cz) for a in (volume_fraction, cut_mask, merge_code))
    f32, i32 = jnp.float32, jnp.int32
    on_chip, far = pl.BlockSpec(memory_space=pltpu.VMEM), pl.BlockSpec(memory_space=pltpu.HBM)

    def vmem(*shape, dtype=f32):
        return pltpu.VMEM((*shape, cz), dtype)

    def swap(value, stride, extent, odd):
        return lax.ppermute(value, AXIS, pairing(stride, extent, devices, odd))

    n = NF * cx
    copies = 2 if two_x else 1
    zp, u, vf, c = call(
        functools.partial(pack_kernel, cx, cy),
        [far] * 4,
        [vmem(2 * cy), vmem(NFIELD * cells), vmem(cells), vmem(cells)],
        [vmem(cells, dtype=i32), vmem(cells, dtype=i32), pltpu.SemaphoreType.DMA((3 + NFIELD,))],
        "pack",
    )(*(pltpu.with_memory_space_constraint(a, pltpu.HBM) for a in (u, vf, mask, code)))
    za, zb = swap(zp, 1, NBZ, False), swap(zp, 1, NBZ, True)
    ya, yb, *xs = call(
        functools.partial(faces_kernel, cx, cy, two_x),
        [on_chip] * 3,
        [vmem(n), vmem(n)] + [vmem(NF * cy)] * copies,
        name="faces",
        flops=1 << 20,
    )(u, vf, c)
    zh, ya, yb = call(
        functools.partial(z_merge_kernel, cx, cy), [on_chip] * 4, [vmem(2 * cy), vmem(n + 8), vmem(n + 8)], name="z_merge"
    )(za, zb, ya, yb)
    ya, yb = swap(ya, NBZ, NBY, False), swap(yb, NBZ, NBY, True)
    y_lo, y_hi, *xs = call(
        functools.partial(y_merge_kernel, cx, cy, two_x),
        [on_chip] * (3 + copies),
        [vmem(n + 8), vmem(n + 8)] + [vmem(NF * cy + 2 * cy + 32)] * copies,
        name="y_merge",
    )(ya, yb, zh, *xs)
    xs = [swap(x, NBY * NBZ, nbx, odd) for odd, x in enumerate(xs)]
    xa, xb = xs if two_x else xs * 2

    rows, ring, layers = cy + 8, cy + 24, cx + 4
    kept = [
        vmem(layers, ring, dtype=i32),
        vmem(rows, dtype=i32),
        vmem(NFIELD + 1, rows),
        vmem(NFIELD + 1, layers, ring),
        vmem(NFIELD + 1, layers, ring),
        vmem(NFIELD + 1, layers, ring),
        vmem(layers, cy),
        vmem(NFIELD, layers, ring),
    ]
    scratch = [
        vmem(C2, layers, 8),
        vmem(3, 2, 8),
        vmem(NF, rows),
        vmem(rows, dtype=i32),
        vmem(4, ring, dtype=i32),
        vmem(6 + 2 * NFIELD, ring),
        vmem(rows, dtype=i32),
        vmem(NFIELD + 1, rows),
        vmem(NFIELD, rows),
    ]
    *state, res = call(
        functools.partial(inner_kernel, cx, cy),
        [on_chip] * 6,
        kept + [vmem(NFIELD * cells)],
        scratch,
        "inner",
        flops=1 << 26,
    )(u, vf, c, zh, y_lo, y_hi)
    first = 9
    out, *_ = call(
        functools.partial(outer_kernel, cx, cy, nbx),
        [on_chip] * (first + len(kept)),
        [pltpu.HBM((NFIELD * cells, cz), f32)] + kept,
        scratch + [vmem(NFIELD * cells), pltpu.SemaphoreType.DMA((3 * NFIELD,))],
        "outer",
        flops=1 << 25,
        input_output_aliases={first + i: 1 + i for i in range(len(kept))},
    )(u, vf, c, zh, y_lo, y_hi, res, xa, xb, *state)
    return out.reshape(conserved.shape)


def solution(mesh):
    return jax.shard_map(
        per_device,
        mesh=mesh,
        in_specs=(
            P(AXIS, None, None, None, None),
            P(AXIS, None, None, None),
            P(AXIS, None, None, None),
            P(AXIS, None, None, None),
        ),
        out_specs=P(AXIS, None, None, None, None),
        check_vma=False,
    )
```

time: 219 us -> 30.8 us (0.14)
  the two profiles are of different devices: /device:TPU:5 before, /device:TPU:0 now
where the time goes in v3:
time: 30.8 us; the launch traced here: 30.6 us
  Pallas kernels  16.1 us (52%)
  starting transfers between devices  9.84 us (32%)
  waiting for transfers between devices  4.65 us (15%)
    ppermute x5, starting transfers between devices, swap(): return lax.ppermute(value, AXIS, pairing(stride, extent, devices, odd))  9.84 us
    pallas_call x1, Pallas kernels, per_device(): call(functools.partial(inner_kernel, cx, cy), [on_chip] * 6, kept + [vmem...  8.86 us
    pallas_call x1, Pallas kernels, per_device(): call(functools.partial(outer_kernel, cx, cy, nbx), [on_chip] * (first + l...  4.72 us
    ppermute x5, waiting for transfers between devices, swap(): return lax.ppermute(value, AXIS, pairing(stride, extent, devices, odd))  4.65 us
    pallas_call x1, Pallas kernels, per_device(): call(functools.partial(pack_kernel, cx, cy), [far] * 4, [vmem(2 * cy), vm...  2.24 us
  transfers between devices with their start and end apart: 5, of which 3 were waited for; matrix products, arithmetic and copies ran while one was open for 0% of the time, Pallas kernels for 29%

profile of v3, /device:TPU:0, one launch (start us, length us, event | category | flops | bytes accessed | tf_op | source)
XLA Modules:
  0.0 30.6 jit_solution(2082327353910534176)
XLA Ops:
  0.0 2.2 %pack.1 = (f32[64,128]{1,0:T(8,128)S(1)}, f32[2560,128]{1,0:T(8,128)S(1)}, f32[512,128]{1,0:T(8,128)S(1)}, f32[512,128]{1,0:T(8,128)S(1)}) custom-call(f32[2560,128]{1,0:T(8,128)} %bitcast.5, f32[512,128]{1,0:T(8,128)} %bitcast.6, s32[512,128]{1,0:T(8,128)} %bitcast.7, s32[512,128]{1,0:T(8,128)} %bitcast.8), custom_call_target="tpu_custom_call" | custom-call | tf_op jit(solution)/shard_map/pack/pallas_call | solution.py:588
  2.2 2.5 %collective-permute-start.1 = (f32[64,128]{1,0:T(8,128)S(1)}, f32[64,128]{1,0:T(8,128)S(1)}, u32[]{:S(2)}, u32[]{:S(2)}) collective-permute-start(f32[64,128]{1,0:T(8,128)S(1)} %get-tuple-element.31), channel_id=1, source_target_pairs={{0,3},{1,2},{2,1},{3,0},{4,7},{5,6},{6,5},{7,4},{8,11},{9,10},{10,... | collective-permute-start | bytes 98312 | tf_op jit(solution)/shard_map/ppermute | solution.py:584
  4.7 0.7 %collective-permute-start = (f32[64,128]{1,0:T(8,128)S(1)}, f32[64,128]{1,0:T(8,128)S(1)}, u32[]{:S(2)}, u32[]{:S(2)}) collective-permute-start(f32[64,128]{1,0:T(8,128)S(1)} %get-tuple-element.31), channel_id=1, source_target_pairs={{0,1},{1,0},{2,3},{3,2},{4,5},{5,4},{6,7},{7,6},{8,9},{9,8},{10,11... | collective-permute-start | bytes 98312 | tf_op jit(solution)/shard_map/ppermute | solution.py:584
  5.4 0.1 faces.1
  5.5 1.0 %collective-permute-done.1.r_b = f32[64,128]{1,0:T(8,128)S(1)} collective-permute-done((f32[64,128]{1,0:T(8,128)S(1)}, f32[64,128]{1,0:T(8,128)S(1)}, u32[]{:S(2)}, u32[]{:S(2)}) %collective-permute-start.1) | collective-permute-done | bytes 32800 | tf_op jit(solution)/shard_map/ppermute | solution.py:584
  6.5 0.0 collective-permute-done.r_a
  6.5 0.1 z_merge.1
  6.6 2.5 %collective-permute-start.2 = (f32[136,128]{1,0:T(8,128)S(1)}, f32[136,128]{1,0:T(8,128)S(1)}, u32[]{:S(2)}, u32[]{:S(2)}) collective-permute-start(f32[136,128]{1,0:T(8,128)S(1)} %get-tuple-element.35), channel_id=1, source_target_pairs={{0,4},{1,5},{2,6},{3,7},{4,0},{5,1},{6,2},{7,3},{8,12},{9,13},{10,... | collective-permute-start | bytes 208904 | tf_op jit(solution)/shard_map/ppermute | solution.py:584
  9.1 1.5 %collective-permute-start.3 = (f32[136,128]{1,0:T(8,128)S(1)}, f32[136,128]{1,0:T(8,128)S(1)}, u32[]{:S(2)}, u32[]{:S(2)}) collective-permute-start(f32[136,128]{1,0:T(8,128)S(1)} %get-tuple-element.36), channel_id=1, source_target_pairs={{0,12},{1,13},{2,14},{3,15},{4,8},{5,9},{6,10},{7,11},{8,4},{9,5},... | collective-permute-start | bytes 208904 | tf_op jit(solution)/shard_map/ppermute | solution.py:584
  10.6 1.8 %collective-permute-done.2.r_a = f32[136,128]{1,0:T(8,128)S(1)} collective-permute-done((f32[136,128]{1,0:T(8,128)S(1)}, f32[136,128]{1,0:T(8,128)S(1)}, u32[]{:S(2)}, u32[]{:S(2)}) %collective-permute-start.2) | collective-permute-done | bytes 69664 | tf_op jit(solution)/shard_map/ppermute | solution.py:584
  12.5 1.9 %collective-permute-done.3.r_b = f32[136,128]{1,0:T(8,128)S(1)} collective-permute-done((f32[136,128]{1,0:T(8,128)S(1)}, f32[136,128]{1,0:T(8,128)S(1)}, u32[]{:S(2)}, u32[]{:S(2)}) %collective-permute-start.3) | collective-permute-done | bytes 69664 | tf_op jit(solution)/shard_map/ppermute | solution.py:584
  14.4 2.7 %collective-permute-start.4 = (f32[352,128]{1,0:T(8,128)S(1)}, f32[352,128]{1,0:T(8,128)S(1)}, u32[]{:S(2)}, u32[]{:S(2)}) collective-permute-start(f32[352,128]{1,0:T(8,128)S(1)} %get-tuple-element.41), channel_id=1, source_target_pairs={{0,16},{1,17},{2,18},{3,19},{4,20},{5,21},{6,22},{7,23},{8,24},{9,... | collective-permute-start | bytes 540680 | tf_op jit(solution)/shard_map/ppermute | solution.py:584
  17.0 8.9 %inner.1 = (s32[20,56,128]{2,1,0:T(8,128)S(1)}, s32[40,128]{1,0:T(8,128)S(1)}, f32[6,40,128]{2,1,0:T(8,128)S(1)}, f32[6,20,56,128]{3,2,1,0:T(8,128)S(1)}, f32[6,...) custom-call(f32[2560,128]{1,0:T(8,128)S(1)} %get-tuple-element.28.u., ...), custom_call_target="tpu_custom_call" | custom-call | flops 67108864 | tf_op jit(solution)/shard_map/inner/pallas_call | solution.py:638
  25.9 0.0 collective-permute-done.4.refs_7_.refs_8_
  25.9 4.7 %outer.1 = (f32[2560,128]{1,0:T(8,128)}, s32[20,56,128]{2,1,0:T(8,128)S(1)}, s32[40,128]{1,0:T(8,128)S(1)}, f32[6,40,128]{2,1,0:T(8,128)S(1)}, f32[6,20,56,128]{...) custom-call(f32[2560,128]{1,0:T(8,128)S(1)} %get-tuple-element.28.u., ...), custom_call_target="tpu_custom_call", output_to_operand_aliasing={{1}: (9, {}), {2}: (10, {}), {3}: (11, {}), {4}: (12, {}), ... | custom-call | flops 33554432 | tf_op jit(solution)/shard_map/outer/pallas_call | solution.py:647
  (1 shorter events, 0.0 us)
Async XLA Ops:
  2.2 4.3 %collective-permute-start.1 = (f32[64,128]{1,0:T(8,128)S(1)}, f32[64,128]{1,0:T(8,128)S(1)}, u32[]{:S(2)}, u32[]{:S(2)}) collective-permute-start(f32[64,128]{1,0:T(8,128)S(1)} %get-tuple-element.31), channel_id=1, source_target_pairs={{0,3},{1,2},{2,1},{3,0},{4,7},{5,6},{6,5},{7,4},{8,11},{9,10},{10,... | collective-permute-start | bytes 98312 | tf_op jit(solution)/shard_map/ppermute | solution.py:584
  4.7 1.8 %collective-permute-start = (f32[64,128]{1,0:T(8,128)S(1)}, f32[64,128]{1,0:T(8,128)S(1)}, u32[]{:S(2)}, u32[]{:S(2)}) collective-permute-start(f32[64,128]{1,0:T(8,128)S(1)} %get-tuple-element.31), channel_id=1, source_target_pairs={{0,1},{1,0},{2,3},{3,2},{4,5},{5,4},{6,7},{7,6},{8,9},{9,8},{10,11... | collective-permute-start | bytes 98312 | tf_op jit(solution)/shard_map/ppermute | solution.py:584
  6.6 5.9 %collective-permute-start.2 = (f32[136,128]{1,0:T(8,128)S(1)}, f32[136,128]{1,0:T(8,128)S(1)}, u32[]{:S(2)}, u32[]{:S(2)}) collective-permute-start(f32[136,128]{1,0:T(8,128)S(1)} %get-tuple-element.35), channel_id=1, source_target_pairs={{0,4},{1,5},{2,6},{3,7},{4,0},{5,1},{6,2},{7,3},{8,12},{9,13},{10,... | collective-permute-start | bytes 208904 | tf_op jit(solution)/shard_map/ppermute | solution.py:584
  9.1 5.2 %collective-permute-start.3 = (f32[136,128]{1,0:T(8,128)S(1)}, f32[136,128]{1,0:T(8,128)S(1)}, u32[]{:S(2)}, u32[]{:S(2)}) collective-permute-start(f32[136,128]{1,0:T(8,128)S(1)} %get-tuple-element.36), channel_id=1, source_target_pairs={{0,12},{1,13},{2,14},{3,15},{4,8},{5,9},{6,10},{7,11},{8,4},{9,5},... | collective-permute-start | bytes 208904 | tf_op jit(solution)/shard_map/ppermute | solution.py:584
  14.4 11.5 %collective-permute-start.4 = (f32[352,128]{1,0:T(8,128)S(1)}, f32[352,128]{1,0:T(8,128)S(1)}, u32[]{:S(2)}, u32[]{:S(2)}) collective-permute-start(f32[352,128]{1,0:T(8,128)S(1)} %get-tuple-element.41), channel_id=1, source_target_pairs={{0,16},{1,17},{2,18},{3,19},{4,20},{5,21},{6,22},{7,23},{8,24},{9,... | collective-permute-start | bytes 540680 | tf_op jit(solution)/shard_map/ppermute | solution.py:584

commit v4 on v3

--- a/solution.py
+++ b/solution.py
@@ -175,8 +175,16 @@
         second = jnp.where(high, cx - 2, 1)
         at = NF * cy
         out[:at, :] = main[...]
-        out[at : at + 2 * cy, :] = zh[...]
-        at += 2 * cy
+        lane = lanes_of((8, 128))
+        spot = (lane - jnp.where(high, 2 * cx - 5, 2 * cx - 1)) & (2 * cx - 1)
+        tile = jnp.zeros((8, 128), jnp.float32)
+        for t in range(cy // 8):
+            for g in range(2):
+                start = 8 * t + 4 * g
+                part = roll(zh[g * cy + 8 * t : g * cy + 8 * t + 8, :], start)
+                tile = jnp.where((spot >= start) & (spot < start + 4), part, tile)
+        out[at : at + 8, :] = tile
+        at += 8
         for y in (y_lo, y_hi):
             out[at : at + 4, :] = y[n : n + 4, :]
             at += 4
@@ -212,7 +220,14 @@
     n = value.shape[0]
     ref[(*lead, slice(8, 8 + n), slice(None))] = value
     ref[(*lead, slice(0, 8), slice(None))] = value[n - 8 :]
-    ref[(*lead, slice(8 + n, 16 + n), slice(None))] = value[:8]
+
+
+def ring_load(ref, lead, step):
+    n = ref.shape[-2] - 16
+    if step <= 0:
+        return ref[(*lead, slice(8 + step, 8 + step + n), slice(None))]
+    own = ref[(*lead, slice(8 + step, n + step), slice(None))]
+    return jnp.concatenate([own, ref[(*lead, slice(step, 8 + step), slice(None))]], axis=0)
 
 
 def y_rows(r, x):
@@ -237,9 +252,9 @@
     return jnp.where(z_pair(r, layer), roll(r.cw[layer, 8 : 8 + r.rows, :], 2 * layer), acc)
 
 
-def z_halo(r, f, rows_of, shift):
+def z_halo(r, f, own):
     g, k = f // 4, f % 4
-    return roll(rows_of(g), 4 - 2 * r.cx * k + shift)
+    return roll(own(g), 4 - 2 * r.cx * k)
 
 
 def spread_counts(r, planes):
@@ -253,7 +268,7 @@
         down = down + jnp.where((word & XD) != 0, v, 0)
     total = mid + roll(up, 2) + roll(down, -2)
     ring_store(r.tmp_i, (0,), total)
-    before, after = r.tmp_i[0, 7 : 7 + r.rows, :], r.tmp_i[0, 9 : 9 + r.rows, :]
+    before, after = ring_load(r.tmp_i, (0,), -1), ring_load(r.tmp_i, (0,), 1)
     return (total & 255) + ((before >> 8) & 255) + ((after >> 16) & 255)
 
 
@@ -268,29 +283,37 @@
         r.zw[f + 1] = z_weight * r.zf[f]
 
 
-def weigh(r, layer, field, slot=0):
+def weigh(r, group):
     rows = r.rows
-    mid, left, right = (r.cw[layer + d, 8 : 8 + rows, :] for d in (0, -1, 1))
-    total = (mid & LOW) + jnp.where((left & XU) != 0, left & LOW, 0) + jnp.where((right & XD) != 0, right & LOW, 0)
-    ring_store(r.tmp_i, (slot,), total)
-    before, after = r.tmp_i[slot, 7 : 7 + rows, :], r.tmp_i[slot, 9 : 9 + rows, :]
-    total = (total & 0x333) + ((before >> 2) & 0x333) + ((after >> 12) & 0x333)
-    back = 128 - 2 * layer
-    extra = roll(r.i1[...], back)
     first_lane, last_lane = r.lane == 0, r.lane == 127
-    count = (total & 15) + jnp.where(first_lane, extra, (roll(total, 1) >> 4) & 15)
-    count = count + jnp.where(last_lane, extra, (roll(total, -1) >> 8) & 15)
-    inverse = 1.0 / count.astype(jnp.float32)
-    r.rc[layer] = inverse[: r.cy]
-    weight = field(VF) * inverse
-    pair = z_pair(r, layer)
-    for f in range(NFIELD + 1):
-        w = weight * field(f - 1) if f else weight
-        halo = roll(r.zw[f], back)
-        ring_store(r.h0, (f, layer), w)
-        ring_store(r.hm, (f, layer), w + jnp.where(first_lane, halo, roll(w, 1)))
-        ring_store(r.hp, (f, layer), w + jnp.where(last_lane, halo, roll(w, -1)))
-        r.zi[f] = jnp.where(pair, roll(w, 2 * layer), r.zi[f])
+    totals = []
+    for slot, (layer, _) in enumerate(group):
+        mid, left, right = (r.cw[layer + d, 8 : 8 + rows, :] for d in (0, -1, 1))
+        total = (mid & LOW) + jnp.where((left & XU) != 0, left & LOW, 0)
+        ring_store(r.tmp_i, (slot,), total + jnp.where((right & XD) != 0, right & LOW, 0))
+    for slot, (layer, _) in enumerate(group):
+        total, before, after = (ring_load(r.tmp_i, (slot,), step) for step in (0, -1, 1))
+        total = (total & 0x333) + ((before >> 2) & 0x333) + ((after >> 12) & 0x333)
+        totals.append((total, roll(total, 1), roll(total, -1), roll(r.i1[...], -2 * layer)))
+    for slot, (layer, field) in enumerate(group):
+        total, below, above, extra = totals[slot]
+        count = (total & 15) + jnp.where(first_lane, extra, (below >> 4) & 15)
+        count = count + jnp.where(last_lane, extra, (above >> 8) & 15)
+        inverse = 1.0 / count.astype(jnp.float32)
+        r.rc[layer] = inverse[: r.cy]
+        ring_store(r.h0, (0, layer), field(VF) * inverse)
+    for slot, (layer, field) in enumerate(group):
+        weight = ring_load(r.h0, (0, layer), 0)
+        pair = z_pair(r, layer)
+        for f in range(NFIELD + 1):
+            w = weight
+            if f:
+                w = weight * field(f - 1)
+                ring_store(r.h0, (f, layer), w)
+            halo = roll(r.zw[f], -2 * layer)
+            ring_store(r.hm, (f, layer), w + jnp.where(first_lane, halo, roll(w, 1)))
+            ring_store(r.hp, (f, layer), w + jnp.where(last_lane, halo, roll(w, -1)))
+            r.zi[f] = jnp.where(pair, roll(w, 2 * layer), r.zi[f])
 
 
 def own_field(r, x, f):
@@ -302,11 +325,11 @@
 
 
 def z_averages(r):
-    rows, word, tmp = r.rows, r.ow[...], r.tmp_f
+    word, tmp = r.ow[...], r.tmp_f
     sums = []
     for f in range(NFIELD + 1):
         ring_store(tmp, (f,), r.zw[f] + r.zi[f])
-        mid, before, after = (tmp[f, s : s + rows, :] for s in (8, 7, 9))
+        mid, before, after = (ring_load(tmp, (f,), step) for step in (0, -1, 1))
         parts = []
         for d in (0, 1, -1):
             m, b, a = (roll(v, -2 * d) for v in (mid, before, after))
@@ -322,7 +345,7 @@
             spread.append(w + roll(up, 2) + roll(down, -2))
         ring_store(tmp, (6 + 2 * f,), spread[1])
         ring_store(tmp, (7 + 2 * f,), spread[2])
-        r.dz[f] = spread[0] + tmp[6 + 2 * f, 7 : 7 + rows, :] + tmp[7 + 2 * f, 9 : 9 + rows, :]
+        r.dz[f] = spread[0] + ring_load(tmp, (6 + 2 * f,), -1) + ring_load(tmp, (7 + 2 * f,), 1)
 
 
 def average(r, layer):
@@ -340,7 +363,8 @@
             for d in (0, 1, -1):
                 line = []
                 for e in (0, 1, -1):
-                    at_e = slice(at + e, at + e + 8)
+                    base = 0 if t == tiles - 1 and e == 1 else at
+                    at_e = slice(base + e, base + e + 8)
                     v0, vm, vp = (h[f, layer + d, at_e, :] for h in (r.h0, r.hm, r.hp))
                     line.append(jnp.where(zu, vp, jnp.where(zd, vm, v0)))
                 parts.append(line[0] + jnp.where(yu, line[1], jnp.where(yd, line[2], 0.0)))
@@ -349,8 +373,6 @@
         for f in range(NFIELD):
             a = sums[f + 1] * inverse
             r.av[f, layer, at : at + 8, :] = a
-            if t == 0:
-                r.av[f, layer, 8 + rows : 16 + rows, :] = a
             if t == tiles - 1:
                 r.av[f, layer, 0:8, :] = a
 
@@ -426,17 +448,11 @@
     inner = lax.fori_loop(0, cx, words, jnp.ones((r.rows, 128), jnp.int32), unroll=4)
     r.inner[...] = inner
     for f in range(NF):
-        r.zf[f] = z_halo(r, f, own_z, 0)
+        r.zf[f] = z_halo(r, f, own_z)
     z_counts(r, inner)
     r.zi[...] = jnp.zeros(r.zi.shape, jnp.float32)
 
-    def weigh_two(i, _):
-        for j in range(2):
-            x = 1 + 2 * i + j
-            weigh(r, x + 2, functools.partial(own_field, r, x), j)
-        return 0
-
-    lax.fori_loop(0, (cx - 2) // 2, weigh_two, 0)
+    weigh(r, [(x + 2, functools.partial(own_field, r, x)) for x in range(1, cx - 1)])
     z_averages(r)
 
     def average_one(layer, _):
@@ -485,7 +501,7 @@
         return jnp.where(has_hi if side else has_lo, x_part(side, f * cy, cy), edge)
 
     zrow = NF * cy
-    edges = zrow + 2 * cy
+    edges = zrow + 8
     for x in (0, cx - 1):
         y_rows(r, x)
     for side, layer, second in ((0, 1, 0), (1, cx + 2, cx + 3)):
@@ -514,24 +530,32 @@
                 r.hz[1 + side, g, row : row + 1, :] = x_part(side, hi, 1)
                 r.hz[1 + side, g, 7 - row : 8 - row, :] = x_part(side, lo, 1)
 
-    def x_z(side):
-        return lambda g: jnp.concatenate([x_part(side, zrow + g * cy, cy), r.hz[1 + side, g]], axis=0)
+    def x_z(side, f):
+        g, k = f // 4, f % 4
+        shift = 4 - 2 * cx * k + (2 * cx if side else -2 * cx)
+        tile = x_part(side, zrow, 8)
+        tiles = [roll(tile, shift - 8 * t - 4 * g) for t in range(cy // 8)]
+        return jnp.concatenate([*tiles, roll(r.hz[1 + side, g], shift)], axis=0)
 
     below = (r.lane == 127) | (r.lane <= 2)
     above = (r.lane >= 2 * cx + 3) & (r.lane <= 2 * cx + 6)
     for f in range(NF):
         edge = EDGE if f >= C1 else 0.0
-        lo = jnp.where(has_lo, z_halo(r, f, x_z(0), -2 * cx), edge)
-        hi = jnp.where(has_hi, z_halo(r, f, x_z(1), 2 * cx), edge)
-        r.zf[f] = jnp.where(below, lo, jnp.where(above, hi, z_halo(r, f, own_z, 0)))
+        lo, hi = jnp.where(has_lo, x_z(0, f), edge), jnp.where(has_hi, x_z(1, f), edge)
+        r.zf[f] = jnp.where(below, lo, jnp.where(above, hi, z_halo(r, f, own_z)))
     inner = r.inner[...]
     for layer in (0, 1, cx + 2, cx + 3):
         inner = collect(r, layer, inner)
     z_counts(r, inner)
-    weigh(r, 1, lambda f: jnp.concatenate([x_raw(f, 0), r.ht[f, 1]], axis=0), 0)
-    weigh(r, 2, functools.partial(own_field, r, 0), 1)
-    weigh(r, cx + 1, functools.partial(own_field, r, cx - 1), 2)
-    weigh(r, cx + 2, lambda f: jnp.concatenate([x_raw(f, 1), r.ht[f, cx + 2]], axis=0), 3)
+    weigh(
+        r,
+        [
+            (1, lambda f: jnp.concatenate([x_raw(f, 0), r.ht[f, 1]], axis=0)),
+            (2, functools.partial(own_field, r, 0)),
+            (cx + 1, functools.partial(own_field, r, cx - 1)),
+            (cx + 2, lambda f: jnp.concatenate([x_raw(f, 1), r.ht[f, cx + 2]], axis=0)),
+        ],
+    )
     z_averages(r)
 
     def average_one(i, _):
@@ -603,11 +627,12 @@
     zh, ya, yb = call(
         functools.partial(z_merge_kernel, cx, cy), [on_chip] * 4, [vmem(2 * cy), vmem(n + 8), vmem(n + 8)], name="z_merge"
     )(za, zb, ya, yb)
-    ya, yb = swap(ya, NBZ, NBY, False), swap(yb, NBZ, NBY, True)
+    yb = swap(yb, NBZ, NBY, True)
+    ya = swap(ya, NBZ, NBY, False)
     y_lo, y_hi, *xs = call(
         functools.partial(y_merge_kernel, cx, cy, two_x),
         [on_chip] * (3 + copies),
-        [vmem(n + 8), vmem(n + 8)] + [vmem(NF * cy + 2 * cy + 32)] * copies,
+        [vmem(n + 8), vmem(n + 8)] + [vmem(NF * cy + 40)] * copies,
         name="y_merge",
     )(ya, yb, zh, *xs)
     xs = [swap(x, NBY * NBZ, nbx, odd) for odd, x in enumerate(xs)]
@@ -629,7 +654,7 @@
         vmem(3, 2, 8),
         vmem(NF, rows),
         vmem(rows, dtype=i32),
-        vmem(4, ring, dtype=i32),
+        vmem(cx, ring, dtype=i32),
         vmem(6 + 2 * NFIELD, ring),
         vmem(rows, dtype=i32),
         vmem(NFIELD + 1, rows),

time: 30.8 us -> 29.1 us (0.945)
  Pallas kernels: 16.1 us -> 14.5 us
    pallas_call x1, Pallas kernels: 8.86 us -> 7.45 us  [per_device(): call(functools.partial(inner_kernel, cx, cy), [on_chip] * 6, kept + [vmem...]
  transfers between devices with their start and end apart: 5 -> 5, of which waited for: 3 -> 3; matrix products, arithmetic and copies ran while one was open for 0% -> 0% of each run, Pallas kernels for 29% -> 26%
where the time goes in v4:
time: 29.1 us; the launch traced here: 29 us
  Pallas kernels  14.5 us (50%)
  starting transfers between devices  9.83 us (34%)
  waiting for transfers between devices  4.65 us (16%)
    ppermute x5, starting transfers between devices, swap(): return lax.ppermute(value, AXIS, pairing(stride, extent, devices, odd))  9.83 us
    pallas_call x1, Pallas kernels, per_device(): call(functools.partial(inner_kernel, cx, cy), [on_chip] * 6, kept + [vmem...  7.45 us
    ppermute x5, waiting for transfers between devices, swap(): return lax.ppermute(value, AXIS, pairing(stride, extent, devices, odd))  4.65 us
    pallas_call x1, Pallas kernels, per_device(): call(functools.partial(outer_kernel, cx, cy, nbx), [on_chip] * (first + l...  4.48 us
    pallas_call x1, Pallas kernels, per_device(): call(functools.partial(pack_kernel, cx, cy), [far] * 4, [vmem(2 * cy), vm...  2.24 us
  transfers between devices with their start and end apart: 5, of which 3 were waited for; matrix products, arithmetic and copies ran while one was open for 0% of the time, Pallas kernels for 26%

profile of v4, /device:TPU:0, one launch (start us, length us, event | category | flops | bytes accessed | tf_op | source)
XLA Modules:
  0.0 29.0 jit_solution(1563181529482748110)
XLA Ops:
  0.0 2.2 %pack.1 = (f32[64,128]{1,0:T(8,128)S(1)}, f32[2560,128]{1,0:T(8,128)S(1)}, f32[512,128]{1,0:T(8,128)S(1)}, f32[512,128]{1,0:T(8,128)S(1)}) custom-call(f32[2560,128]{1,0:T(8,128)} %bitcast.5, f32[512,128]{1,0:T(8,128)} %bitcast.6, s32[512,128]{1,0:T(8,128)} %bitcast.7, s32[512,128]{1,0:T(8,128)} %bitcast.8), custom_call_target="tpu_custom_call" | custom-call | tf_op jit(solution)/shard_map/pack/pallas_call | solution.py:612
  2.2 2.5 %collective-permute-start.1 = (f32[64,128]{1,0:T(8,128)S(1)}, f32[64,128]{1,0:T(8,128)S(1)}, u32[]{:S(2)}, u32[]{:S(2)}) collective-permute-start(f32[64,128]{1,0:T(8,128)S(1)} %get-tuple-element.31), channel_id=1, source_target_pairs={{0,3},{1,2},{2,1},{3,0},{4,7},{5,6},{6,5},{7,4},{8,11},{9,10},{10,... | collective-permute-start | bytes 98312 | tf_op jit(solution)/shard_map/ppermute | solution.py:608
  4.7 0.7 %collective-permute-start = (f32[64,128]{1,0:T(8,128)S(1)}, f32[64,128]{1,0:T(8,128)S(1)}, u32[]{:S(2)}, u32[]{:S(2)}) collective-permute-start(f32[64,128]{1,0:T(8,128)S(1)} %get-tuple-element.31), channel_id=1, source_target_pairs={{0,1},{1,0},{2,3},{3,2},{4,5},{5,4},{6,7},{7,6},{8,9},{9,8},{10,11... | collective-permute-start | bytes 98312 | tf_op jit(solution)/shard_map/ppermute | solution.py:608
  5.4 0.1 faces.1
  5.5 1.0 %collective-permute-done.1.r_b = f32[64,128]{1,0:T(8,128)S(1)} collective-permute-done((f32[64,128]{1,0:T(8,128)S(1)}, f32[64,128]{1,0:T(8,128)S(1)}, u32[]{:S(2)}, u32[]{:S(2)}) %collective-permute-start.1) | collective-permute-done | bytes 32800 | tf_op jit(solution)/shard_map/ppermute | solution.py:608
  6.5 0.0 collective-permute-done.r_a
  6.5 0.1 z_merge.1
  6.6 2.5 %collective-permute-start.2 = (f32[136,128]{1,0:T(8,128)S(1)}, f32[136,128]{1,0:T(8,128)S(1)}, u32[]{:S(2)}, u32[]{:S(2)}) collective-permute-start(f32[136,128]{1,0:T(8,128)S(1)} %get-tuple-element.35), channel_id=1, source_target_pairs={{0,4},{1,5},{2,6},{3,7},{4,0},{5,1},{6,2},{7,3},{8,12},{9,13},{10,... | collective-permute-start | bytes 208904 | tf_op jit(solution)/shard_map/ppermute | solution.py:608
  9.1 1.5 %collective-permute-start.3 = (f32[136,128]{1,0:T(8,128)S(1)}, f32[136,128]{1,0:T(8,128)S(1)}, u32[]{:S(2)}, u32[]{:S(2)}) collective-permute-start(f32[136,128]{1,0:T(8,128)S(1)} %get-tuple-element.36), channel_id=1, source_target_pairs={{0,12},{1,13},{2,14},{3,15},{4,8},{5,9},{6,10},{7,11},{8,4},{9,5},... | collective-permute-start | bytes 208904 | tf_op jit(solution)/shard_map/ppermute | solution.py:608
  10.6 1.8 %collective-permute-done.2.r_a = f32[136,128]{1,0:T(8,128)S(1)} collective-permute-done((f32[136,128]{1,0:T(8,128)S(1)}, f32[136,128]{1,0:T(8,128)S(1)}, u32[]{:S(2)}, u32[]{:S(2)}) %collective-permute-start.2) | collective-permute-done | bytes 69664 | tf_op jit(solution)/shard_map/ppermute | solution.py:608
  12.5 1.9 %collective-permute-done.3.r_b = f32[136,128]{1,0:T(8,128)S(1)} collective-permute-done((f32[136,128]{1,0:T(8,128)S(1)}, f32[136,128]{1,0:T(8,128)S(1)}, u32[]{:S(2)}, u32[]{:S(2)}) %collective-permute-start.3) | collective-permute-done | bytes 69664 | tf_op jit(solution)/shard_map/ppermute | solution.py:608
  14.3 0.1 y_merge.1
  14.4 2.6 %collective-permute-start.4 = (f32[296,128]{1,0:T(8,128)S(1)}, f32[296,128]{1,0:T(8,128)S(1)}, u32[]{:S(2)}, u32[]{:S(2)}) collective-permute-start(f32[296,128]{1,0:T(8,128)S(1)} %get-tuple-element.41), channel_id=1, source_target_pairs={{0,16},{1,17},{2,18},{3,19},{4,20},{5,21},{6,22},{7,23},{8,24},{9,... | collective-permute-start | bytes 454664 | tf_op jit(solution)/shard_map/ppermute | solution.py:608
  17.1 7.5 %inner.1 = (s32[20,56,128]{2,1,0:T(8,128)S(1)}, s32[40,128]{1,0:T(8,128)S(1)}, f32[6,40,128]{2,1,0:T(8,128)S(1)}, f32[6,20,56,128]{3,2,1,0:T(8,128)S(1)}, f32[6,...) custom-call(f32[2560,128]{1,0:T(8,128)S(1)} %get-tuple-element.28.u., ...), custom_call_target="tpu_custom_call" | custom-call | flops 67108864 | tf_op jit(solution)/shard_map/inner/pallas_call | solution.py:663
  24.5 0.0 collective-permute-done.4.refs_7_.refs_8_
  24.5 4.5 %outer.1 = (f32[2560,128]{1,0:T(8,128)}, s32[20,56,128]{2,1,0:T(8,128)S(1)}, s32[40,128]{1,0:T(8,128)S(1)}, f32[6,40,128]{2,1,0:T(8,128)S(1)}, f32[6,20,56,128]{...) custom-call(f32[2560,128]{1,0:T(8,128)S(1)} %get-tuple-element.28.u., ...), custom_call_target="tpu_custom_call", output_to_operand_aliasing={{1}: (9, {}), {2}: (10, {}), {3}: (11, {}), {4}: (12, {}), ... | custom-call | flops 33554432 | tf_op jit(solution)/shard_map/outer/pallas_call | solution.py:672
Async XLA Ops:
  2.2 4.3 %collective-permute-start.1 = (f32[64,128]{1,0:T(8,128)S(1)}, f32[64,128]{1,0:T(8,128)S(1)}, u32[]{:S(2)}, u32[]{:S(2)}) collective-permute-start(f32[64,128]{1,0:T(8,128)S(1)} %get-tuple-element.31), channel_id=1, source_target_pairs={{0,3},{1,2},{2,1},{3,0},{4,7},{5,6},{6,5},{7,4},{8,11},{9,10},{10,... | collective-permute-start | bytes 98312 | tf_op jit(solution)/shard_map/ppermute | solution.py:608
  4.7 1.8 %collective-permute-start = (f32[64,128]{1,0:T(8,128)S(1)}, f32[64,128]{1,0:T(8,128)S(1)}, u32[]{:S(2)}, u32[]{:S(2)}) collective-permute-start(f32[64,128]{1,0:T(8,128)S(1)} %get-tuple-element.31), channel_id=1, source_target_pairs={{0,1},{1,0},{2,3},{3,2},{4,5},{5,4},{6,7},{7,6},{8,9},{9,8},{10,11... | collective-permute-start | bytes 98312 | tf_op jit(solution)/shard_map/ppermute | solution.py:608
  6.6 5.9 %collective-permute-start.2 = (f32[136,128]{1,0:T(8,128)S(1)}, f32[136,128]{1,0:T(8,128)S(1)}, u32[]{:S(2)}, u32[]{:S(2)}) collective-permute-start(f32[136,128]{1,0:T(8,128)S(1)} %get-tuple-element.35), channel_id=1, source_target_pairs={{0,4},{1,5},{2,6},{3,7},{4,0},{5,1},{6,2},{7,3},{8,12},{9,13},{10,... | collective-permute-start | bytes 208904 | tf_op jit(solution)/shard_map/ppermute | solution.py:608
  9.1 5.2 %collective-permute-start.3 = (f32[136,128]{1,0:T(8,128)S(1)}, f32[136,128]{1,0:T(8,128)S(1)}, u32[]{:S(2)}, u32[]{:S(2)}) collective-permute-start(f32[136,128]{1,0:T(8,128)S(1)} %get-tuple-element.36), channel_id=1, source_target_pairs={{0,12},{1,13},{2,14},{3,15},{4,8},{5,9},{6,10},{7,11},{8,4},{9,5},... | collective-permute-start | bytes 208904 | tf_op jit(solution)/shard_map/ppermute | solution.py:608
  14.4 10.1 %collective-permute-start.4 = (f32[296,128]{1,0:T(8,128)S(1)}, f32[296,128]{1,0:T(8,128)S(1)}, u32[]{:S(2)}, u32[]{:S(2)}) collective-permute-start(f32[296,128]{1,0:T(8,128)S(1)} %get-tuple-element.41), channel_id=1, source_target_pairs={{0,16},{1,17},{2,18},{3,19},{4,20},{5,21},{6,22},{7,23},{8,24},{9,... | collective-permute-start | bytes 454664 | tf_op jit(solution)/shard_map/ppermute | solution.py:608

commit v5 on v4

--- a/solution.py
+++ b/solution.py
@@ -40,6 +40,8 @@
         shift %= value.shape[axis]
         if shift == 0:
             return value
+    else:
+        shift &= value.shape[axis] - 1
     return pltpu.roll(value, shift, axis)
 
 
@@ -233,10 +235,10 @@
 def y_rows(r, x):
     cx = r.cx
     for f in range(C2):
-        r.ht[f, x + 2, 0:1, :] = r.y_hi[f * cx + x : f * cx + x + 1, :]
-        r.ht[f, x + 2, 7:8, :] = r.y_lo[f * cx + x : f * cx + x + 1, :]
-    r.ht[C1, x + 2, 1:2, :] = r.y_hi[C2 * cx + x : C2 * cx + x + 1, :]
-    r.ht[C1, x + 2, 6:7, :] = r.y_lo[C2 * cx + x : C2 * cx + x + 1, :]
+        r.ht[f, x + 2, 0:1, :] = r.y_hi[pl.ds(f * cx + x, 1), :]
+        r.ht[f, x + 2, 7:8, :] = r.y_lo[pl.ds(f * cx + x, 1), :]
+    r.ht[C1, x + 2, 1:2, :] = r.y_hi[pl.ds(C2 * cx + x, 1), :]
+    r.ht[C1, x + 2, 6:7, :] = r.y_lo[pl.ds(C2 * cx + x, 1), :]
 
 
 def set_words(r, own, layer):
@@ -326,26 +328,30 @@
 
 def z_averages(r):
     word, tmp = r.ow[...], r.tmp_f
+
+    def pick(up, down, values):
+        mid, plus, minus = values
+        return mid + jnp.where((word & up) != 0, plus, jnp.where((word & down) != 0, minus, 0.0))
+
     sums = []
     for f in range(NFIELD + 1):
-        ring_store(tmp, (f,), r.zw[f] + r.zi[f])
-        mid, before, after = (ring_load(tmp, (f,), step) for step in (0, -1, 1))
-        parts = []
-        for d in (0, 1, -1):
-            m, b, a = (roll(v, -2 * d) for v in (mid, before, after))
-            parts.append(m + jnp.where((word & YU) != 0, a, jnp.where((word & YD) != 0, b, 0.0)))
-        sums.append(parts[0] + jnp.where((word & XU) != 0, parts[1], jnp.where((word & XD) != 0, parts[2], 0.0)))
+        both = r.zw[f] + r.zi[f]
+        for i, value in enumerate((both, roll(both, -2), roll(both, 2))):
+            ring_store(tmp, (3 * f + i,), value)
+        lines = [pick(YU, YD, [ring_load(tmp, (3 * f + i,), step) for step in (0, 1, -1)]) for i in range(3)]
+        sums.append(pick(XU, XD, lines))
     inverse = 1.0 / sums[0]
+    first = 3 * NFIELD + 3
     for f in range(NFIELD):
         v = jnp.where((word & r.inward) != 0, sums[f + 1] * inverse, 0.0)
-        spread = []
-        for bits in (0, YU, YD):
+        totals = []
+        for i, bits in enumerate((0, XU, XD)):
             w = jnp.where((word & bits) != 0, v, 0.0) if bits else v
-            up, down = jnp.where((word & XU) != 0, w, 0.0), jnp.where((word & XD) != 0, w, 0.0)
-            spread.append(w + roll(up, 2) + roll(down, -2))
-        ring_store(tmp, (6 + 2 * f,), spread[1])
-        ring_store(tmp, (7 + 2 * f,), spread[2])
-        r.dz[f] = spread[0] + ring_load(tmp, (6 + 2 * f,), -1) + ring_load(tmp, (7 + 2 * f,), 1)
+            slot = first + 6 * f + 2 * i
+            ring_store(tmp, (slot,), jnp.where((word & YU) != 0, w, 0.0))
+            ring_store(tmp, (slot + 1,), jnp.where((word & YD) != 0, w, 0.0))
+            totals.append(w + ring_load(tmp, (slot,), -1) + ring_load(tmp, (slot + 1,), 1))
+        r.dz[f] = totals[0] + roll(totals[1], 2) + roll(totals[2], -2)
 
 
 def average(r, layer):
@@ -380,7 +386,7 @@
 def redistribute(r, x, out):
     cx, cy = r.cx, r.cy
     layer = x + 2
-    back = 128 - 2 * layer
+    back = -2 * layer
     lane = lanes_of((8, 128))
     first_lane, last_lane = lane == 0, lane == 127
     for t in range(cy // 8):
@@ -429,14 +435,63 @@
     return own_z
 
 
-KEPT = ("cw", "inner", "zi", "h0", "hm", "hp", "rc", "av")
-SCRATCH = ("ht", "hz", "zf", "ow", "tmp_i", "tmp_f", "i1", "zw", "dz")
-
-
-def inner_kernel(cx, cy, *refs):
+KEPT = ("cw", "inner", "zi", "zf", "h0", "hm", "hp", "rc", "av")
+SCRATCH = ("ht", "hz", "ow", "tmp_i", "tmp_f", "i1", "zw", "dz")
+
+
+def plan(cx, nbx, bx):
+    if nbx == 2:
+        high = bx == 0
+
+        def at(j):
+            return jnp.where(high, j + 1, cx + 2 - j)
+
+        return types.SimpleNamespace(
+            at=at,
+            inner_weigh=[at(j) for j in range(1, cx)],
+            inner_average=(1, cx - 2),
+            inner_spread=(1, cx - 3),
+            outer_weigh=[at(cx)],
+            outer_average=[(cx - 1, 3)],
+            outer_spread=[(cx - 2, 3)],
+            inner_rows=(jnp.where(high, 0, 3), cx - 3),
+            outer_rows=[(jnp.where(high, cx - 3, 0), 3)],
+        )
+    return types.SimpleNamespace(
+        at=lambda j: j + 1,
+        inner_weigh=range(3, cx + 1),
+        inner_average=(3, cx - 4),
+        inner_spread=(4, cx - 6),
+        outer_weigh=[2, cx + 1],
+        outer_average=[(0, 3), (cx - 1, 3)],
+        outer_spread=[(1, 3), (cx - 2, 3)],
+        inner_rows=(3, cx - 6),
+        outer_rows=[(0, 3), (cx - 3, 3)],
+    )
+
+
+def x_lanes(r, high):
+    below = (r.lane == 127) | (r.lane <= 2)
+    above = (r.lane >= 2 * r.cx + 3) & (r.lane <= 2 * r.cx + 6)
+    if isinstance(high, bool):
+        return above if high else below
+    return (above & high) | (below & jnp.logical_not(high))
+
+
+def each(span, step):
+    def body(j, _):
+        step(j)
+        return 0
+
+    lax.fori_loop(span[0], span[0] + span[1], body, 0)
+
+
+def inner_kernel(cx, cy, nbx, *refs):
     names = ("u", "vf", "c", "zh", "y_lo", "y_hi", *KEPT, "res", *SCRATCH)
     r = types.SimpleNamespace(cx=cx, cy=cy, **dict(zip(names, refs)))
     own_z = common(r)
+    bx, by, bz = place()
+    todo = plan(cx, nbx, bx)
     r.ht[...] = jnp.zeros(r.ht.shape, jnp.float32)
     for x in range(cx):
         y_rows(r, x)
@@ -447,25 +502,24 @@
 
     inner = lax.fori_loop(0, cx, words, jnp.ones((r.rows, 128), jnp.int32), unroll=4)
     r.inner[...] = inner
+    outside = x_lanes(r, bx > 0) if nbx == 2 else None
     for f in range(NF):
-        r.zf[f] = z_halo(r, f, own_z)
+        value = z_halo(r, f, own_z)
+        if nbx == 2:
+            value = jnp.where(outside, EDGE if f >= C1 else 0.0, value)
+        r.zf[f] = value
+    if nbx == 2:
+        edge = todo.at(0)
+        ring_store(r.cw, (edge,), jnp.ones((r.rows, 128), jnp.int32))
+        for f in range(NFIELD + 1):
+            for h in (r.h0, r.hm, r.hp):
+                ring_store(h, (f, edge), jnp.zeros((r.rows, 128), jnp.float32))
     z_counts(r, inner)
     r.zi[...] = jnp.zeros(r.zi.shape, jnp.float32)
-
-    weigh(r, [(x + 2, functools.partial(own_field, r, x)) for x in range(1, cx - 1)])
+    weigh(r, [(layer, functools.partial(own_field, r, layer - 2)) for layer in todo.inner_weigh])
     z_averages(r)
-
-    def average_one(layer, _):
-        average(r, layer)
-        return 0
-
-    lax.fori_loop(4, cx, average_one, 0)
-
-    def spread_one(x, _):
-        redistribute(r, x, r.res)
-        return 0
-
-    lax.fori_loop(3, cx - 3, spread_one, 0)
+    each(todo.inner_average, lambda j: average(r, todo.at(j)))
+    each(todo.inner_spread, lambda j: redistribute(r, todo.at(j) - 2, r.res))
 
 
 def outer_kernel(cx, cy, nbx, *refs):
@@ -476,41 +530,56 @@
     r = types.SimpleNamespace(cx=cx, cy=cy, **dict(zip(names, ins)))
     r.__dict__.update(zip(("out", *KEPT, *SCRATCH, "rim", "sems"), rest))
     size = cx * cy
-
-    def send(src, first, last, base):
+    bx, by, bz = place()
+    todo = plan(cx, nbx, bx)
+
+    def send(src, rows, base):
         copies = []
         for f in range(NFIELD):
-            rows = pl.ds(f * size + first * cy, (last - first) * cy)
-            copies.append(pltpu.make_async_copy(src.at[rows, :], r.out.at[rows, :], r.sems.at[base + f]))
+            part = pl.ds(pl.multiple_of(f * size + rows[0] * cy, 8), rows[1] * cy)
+            copies.append(pltpu.make_async_copy(src.at[part, :], r.out.at[part, :], r.sems.at[base + f]))
         for copy in copies:
             copy.start()
         return copies
 
-    copies = send(r.res, 3, cx - 3, 0)
-    own_z = common(r)
-    bx, by, bz = place()
+    copies = send(r.res, todo.inner_rows, 0)
+    common(r)
     x_odd = bx % 2 == 1
-    has_lo, has_hi = bx > 0, bx < nbx - 1
-
-    def x_part(side, first, count):
-        a, b = r.xa[first : first + count, :], r.xb[first : first + count, :]
-        return jnp.where(x_odd, a, b) if side == 0 else jnp.where(x_odd, b, a)
-
-    def x_raw(f, side):
-        edge = EDGE if f >= C1 else 0.0
-        return jnp.where(has_hi if side else has_lo, x_part(side, f * cy, cy), edge)
+
+    if nbx == 2:
+        sides = [(bx == 0, True, lambda first, count: r.xa[first : first + count, :])]
+    else:
+
+        def message(high):
+            def rows(first, count):
+                a, b = r.xa[first : first + count, :], r.xb[first : first + count, :]
+                return jnp.where(x_odd, b, a) if high else jnp.where(x_odd, a, b)
+
+            return rows
+
+        sides = [(False, bx > 0, message(False)), (True, bx < nbx - 1, message(True))]
+
+    def choose(high, a, b):
+        return (a if high else b) if isinstance(high, bool) else jnp.where(high, a, b)
+
+    def present_or(present, value, edge):
+        return value if present is True else jnp.where(present, value, edge)
 
     zrow = NF * cy
     edges = zrow + 8
-    for x in (0, cx - 1):
-        y_rows(r, x)
-    for side, layer, second in ((0, 1, 0), (1, cx + 2, cx + 3)):
-        present = has_hi if side else has_lo
+    halo = []
+    for high, present, part in sides:
+        layer, second, own = (choose(high, a, b) for a, b in ((cx + 2, 1), (cx + 3, 0), (cx - 1, 0)))
+        y_rows(r, own)
+
+        def raw(f, present=present, part=part):
+            return present_or(present, part(f * cy, cy), EDGE if f >= C1 else 0.0)
+
         for y, row1, row2 in ((0, 7, 6), (1, 0, 1)):
             base = edges + 8 + 10 * y
 
-            def rim(i, edge, base=base, side=side, present=present):
-                return jnp.where(present, x_part(side, base + i, 1), edge)
+            def rim(i, edge, base=base, present=present, part=part):
+                return present_or(present, part(base + i, 1), edge)
 
             for f in range(C1):
                 r.ht[f, layer, row1 : row1 + 1, :] = rim(f, 0.0)
@@ -518,60 +587,35 @@
             r.ht[C1, layer, row2 : row2 + 1, :] = rim(C2, EDGE)
             r.ht[C1, second, row1 : row1 + 1, :] = rim(NF, EDGE)
             r.ht[C1, second, row2 : row2 + 1, :] = rim(NF + 1, EDGE)
-    set_words(r, x_raw(C2, 0), 0)
-    set_words(r, x_raw(C1, 0), 1)
-    set_words(r, x_raw(C1, 1), cx + 2)
-    set_words(r, x_raw(C2, 1), cx + 3)
-
-    for side in (0, 1):
+        set_words(r, raw(C1), layer)
+        set_words(r, raw(C2), second)
+        halo.append((layer, lambda f, raw=raw, layer=layer: jnp.concatenate([raw(f), r.ht[f, layer]], axis=0)))
+
         for g in range(2):
             for i, row in enumerate((0, 1)):
                 lo, hi = edges + 2 * g + i, edges + 4 + 2 * g + i
-                r.hz[1 + side, g, row : row + 1, :] = x_part(side, hi, 1)
-                r.hz[1 + side, g, 7 - row : 8 - row, :] = x_part(side, lo, 1)
-
-    def x_z(side, f):
-        g, k = f // 4, f % 4
-        shift = 4 - 2 * cx * k + (2 * cx if side else -2 * cx)
-        tile = x_part(side, zrow, 8)
-        tiles = [roll(tile, shift - 8 * t - 4 * g) for t in range(cy // 8)]
-        return jnp.concatenate([*tiles, roll(r.hz[1 + side, g], shift)], axis=0)
-
-    below = (r.lane == 127) | (r.lane <= 2)
-    above = (r.lane >= 2 * cx + 3) & (r.lane <= 2 * cx + 6)
-    for f in range(NF):
-        edge = EDGE if f >= C1 else 0.0
-        lo, hi = jnp.where(has_lo, x_z(0, f), edge), jnp.where(has_hi, x_z(1, f), edge)
-        r.zf[f] = jnp.where(below, lo, jnp.where(above, hi, z_halo(r, f, own_z)))
+                r.hz[1, g, row : row + 1, :] = part(hi, 1)
+                r.hz[1, g, 7 - row : 8 - row, :] = part(lo, 1)
+        lanes = x_lanes(r, high)
+        for f in range(NF):
+            g, k = f // 4, f % 4
+            shift = 4 - 2 * cx * k + choose(high, 2 * cx, -2 * cx)
+            tile = part(zrow, 8)
+            tiles = [roll(tile, shift - 8 * t - 4 * g) for t in range(cy // 8)]
+            value = jnp.concatenate([*tiles, roll(r.hz[1, g], shift)], axis=0)
+            r.zf[f] = jnp.where(lanes, present_or(present, value, EDGE if f >= C1 else 0.0), r.zf[f])
     inner = r.inner[...]
-    for layer in (0, 1, cx + 2, cx + 3):
-        inner = collect(r, layer, inner)
+    for high, _, _ in sides:
+        for a, b in ((cx + 2, 1), (cx + 3, 0)):
+            inner = collect(r, choose(high, a, b), inner)
     z_counts(r, inner)
-    weigh(
-        r,
-        [
-            (1, lambda f: jnp.concatenate([x_raw(f, 0), r.ht[f, 1]], axis=0)),
-            (2, functools.partial(own_field, r, 0)),
-            (cx + 1, functools.partial(own_field, r, cx - 1)),
-            (cx + 2, lambda f: jnp.concatenate([x_raw(f, 1), r.ht[f, cx + 2]], axis=0)),
-        ],
-    )
+    weigh(r, [(layer, functools.partial(own_field, r, layer - 2)) for layer in todo.outer_weigh] + halo)
     z_averages(r)
-
-    def average_one(i, _):
-        average(r, 1 + i + jnp.where(i >= 3, cx - 4, 0))
-        return 0
-
-    lax.fori_loop(0, 6, average_one, 0)
-
-    def spread_one(x, _):
-        redistribute(r, x, r.rim)
-        return 0
-
-    lax.fori_loop(0, 3, spread_one, 0)
-    copies += send(r.rim, 0, 3, NFIELD)
-    lax.fori_loop(cx - 3, cx, spread_one, 0)
-    copies += send(r.rim, cx - 3, cx, 2 * NFIELD)
+    for span in todo.outer_average:
+        each(span, lambda j: average(r, todo.at(j)))
+    for i, (span, rows) in enumerate(zip(todo.outer_spread, todo.outer_rows)):
+        each(span, lambda j: redistribute(r, todo.at(j) - 2, r.rim))
+        copies += send(r.rim, rows, (1 + i) * NFIELD)
     for copy in copies:
         copy.wait()
 
@@ -643,6 +687,7 @@
         vmem(layers, ring, dtype=i32),
         vmem(rows, dtype=i32),
         vmem(NFIELD + 1, rows),
+        vmem(NF, rows),
         vmem(NFIELD + 1, layers, ring),
         vmem(NFIELD + 1, layers, ring),
         vmem(NFIELD + 1, layers, ring),
@@ -651,17 +696,16 @@
     ]
     scratch = [
         vmem(C2, layers, 8),
-        vmem(3, 2, 8),
-        vmem(NF, rows),
+        vmem(2, 2, 8),
         vmem(rows, dtype=i32),
         vmem(cx, ring, dtype=i32),
-        vmem(6 + 2 * NFIELD, ring),
+        vmem(9 * NFIELD + 3, ring),
         vmem(rows, dtype=i32),
         vmem(NFIELD + 1, rows),
         vmem(NFIELD, rows),
     ]
     *state, res = call(
-        functools.partial(inner_kernel, cx, cy),
+        functools.partial(inner_kernel, cx, cy, nbx),
         [on_chip] * 6,
         kept + [vmem(NFIELD * cells)],
         scratch,

time: 29.1 us -> 28.6 us (0.983)
  Pallas kernels: 14.5 us -> 13.9 us
    pallas_call x1, Pallas kernels: 4.48 us -> 2.85 us  [per_device(): call(functools.partial(outer_kernel, cx, cy, nbx), [on_chip] * (first + l...]
    pallas_call x1, Pallas kernels: 7.45 us -> 8.54 us  [per_device(): call(functools.partial(inner_kernel, cx, cy, nbx), [on_chip] * 6, kept +...]
  transfers between devices with their start and end apart: 5 -> 5, of which waited for: 3 -> 3; matrix products, arithmetic and copies ran while one was open for 0% -> 0% of each run, Pallas kernels for 26% -> 30%
where the time goes in v5:
time: 28.6 us; the launch traced here: 28.5 us
  Pallas kernels  13.9 us (49%)
  starting transfers between devices  9.83 us (34%)
  waiting for transfers between devices  4.65 us (16%)
    ppermute x5, starting transfers between devices, swap(): return lax.ppermute(value, AXIS, pairing(stride, extent, devices, odd))  9.83 us
    pallas_call x1, Pallas kernels, per_device(): call(functools.partial(inner_kernel, cx, cy, nbx), [on_chip] * 6, kept +...  8.54 us
    ppermute x5, waiting for transfers between devices, swap(): return lax.ppermute(value, AXIS, pairing(stride, extent, devices, odd))  4.65 us
    pallas_call x1, Pallas kernels, per_device(): call(functools.partial(outer_kernel, cx, cy, nbx), [on_chip] * (first + l...  2.85 us
    pallas_call x1, Pallas kernels, per_device(): call(functools.partial(pack_kernel, cx, cy), [far] * 4, [vmem(2 * cy), vm...  2.24 us
  transfers between devices with their start and end apart: 5, of which 3 were waited for; matrix products, arithmetic and copies ran while one was open for 0% of the time, Pallas kernels for 30%

profile of v5, /device:TPU:0, one launch (start us, length us, event | category | flops | bytes accessed | tf_op | source)
XLA Modules:
  0.0 28.5 jit_solution(9645256446503547633)
XLA Ops:
  0.0 2.2 %pack.1 = (f32[64,128]{1,0:T(8,128)S(1)}, f32[2560,128]{1,0:T(8,128)S(1)}, f32[512,128]{1,0:T(8,128)S(1)}, f32[512,128]{1,0:T(8,128)S(1)}) custom-call(f32[2560,128]{1,0:T(8,128)} %bitcast.5, f32[512,128]{1,0:T(8,128)} %bitcast.6, s32[512,128]{1,0:T(8,128)} %bitcast.7, s32[512,128]{1,0:T(8,128)} %bitcast.8), custom_call_target="tpu_custom_call" | custom-call | tf_op jit(solution)/shard_map/pack/pallas_call | solution.py:656
  2.2 2.5 %collective-permute-start.1 = (f32[64,128]{1,0:T(8,128)S(1)}, f32[64,128]{1,0:T(8,128)S(1)}, u32[]{:S(2)}, u32[]{:S(2)}) collective-permute-start(f32[64,128]{1,0:T(8,128)S(1)} %get-tuple-element.32), channel_id=1, source_target_pairs={{0,3},{1,2},{2,1},{3,0},{4,7},{5,6},{6,5},{7,4},{8,11},{9,10},{10,... | collective-permute-start | bytes 98312 | tf_op jit(solution)/shard_map/ppermute | solution.py:652
  4.7 0.7 %collective-permute-start = (f32[64,128]{1,0:T(8,128)S(1)}, f32[64,128]{1,0:T(8,128)S(1)}, u32[]{:S(2)}, u32[]{:S(2)}) collective-permute-start(f32[64,128]{1,0:T(8,128)S(1)} %get-tuple-element.32), channel_id=1, source_target_pairs={{0,1},{1,0},{2,3},{3,2},{4,5},{5,4},{6,7},{7,6},{8,9},{9,8},{10,11... | collective-permute-start | bytes 98312 | tf_op jit(solution)/shard_map/ppermute | solution.py:652
  5.4 0.1 faces.1
  5.5 1.0 %collective-permute-done.1.r_b = f32[64,128]{1,0:T(8,128)S(1)} collective-permute-done((f32[64,128]{1,0:T(8,128)S(1)}, f32[64,128]{1,0:T(8,128)S(1)}, u32[]{:S(2)}, u32[]{:S(2)}) %collective-permute-start.1) | collective-permute-done | bytes 32800 | tf_op jit(solution)/shard_map/ppermute | solution.py:652
  6.5 0.0 collective-permute-done.r_a
  6.5 0.1 z_merge.1
  6.6 2.5 %collective-permute-start.2 = (f32[136,128]{1,0:T(8,128)S(1)}, f32[136,128]{1,0:T(8,128)S(1)}, u32[]{:S(2)}, u32[]{:S(2)}) collective-permute-start(f32[136,128]{1,0:T(8,128)S(1)} %get-tuple-element.36), channel_id=1, source_target_pairs={{0,4},{1,5},{2,6},{3,7},{4,0},{5,1},{6,2},{7,3},{8,12},{9,13},{10,... | collective-permute-start | bytes 208904 | tf_op jit(solution)/shard_map/ppermute | solution.py:652
  9.1 1.5 %collective-permute-start.3 = (f32[136,128]{1,0:T(8,128)S(1)}, f32[136,128]{1,0:T(8,128)S(1)}, u32[]{:S(2)}, u32[]{:S(2)}) collective-permute-start(f32[136,128]{1,0:T(8,128)S(1)} %get-tuple-element.37), channel_id=1, source_target_pairs={{0,12},{1,13},{2,14},{3,15},{4,8},{5,9},{6,10},{7,11},{8,4},{9,5},... | collective-permute-start | bytes 208904 | tf_op jit(solution)/shard_map/ppermute | solution.py:652
  10.6 1.8 %collective-permute-done.2.r_a = f32[136,128]{1,0:T(8,128)S(1)} collective-permute-done((f32[136,128]{1,0:T(8,128)S(1)}, f32[136,128]{1,0:T(8,128)S(1)}, u32[]{:S(2)}, u32[]{:S(2)}) %collective-permute-start.2) | collective-permute-done | bytes 69664 | tf_op jit(solution)/shard_map/ppermute | solution.py:652
  12.5 1.9 %collective-permute-done.3.r_b = f32[136,128]{1,0:T(8,128)S(1)} collective-permute-done((f32[136,128]{1,0:T(8,128)S(1)}, f32[136,128]{1,0:T(8,128)S(1)}, u32[]{:S(2)}, u32[]{:S(2)}) %collective-permute-start.3) | collective-permute-done | bytes 69664 | tf_op jit(solution)/shard_map/ppermute | solution.py:652
  14.3 0.1 y_merge.1
  14.4 2.6 %collective-permute-start.4 = (f32[296,128]{1,0:T(8,128)S(1)}, f32[296,128]{1,0:T(8,128)S(1)}, u32[]{:S(2)}, u32[]{:S(2)}) collective-permute-start(f32[296,128]{1,0:T(8,128)S(1)} %get-tuple-element.42), channel_id=1, source_target_pairs={{0,16},{1,17},{2,18},{3,19},{4,20},{5,21},{6,22},{7,23},{8,24},{9,... | collective-permute-start | bytes 454664 | tf_op jit(solution)/shard_map/ppermute | solution.py:652
  17.1 8.5 %inner.1 = (s32[20,56,128]{2,1,0:T(8,128)S(1)}, s32[40,128]{1,0:T(8,128)S(1)}, f32[6,40,128]{2,1,0:T(8,128)S(1)}, f32[8,40,128]{2,1,0:T(8,128)S(1)}, f32[6,20,56...) custom-call(f32[2560,128]{1,0:T(8,128)S(1)} %get-tuple-element.29.u., ...), custom_call_target="tpu_custom_call" | custom-call | flops 67108864 | tf_op jit(solution)/shard_map/inner/pallas_call | solution.py:707
  25.6 0.0 collective-permute-done.4.refs_7_.refs_8_
  25.6 2.8 %outer.1 = (f32[2560,128]{1,0:T(8,128)}, s32[20,56,128]{2,1,0:T(8,128)S(1)}, s32[40,128]{1,0:T(8,128)S(1)}, f32[6,40,128]{2,1,0:T(8,128)S(1)}, f32[8,40,128]{2,1...) custom-call(f32[2560,128]{1,0:T(8,128)S(1)} %get-tuple-element.29.u., ...), custom_call_target="tpu_custom_call", output_to_operand_aliasing={{1}: (9, {}), {2}: (10, {}), {3}: (11, {}), {4}: (12, {}), ... | custom-call | flops 33554432 | tf_op jit(solution)/shard_map/outer/pallas_call | solution.py:716
Async XLA Ops:
  2.2 4.3 %collective-permute-start.1 = (f32[64,128]{1,0:T(8,128)S(1)}, f32[64,128]{1,0:T(8,128)S(1)}, u32[]{:S(2)}, u32[]{:S(2)}) collective-permute-start(f32[64,128]{1,0:T(8,128)S(1)} %get-tuple-element.32), channel_id=1, source_target_pairs={{0,3},{1,2},{2,1},{3,0},{4,7},{5,6},{6,5},{7,4},{8,11},{9,10},{10,... | collective-permute-start | bytes 98312 | tf_op jit(solution)/shard_map/ppermute | solution.py:652
  4.7 1.8 %collective-permute-start = (f32[64,128]{1,0:T(8,128)S(1)}, f32[64,128]{1,0:T(8,128)S(1)}, u32[]{:S(2)}, u32[]{:S(2)}) collective-permute-start(f32[64,128]{1,0:T(8,128)S(1)} %get-tuple-element.32), channel_id=1, source_target_pairs={{0,1},{1,0},{2,3},{3,2},{4,5},{5,4},{6,7},{7,6},{8,9},{9,8},{10,11... | collective-permute-start | bytes 98312 | tf_op jit(solution)/shard_map/ppermute | solution.py:652
  6.6 5.9 %collective-permute-start.2 = (f32[136,128]{1,0:T(8,128)S(1)}, f32[136,128]{1,0:T(8,128)S(1)}, u32[]{:S(2)}, u32[]{:S(2)}) collective-permute-start(f32[136,128]{1,0:T(8,128)S(1)} %get-tuple-element.36), channel_id=1, source_target_pairs={{0,4},{1,5},{2,6},{3,7},{4,0},{5,1},{6,2},{7,3},{8,12},{9,13},{10,... | collective-permute-start | bytes 208904 | tf_op jit(solution)/shard_map/ppermute | solution.py:652
  9.1 5.2 %collective-permute-start.3 = (f32[136,128]{1,0:T(8,128)S(1)}, f32[136,128]{1,0:T(8,128)S(1)}, u32[]{:S(2)}, u32[]{:S(2)}) collective-permute-start(f32[136,128]{1,0:T(8,128)S(1)} %get-tuple-element.37), channel_id=1, source_target_pairs={{0,12},{1,13},{2,14},{3,15},{4,8},{5,9},{6,10},{7,11},{8,4},{9,5},... | collective-permute-start | bytes 208904 | tf_op jit(solution)/shard_map/ppermute | solution.py:652
  14.4 11.2 %collective-permute-start.4 = (f32[296,128]{1,0:T(8,128)S(1)}, f32[296,128]{1,0:T(8,128)S(1)}, u32[]{:S(2)}, u32[]{:S(2)}) collective-permute-start(f32[296,128]{1,0:T(8,128)S(1)} %get-tuple-element.42), channel_id=1, source_target_pairs={{0,16},{1,17},{2,18},{3,19},{4,20},{5,21},{6,22},{7,23},{8,24},{9,... | collective-permute-start | bytes 454664 | tf_op jit(solution)/shard_map/ppermute | solution.py:652

commit v6 on v5

--- a/solution.py
+++ b/solution.py
@@ -48,6 +48,34 @@
 def place():
     me = lax.axis_index(AXIS)
     return me // (NBY * NBZ), me // NBZ % NBY, me % NBZ
+
+
+def decode(code):
+    qx = (code * 57) >> 9
+    rest = code - 9 * qx
+    qy = (rest * 11) >> 5
+    qz = rest - 3 * qy
+    word = 1 + jnp.where(qz == 2, ZU, 0) + jnp.where(qz == 0, ZD, 0)
+    word = word * jnp.where(qy == 2, 1 + YU, jnp.where(qy == 0, 1 + YD, 1))
+    return word | jnp.where(qx == 2, XU, jnp.where(qx == 0, XD, 0))
+
+
+def on(word, bits):
+    return (word & bits) == bits
+
+
+def ring_store(ref, lead, value):
+    n = value.shape[0]
+    ref[(*lead, slice(8, 8 + n), slice(None))] = value
+    ref[(*lead, slice(0, 8), slice(None))] = value[n - 8 :]
+
+
+def ring_load(ref, lead, step):
+    n = ref.shape[-2] - 16
+    if step <= 0:
+        return ref[(*lead, slice(8 + step, 8 + step + n), slice(None))]
+    own = ref[(*lead, slice(8 + step, n + step), slice(None))]
+    return jnp.concatenate([own, ref[(*lead, slice(step, 8 + step), slice(None))]], axis=0)
 
 
 def pack_kernel(cx, cy, u_in, vf_in, mask_in, code_in, zp, u, vf, c, mask, code, sems):
@@ -88,8 +116,10 @@
         zp[g * cy : (g + 1) * cy, :] = acc
 
 
-def faces_kernel(cx, cy, two_x, u, vf, c, y_a, y_b, *xs):
+def faces_kernel(cx, cy, two_x, u, vf, c, cw, y_a, y_b, *xs):
     bx, by, bz = place()
+    for x in range(cx):
+        cw[x + 2, 8 : 8 + cy, :] = decode(c[x * cy : (x + 1) * cy, :].astype(jnp.int32))
 
     def y_face(out, high):
         rim = jnp.where(high, cy - 1, 0)
@@ -125,7 +155,7 @@
         x_face(xs[1], bx % 2 == 1)
 
 
-def z_merge_kernel(cx, cy, r_a, r_b, ya_in, yb_in, zh, y_a, y_b):
+def z_merge_kernel(cx, cy, r_a, r_b, zp, ya_in, yb_in, zh, y_a, y_b):
     bx, by, bz = place()
     odd = bz % 2 == 1
     lane = lanes_of((cy, 128))
@@ -138,16 +168,16 @@
         low = jnp.where(bz > 0, roll(jnp.where(odd, a, b), 1), edge)
         high = jnp.where(bz < NBZ - 1, roll(jnp.where(odd, b, a), -1), edge)
         zh[rows, :] = jnp.where(low_lane, low, high)
+    zh[2 * cy :, :] = zp[...]
     n = NF * cx
 
     def finish(out, main, high):
         out[:n, :] = main[...]
         rim = jnp.where(high, cy - 1, 0)
         second = jnp.where(high, cy - 2, 1)
-        for g in range(2):
+        for g in range(4):
             out[n + 2 * g : n + 2 * g + 1, :] = zh[pl.ds(g * cy + rim, 1), :]
             out[n + 2 * g + 1 : n + 2 * g + 2, :] = zh[pl.ds(g * cy + second, 1), :]
-        out[n + 4 : n + 8, :] = jnp.zeros((4, 128), jnp.float32)
 
     finish(y_a, ya_in, by % 2 == 0)
     finish(y_b, yb_in, by % 2 == 1)
@@ -157,7 +187,7 @@
     n = NF * cx
     row = lax.broadcasted_iota(jnp.int32, (n + 8, 128), 0)
     lane = lanes_of((n + 8, 128))
-    codes = ((row >= C1 * cx) & (row < n)) | ((row >= n + 2) & (lane >= 63) & (lane <= 126))
+    codes = ((row >= C1 * cx) & (row < n)) | ((row >= n) & ((row & 2) != 0) & (lane >= 63) & (lane <= 126))
     return jnp.where(codes, EDGE, 0.0)
 
 
@@ -179,17 +209,17 @@
         out[:at, :] = main[...]
         lane = lanes_of((8, 128))
         spot = (lane - jnp.where(high, 2 * cx - 5, 2 * cx - 1)) & (2 * cx - 1)
-        tile = jnp.zeros((8, 128), jnp.float32)
-        for t in range(cy // 8):
-            for g in range(2):
-                start = 8 * t + 4 * g
-                part = roll(zh[g * cy + 8 * t : g * cy + 8 * t + 8, :], start)
-                tile = jnp.where((spot >= start) & (spot < start + 4), part, tile)
-        out[at : at + 8, :] = tile
-        at += 8
+        for half in range(2):
+            tile = jnp.zeros((8, 128), jnp.float32)
+            for t in range(cy // 8):
+                for g in range(2):
+                    start, row = 8 * t + 4 * g, (2 * half + g) * cy + 8 * t
+                    tile = jnp.where((spot >= start) & (spot < start + 4), roll(zh[row : row + 8, :], start), tile)
+            out[at : at + 8, :] = tile
+            at += 8
         for y in (y_lo, y_hi):
-            out[at : at + 4, :] = y[n : n + 4, :]
-            at += 4
+            out[at : at + 8, :] = y[n : n + 8, :]
+            at += 8
         for y in (y_lo, y_hi):
             for f in range(NF):
                 out[at : at + 1, :] = y[pl.ds(f * cx + rim, 1), :]
@@ -204,34 +234,6 @@
         x_rim(xs[1], mains[1], bx % 2 == 1)
 
 
-def decode(code):
-    qx = (code * 57) >> 9
-    rest = code - 9 * qx
-    qy = (rest * 11) >> 5
-    qz = rest - 3 * qy
-    word = 1 + jnp.where(qz == 2, ZU, 0) + jnp.where(qz == 0, ZD, 0)
-    word = word * jnp.where(qy == 2, 1 + YU, jnp.where(qy == 0, 1 + YD, 1))
-    return word | jnp.where(qx == 2, XU, jnp.where(qx == 0, XD, 0))
-
-
-def on(word, bits):
-    return (word & bits) == bits
-
-
-def ring_store(ref, lead, value):
-    n = value.shape[0]
-    ref[(*lead, slice(8, 8 + n), slice(None))] = value
-    ref[(*lead, slice(0, 8), slice(None))] = value[n - 8 :]
-
-
-def ring_load(ref, lead, step):
-    n = ref.shape[-2] - 16
-    if step <= 0:
-        return ref[(*lead, slice(8 + step, 8 + step + n), slice(None))]
-    own = ref[(*lead, slice(8 + step, n + step), slice(None))]
-    return jnp.concatenate([own, ref[(*lead, slice(step, 8 + step), slice(None))]], axis=0)
-
-
 def y_rows(r, x):
     cx = r.cx
     for f in range(C2):
@@ -246,12 +248,10 @@
     ring_store(r.cw, (layer,), decode(both.astype(jnp.int32)))
 
 
-def z_pair(r, layer):
-    return (r.lane == 2 * layer) | (r.lane == 2 * layer - 1) | ((r.lane == 127) & (layer == 0))
-
-
-def collect(r, layer, acc):
-    return jnp.where(z_pair(r, layer), roll(r.cw[layer, 8 : 8 + r.rows, :], 2 * layer), acc)
+def set_halo_words(r, layer):
+    words = decode(r.ht[C1, layer].astype(jnp.int32))
+    r.cw[layer, 0:8, :] = words
+    r.cw[layer, 8 + r.cy : 16 + r.cy, :] = words
 
 
 def z_halo(r, f, own):
@@ -259,7 +259,7 @@
     return roll(own(g), 4 - 2 * r.cx * k)
 
 
-def spread_counts(r, planes):
+def spread_counts(r, planes, slot):
     mid = up = down = jnp.zeros((r.rows, 128), jnp.int32)
     for word, bits in planes:
         v = 1 + ((word & YU) << 6) + ((word & YD) << 4)
@@ -269,53 +269,50 @@
         up = up + jnp.where((word & XU) != 0, v, 0)
         down = down + jnp.where((word & XD) != 0, v, 0)
     total = mid + roll(up, 2) + roll(down, -2)
-    ring_store(r.tmp_i, (0,), total)
-    before, after = ring_load(r.tmp_i, (0,), -1), ring_load(r.tmp_i, (0,), 1)
+    ring_store(r.tmp_i, (slot,), total)
+    before, after = ring_load(r.tmp_i, (slot,), -1), ring_load(r.tmp_i, (slot,), 1)
     return (total & 255) + ((before >> 8) & 255) + ((after >> 16) & 255)
 
 
-def z_counts(r, inner):
-    outer1, outer2 = (decode(r.zf[f].astype(jnp.int32)) for f in (C1, C2))
-    r.ow[...] = outer1
-    z_count = spread_counts(r, ((outer1, None), (outer2, r.inward), (inner, r.outward)))
-    r.i1[...] = spread_counts(r, ((outer1, r.inward),))
-    z_weight = r.zf[VF] / z_count.astype(jnp.float32)
-    r.zw[0] = z_weight
-    for f in range(NFIELD):
-        r.zw[f + 1] = z_weight * r.zf[f]
+def z_counts(r):
+    outer1, outer2, inner1, inner2 = (decode(r.zf[f].astype(jnp.int32)) for f in (C1, C2, NF + C1, NF + C2))
+    r.ow[...], r.iw[...] = outer1, inner1
+    planes = ((outer1, None), (outer2, r.inward), (inner1, r.outward)), ((inner1, None), (outer1, r.inward), (inner2, r.outward))
+    for first, out, plane in zip((0, NF), (r.zw, r.zi), planes):
+        inverse = 1.0 / spread_counts(r, plane, first // NF).astype(jnp.float32)
+        weight = r.zf[first + VF] * inverse
+        out[0] = weight
+        for f in range(NFIELD):
+            out[f + 1] = weight * r.zf[first + f]
+    r.ci[...] = inverse
 
 
 def weigh(r, group):
     rows = r.rows
-    first_lane, last_lane = r.lane == 0, r.lane == 127
+    edge_lane = (r.lane == 0) | (r.lane == 127)
     totals = []
-    for slot, (layer, _) in enumerate(group):
+    for slot, (layer, _) in enumerate(group, 2):
         mid, left, right = (r.cw[layer + d, 8 : 8 + rows, :] for d in (0, -1, 1))
         total = (mid & LOW) + jnp.where((left & XU) != 0, left & LOW, 0)
         ring_store(r.tmp_i, (slot,), total + jnp.where((right & XD) != 0, right & LOW, 0))
-    for slot, (layer, _) in enumerate(group):
+    for slot, (layer, _) in enumerate(group, 2):
         total, before, after = (ring_load(r.tmp_i, (slot,), step) for step in (0, -1, 1))
         total = (total & 0x333) + ((before >> 2) & 0x333) + ((after >> 12) & 0x333)
-        totals.append((total, roll(total, 1), roll(total, -1), roll(r.i1[...], -2 * layer)))
-    for slot, (layer, field) in enumerate(group):
-        total, below, above, extra = totals[slot]
-        count = (total & 15) + jnp.where(first_lane, extra, (below >> 4) & 15)
-        count = count + jnp.where(last_lane, extra, (above >> 8) & 15)
-        inverse = 1.0 / count.astype(jnp.float32)
+        totals.append((total, roll(total, 1), roll(total, -1), roll(r.ci[...], -2 * layer)))
+    for (layer, field), (total, below, above, edge) in zip(group, totals):
+        count = (total & 15) + ((below >> 4) & 15) + ((above >> 8) & 15)
+        inverse = jnp.where(edge_lane, edge, 1.0 / count.astype(jnp.float32))
         r.rc[layer] = inverse[: r.cy]
         ring_store(r.h0, (0, layer), field(VF) * inverse)
-    for slot, (layer, field) in enumerate(group):
+    for layer, field in group:
         weight = ring_load(r.h0, (0, layer), 0)
-        pair = z_pair(r, layer)
         for f in range(NFIELD + 1):
             w = weight
             if f:
                 w = weight * field(f - 1)
                 ring_store(r.h0, (f, layer), w)
-            halo = roll(r.zw[f], -2 * layer)
-            ring_store(r.hm, (f, layer), w + jnp.where(first_lane, halo, roll(w, 1)))
-            ring_store(r.hp, (f, layer), w + jnp.where(last_lane, halo, roll(w, -1)))
-            r.zi[f] = jnp.where(pair, roll(w, 2 * layer), r.zi[f])
+            ring_store(r.hm, (f, layer), w + roll(w, 1))
+            ring_store(r.hp, (f, layer), w + roll(w, -1))
 
 
 def own_field(r, x, f):
@@ -327,19 +324,24 @@
 
 
 def z_averages(r):
-    word, tmp = r.ow[...], r.tmp_f
-
-    def pick(up, down, values):
+    tmp = r.tmp_f
+
+    def pick(word, up, down, values):
         mid, plus, minus = values
         return mid + jnp.where((word & up) != 0, plus, jnp.where((word & down) != 0, minus, 0.0))
 
-    sums = []
+    sums, inner_sums = [], []
     for f in range(NFIELD + 1):
         both = r.zw[f] + r.zi[f]
         for i, value in enumerate((both, roll(both, -2), roll(both, 2))):
             ring_store(tmp, (3 * f + i,), value)
-        lines = [pick(YU, YD, [ring_load(tmp, (3 * f + i,), step) for step in (0, 1, -1)]) for i in range(3)]
-        sums.append(pick(XU, XD, lines))
+        around = [[ring_load(tmp, (3 * f + i,), step) for step in (0, 1, -1)] for i in range(3)]
+        for word, out in ((r.ow[...], sums), (r.iw[...], inner_sums)):
+            out.append(pick(word, XU, XD, [pick(word, YU, YD, line) for line in around]))
+    inverse = 1.0 / inner_sums[0]
+    for f in range(NFIELD):
+        r.ai[f] = inner_sums[f + 1] * inverse
+    word = r.ow[...]
     inverse = 1.0 / sums[0]
     first = 3 * NFIELD + 3
     for f in range(NFIELD):
@@ -357,6 +359,7 @@
 def average(r, layer):
     rows = r.rows
     tiles = rows // 8
+    lane = lanes_of((8, 128))
     for t in range(tiles):
         at = 8 + 8 * t
         word = r.cw[layer, at : at + 8, :]
@@ -376,8 +379,10 @@
                 parts.append(line[0] + jnp.where(yu, line[1], jnp.where(yd, line[2], 0.0)))
             sums.append(parts[0] + jnp.where(xu, parts[1], jnp.where(xd, parts[2], 0.0)))
         inverse = 1.0 / sums[0]
+        leaves = ((lane == 0) & zd) | ((lane == 127) & zu)
         for f in range(NFIELD):
-            a = sums[f + 1] * inverse
+            column = roll(r.ai[f, 8 * t : 8 * t + 8, :], -2 * layer)
+            a = jnp.where(leaves, column, sums[f + 1] * inverse)
             r.av[f, layer, at : at + 8, :] = a
             if t == tiles - 1:
                 r.av[f, layer, 0:8, :] = a
@@ -424,7 +429,7 @@
     r.inward = jnp.where(even, ZU, ZD)
     r.outward = jnp.where(even, ZD, ZU)
     n = NF * r.cx
-    for g in range(2):
+    for g in range(4):
         for i, row in enumerate((0, 1)):
             r.hz[0, g, row : row + 1, :] = r.y_hi[n + 2 * g + i : n + 2 * g + i + 1, :]
             r.hz[0, g, 7 - row : 8 - row, :] = r.y_lo[n + 2 * g + i : n + 2 * g + i + 1, :]
@@ -435,8 +440,8 @@
     return own_z
 
 
-KEPT = ("cw", "inner", "zi", "zf", "h0", "hm", "hp", "rc", "av")
-SCRATCH = ("ht", "hz", "ow", "tmp_i", "tmp_f", "i1", "zw", "dz")
+KEPT = ("cw", "zf", "h0", "hm", "hp", "rc", "av")
+SCRATCH = ("ht", "hz", "ow", "iw", "tmp_i", "tmp_f", "ci", "zw", "zi", "ai", "dz")
 
 
 def plan(cx, nbx, bx):
@@ -487,7 +492,7 @@
 
 
 def inner_kernel(cx, cy, nbx, *refs):
-    names = ("u", "vf", "c", "zh", "y_lo", "y_hi", *KEPT, "res", *SCRATCH)
+    names = ("u", "vf", "zh", "y_lo", "y_hi", "cw_in", *KEPT, "res", *SCRATCH)
     r = types.SimpleNamespace(cx=cx, cy=cy, **dict(zip(names, refs)))
     own_z = common(r)
     bx, by, bz = place()
@@ -496,17 +501,13 @@
     for x in range(cx):
         y_rows(r, x)
 
-    def words(x, acc):
-        set_words(r, r.c[pl.ds(pl.multiple_of(x * cy, 8), cy), :], x + 2)
-        return collect(r, x + 2, acc)
-
-    inner = lax.fori_loop(0, cx, words, jnp.ones((r.rows, 128), jnp.int32), unroll=4)
-    r.inner[...] = inner
+    for x in range(cx):
+        set_halo_words(r, x + 2)
     outside = x_lanes(r, bx > 0) if nbx == 2 else None
-    for f in range(NF):
+    for f in range(2 * NF):
         value = z_halo(r, f, own_z)
         if nbx == 2:
-            value = jnp.where(outside, EDGE if f >= C1 else 0.0, value)
+            value = jnp.where(outside, EDGE if f % NF >= C1 else 0.0, value)
         r.zf[f] = value
     if nbx == 2:
         edge = todo.at(0)
@@ -514,8 +515,7 @@
         for f in range(NFIELD + 1):
             for h in (r.h0, r.hm, r.hp):
                 ring_store(h, (f, edge), jnp.zeros((r.rows, 128), jnp.float32))
-    z_counts(r, inner)
-    r.zi[...] = jnp.zeros(r.zi.shape, jnp.float32)
+    z_counts(r)
     weigh(r, [(layer, functools.partial(own_field, r, layer - 2)) for layer in todo.inner_weigh])
     z_averages(r)
     each(todo.inner_average, lambda j: average(r, todo.at(j)))
@@ -524,7 +524,7 @@
 
 def outer_kernel(cx, cy, nbx, *refs):
     kept_in = len(KEPT)
-    names = ("u", "vf", "c", "zh", "y_lo", "y_hi", "res", "xa", "xb")
+    names = ("u", "vf", "zh", "y_lo", "y_hi", "res", "xa", "xb")
     ins = refs[: len(names)]
     rest = refs[len(names) + kept_in :]
     r = types.SimpleNamespace(cx=cx, cy=cy, **dict(zip(names, ins)))
@@ -566,7 +566,7 @@
         return value if present is True else jnp.where(present, value, edge)
 
     zrow = NF * cy
-    edges = zrow + 8
+    edges = zrow + 16
     halo = []
     for high, present, part in sides:
         layer, second, own = (choose(high, a, b) for a, b in ((cx + 2, 1), (cx + 3, 0), (cx - 1, 0)))
@@ -576,7 +576,7 @@
             return present_or(present, part(f * cy, cy), EDGE if f >= C1 else 0.0)
 
         for y, row1, row2 in ((0, 7, 6), (1, 0, 1)):
-            base = edges + 8 + 10 * y
+            base = edges + 16 + 10 * y
 
             def rim(i, edge, base=base, present=present, part=part):
                 return present_or(present, part(base + i, 1), edge)
@@ -591,24 +591,20 @@
         set_words(r, raw(C2), second)
         halo.append((layer, lambda f, raw=raw, layer=layer: jnp.concatenate([raw(f), r.ht[f, layer]], axis=0)))
 
-        for g in range(2):
+        for g in range(4):
             for i, row in enumerate((0, 1)):
-                lo, hi = edges + 2 * g + i, edges + 4 + 2 * g + i
+                lo, hi = edges + 2 * g + i, edges + 8 + 2 * g + i
                 r.hz[1, g, row : row + 1, :] = part(hi, 1)
                 r.hz[1, g, 7 - row : 8 - row, :] = part(lo, 1)
         lanes = x_lanes(r, high)
-        for f in range(NF):
+        for f in range(2 * NF):
             g, k = f // 4, f % 4
             shift = 4 - 2 * cx * k + choose(high, 2 * cx, -2 * cx)
-            tile = part(zrow, 8)
-            tiles = [roll(tile, shift - 8 * t - 4 * g) for t in range(cy // 8)]
+            tile = part(zrow + 8 * (g // 2), 8)
+            tiles = [roll(tile, shift - 8 * t - 4 * (g % 2)) for t in range(cy // 8)]
             value = jnp.concatenate([*tiles, roll(r.hz[1, g], shift)], axis=0)
-            r.zf[f] = jnp.where(lanes, present_or(present, value, EDGE if f >= C1 else 0.0), r.zf[f])
-    inner = r.inner[...]
-    for high, _, _ in sides:
-        for a, b in ((cx + 2, 1), (cx + 3, 0)):
-            inner = collect(r, choose(high, a, b), inner)
-    z_counts(r, inner)
+            r.zf[f] = jnp.where(lanes, present_or(present, value, EDGE if f % NF >= C1 else 0.0), r.zf[f])
+    z_counts(r)
     weigh(r, [(layer, functools.partial(own_field, r, layer - 2)) for layer in todo.outer_weigh] + halo)
     z_averages(r)
     for span in todo.outer_average:
@@ -661,33 +657,31 @@
         "pack",
     )(*(pltpu.with_memory_space_constraint(a, pltpu.HBM) for a in (u, vf, mask, code)))
     za, zb = swap(zp, 1, NBZ, False), swap(zp, 1, NBZ, True)
-    ya, yb, *xs = call(
+    rows, ring, layers = cy + 8, cy + 24, cx + 4
+    cw, ya, yb, *xs = call(
         functools.partial(faces_kernel, cx, cy, two_x),
         [on_chip] * 3,
-        [vmem(n), vmem(n)] + [vmem(NF * cy)] * copies,
+        [vmem(layers, ring, dtype=i32), vmem(n), vmem(n)] + [vmem(NF * cy)] * copies,
         name="faces",
         flops=1 << 20,
     )(u, vf, c)
     zh, ya, yb = call(
-        functools.partial(z_merge_kernel, cx, cy), [on_chip] * 4, [vmem(2 * cy), vmem(n + 8), vmem(n + 8)], name="z_merge"
-    )(za, zb, ya, yb)
+        functools.partial(z_merge_kernel, cx, cy), [on_chip] * 5, [vmem(4 * cy), vmem(n + 8), vmem(n + 8)], name="z_merge"
+    )(za, zb, zp, ya, yb)
     yb = swap(yb, NBZ, NBY, True)
     ya = swap(ya, NBZ, NBY, False)
     y_lo, y_hi, *xs = call(
         functools.partial(y_merge_kernel, cx, cy, two_x),
         [on_chip] * (3 + copies),
-        [vmem(n + 8), vmem(n + 8)] + [vmem(NF * cy + 40)] * copies,
+        [vmem(n + 8), vmem(n + 8)] + [vmem(NF * cy + 56)] * copies,
         name="y_merge",
     )(ya, yb, zh, *xs)
     xs = [swap(x, NBY * NBZ, nbx, odd) for odd, x in enumerate(xs)]
     xa, xb = xs if two_x else xs * 2
 
-    rows, ring, layers = cy + 8, cy + 24, cx + 4
     kept = [
         vmem(layers, ring, dtype=i32),
-        vmem(rows, dtype=i32),
-        vmem(NFIELD + 1, rows),
-        vmem(NF, rows),
+        vmem(2 * NF, rows),
         vmem(NFIELD + 1, layers, ring),
         vmem(NFIELD + 1, layers, ring),
         vmem(NFIELD + 1, layers, ring),
@@ -696,12 +690,15 @@
     ]
     scratch = [
         vmem(C2, layers, 8),
-        vmem(2, 2, 8),
+        vmem(2, 4, 8),
         vmem(rows, dtype=i32),
-        vmem(cx, ring, dtype=i32),
+        vmem(rows, dtype=i32),
+        vmem(layers, ring, dtype=i32),
         vmem(9 * NFIELD + 3, ring),
-        vmem(rows, dtype=i32),
+        vmem(rows),
         vmem(NFIELD + 1, rows),
+        vmem(NFIELD + 1, rows),
+        vmem(NFIELD, rows),
         vmem(NFIELD, rows),
     ]
     *state, res = call(
@@ -711,8 +708,9 @@
         scratch,
         "inner",
         flops=1 << 26,
-    )(u, vf, c, zh, y_lo, y_hi)
-    first = 9
+        input_output_aliases={5: 0},
+    )(u, vf, zh, y_lo, y_hi, cw)
+    first = 8
     out, *_ = call(
         functools.partial(outer_kernel, cx, cy, nbx),
         [on_chip] * (first + len(kept)),
@@ -721,7 +719,7 @@
         "outer",
         flops=1 << 25,
         input_output_aliases={first + i: 1 + i for i in range(len(kept))},
-    )(u, vf, c, zh, y_lo, y_hi, res, xa, xb, *state)
+    )(u, vf, zh, y_lo, y_hi, res, xa, xb, *state)
     return out.reshape(conserved.shape)
 
 

time: 28.6 us -> 27.5 us (0.962)
  Pallas kernels: 13.9 us -> 13.1 us
    pallas_call x1, Pallas kernels: 8.54 us -> 7.4 us  [per_device(): call(functools.partial(inner_kernel, cx, cy, nbx), [on_chip] * 6, kept +...]
  transfers between devices with their start and end apart: 5 -> 5, of which waited for: 3 -> 3; matrix products, arithmetic and copies ran while one was open for 0% -> 0% of each run, Pallas kernels for 30% -> 28%
where the time goes in v6:
time: 27.5 us; the launch traced here: 27.4 us
  Pallas kernels  13.1 us (48%)
  starting transfers between devices  9.82 us (36%)
  waiting for transfers between devices  4.45 us (16%)
    ppermute x5, starting transfers between devices, swap(): return lax.ppermute(value, AXIS, pairing(stride, extent, devices, odd))  9.82 us
    pallas_call x1, Pallas kernels, per_device(): call(functools.partial(inner_kernel, cx, cy, nbx), [on_chip] * 6, kept +...  7.4 us
    ppermute x5, waiting for transfers between devices, swap(): return lax.ppermute(value, AXIS, pairing(stride, extent, devices, odd))  4.45 us
    pallas_call x1, Pallas kernels, per_device(): call(functools.partial(outer_kernel, cx, cy, nbx), [on_chip] * (first + l...  2.88 us
    pallas_call x1, Pallas kernels, per_device(): call(functools.partial(pack_kernel, cx, cy), [far] * 4, [vmem(2 * cy), vm...  2.24 us
  transfers between devices with their start and end apart: 5, of which 3 were waited for; matrix products, arithmetic and copies ran while one was open for 0% of the time, Pallas kernels for 28%

profile of v6, /device:TPU:0, one launch (start us, length us, event | category | flops | bytes accessed | tf_op | source)
XLA Modules:
  0.0 27.4 jit_solution(14703486181756504847)
XLA Ops:
  0.0 2.2 %pack.1 = (f32[64,128]{1,0:T(8,128)S(1)}, f32[2560,128]{1,0:T(8,128)S(1)}, f32[512,128]{1,0:T(8,128)S(1)}, f32[512,128]{1,0:T(8,128)S(1)}) custom-call(f32[2560,128]{1,0:T(8,128)} %bitcast.5, f32[512,128]{1,0:T(8,128)} %bitcast.6, s32[512,128]{1,0:T(8,128)} %bitcast.7, s32[512,128]{1,0:T(8,128)} %bitcast.8), custom_call_target="tpu_custom_call" | custom-call | tf_op jit(solution)/shard_map/pack/pallas_call | solution.py:652
  2.2 2.5 %collective-permute-start.1 = (f32[64,128]{1,0:T(8,128)S(1)}, f32[64,128]{1,0:T(8,128)S(1)}, u32[]{:S(2)}, u32[]{:S(2)}) collective-permute-start(f32[64,128]{1,0:T(8,128)S(1)} %get-tuple-element.30.zp), channel_id=1, source_target_pairs={{0,3},{1,2},{2,1},{3,0},{4,7},{5,6},{6,5},{7,4},{8,11},{9,10},{10,... | collective-permute-start | bytes 98312 | tf_op jit(solution)/shard_map/ppermute | solution.py:648
  4.7 0.7 %collective-permute-start = (f32[64,128]{1,0:T(8,128)S(1)}, f32[64,128]{1,0:T(8,128)S(1)}, u32[]{:S(2)}, u32[]{:S(2)}) collective-permute-start(f32[64,128]{1,0:T(8,128)S(1)} %get-tuple-element.30.zp), channel_id=1, source_target_pairs={{0,1},{1,0},{2,3},{3,2},{4,5},{5,4},{6,7},{7,6},{8,9},{9,8},{10,11... | collective-permute-start | bytes 98312 | tf_op jit(solution)/shard_map/ppermute | solution.py:648
  5.4 0.3 %faces.1 = (s32[20,56,128]{2,1,0:T(8,128)S(1)}, f32[128,128]{1,0:T(8,128)S(1)}, f32[128,128]{1,0:T(8,128)S(1)}, f32[256,128]{1,0:T(8,128)S(1)}) custom-call(f32[2560,128]{1,0:T(8,128)S(1)} %get-tuple-element.28.u.refs_0_, f32[512,128]{1,0:T(8,128)S(1)} %get-tuple-element.29.vf.refs_1_, f32[512,128]{1,0:T(8,128)S(1)} %get-tuple-element.31.c), custom_call_target="tpu_custom_call" | custom-call | flops 1048576 | tf_op jit(solution)/shard_map/faces/pallas_call | solution.py:661
  5.7 0.8 %collective-permute-done.1.r_b = f32[64,128]{1,0:T(8,128)S(1)} collective-permute-done((f32[64,128]{1,0:T(8,128)S(1)}, f32[64,128]{1,0:T(8,128)S(1)}, u32[]{:S(2)}, u32[]{:S(2)}) %collective-permute-start.1) | collective-permute-done | bytes 32800 | tf_op jit(solution)/shard_map/ppermute | solution.py:648
  6.5 0.0 collective-permute-done.r_a
  6.5 0.1 z_merge.1
  6.6 2.5 %collective-permute-start.2 = (f32[136,128]{1,0:T(8,128)S(1)}, f32[136,128]{1,0:T(8,128)S(1)}, u32[]{:S(2)}, u32[]{:S(2)}) collective-permute-start(f32[136,128]{1,0:T(8,128)S(1)} %get-tuple-element.35), channel_id=1, source_target_pairs={{0,4},{1,5},{2,6},{3,7},{4,0},{5,1},{6,2},{7,3},{8,12},{9,13},{10,... | collective-permute-start | bytes 208904 | tf_op jit(solution)/shard_map/ppermute | solution.py:648
  9.1 1.5 %collective-permute-start.3 = (f32[136,128]{1,0:T(8,128)S(1)}, f32[136,128]{1,0:T(8,128)S(1)}, u32[]{:S(2)}, u32[]{:S(2)}) collective-permute-start(f32[136,128]{1,0:T(8,128)S(1)} %get-tuple-element.36), channel_id=1, source_target_pairs={{0,12},{1,13},{2,14},{3,15},{4,8},{5,9},{6,10},{7,11},{8,4},{9,5},... | collective-permute-start | bytes 208904 | tf_op jit(solution)/shard_map/ppermute | solution.py:648
  10.6 1.8 %collective-permute-done.2.r_a = f32[136,128]{1,0:T(8,128)S(1)} collective-permute-done((f32[136,128]{1,0:T(8,128)S(1)}, f32[136,128]{1,0:T(8,128)S(1)}, u32[]{:S(2)}, u32[]{:S(2)}) %collective-permute-start.2) | collective-permute-done | bytes 69664 | tf_op jit(solution)/shard_map/ppermute | solution.py:648
  12.5 1.9 %collective-permute-done.3.r_b = f32[136,128]{1,0:T(8,128)S(1)} collective-permute-done((f32[136,128]{1,0:T(8,128)S(1)}, f32[136,128]{1,0:T(8,128)S(1)}, u32[]{:S(2)}, u32[]{:S(2)}) %collective-permute-start.3) | collective-permute-done | bytes 69664 | tf_op jit(solution)/shard_map/ppermute | solution.py:648
  14.3 0.1 y_merge.1
  14.4 2.6 %collective-permute-start.4 = (f32[312,128]{1,0:T(8,128)S(1)}, f32[312,128]{1,0:T(8,128)S(1)}, u32[]{:S(2)}, u32[]{:S(2)}) collective-permute-start(f32[312,128]{1,0:T(8,128)S(1)} %get-tuple-element.42), channel_id=1, source_target_pairs={{0,16},{1,17},{2,18},{3,19},{4,20},{5,21},{6,22},{7,23},{8,24},{9,... | collective-permute-start | bytes 479240 | tf_op jit(solution)/shard_map/ppermute | solution.py:648
  17.1 7.4 %inner.1 = (s32[20,56,128]{2,1,0:T(8,128)S(1)}, f32[16,40,128]{2,1,0:T(8,128)S(1)}, f32[6,20,56,128]{3,2,1,0:T(8,128)S(1)}, f32[6,20,56,128]{3,2,1,0:T(8,128)S(1...) custom-call(f32[2560,128]{1,0:T(8,128)S(1)} %get-tuple-element.28.u., ...), custom_call_target="tpu_custom_call", output_to_operand_aliasing={{0}: (5, {})} | custom-call | flops 67108864 | tf_op jit(solution)/shard_map/inner/pallas_call | solution.py:704
  24.5 0.0 collective-permute-done.4.refs_6_.refs_7_
  24.5 2.9 %outer.1 = (f32[2560,128]{1,0:T(8,128)}, s32[20,56,128]{2,1,0:T(8,128)S(1)}, f32[16,40,128]{2,1,0:T(8,128)S(1)}, f32[6,20,56,128]{3,2,1,0:T(8,128)S(1)}, f32[6,2...) custom-call(f32[2560,128]{1,0:T(8,128)S(1)} %get-tuple-element.28.u., ...), custom_call_target="tpu_custom_call", output_to_operand_aliasing={{1}: (8, {}), {2}: (9, {}), {3}: (10, {}), {4}: (11, {}), {... | custom-call | flops 33554432 | tf_op jit(solution)/shard_map/outer/pallas_call | solution.py:714
Async XLA Ops:
  2.2 4.3 %collective-permute-start.1 = (f32[64,128]{1,0:T(8,128)S(1)}, f32[64,128]{1,0:T(8,128)S(1)}, u32[]{:S(2)}, u32[]{:S(2)}) collective-permute-start(f32[64,128]{1,0:T(8,128)S(1)} %get-tuple-element.30.zp), channel_id=1, source_target_pairs={{0,3},{1,2},{2,1},{3,0},{4,7},{5,6},{6,5},{7,4},{8,11},{9,10},{10,... | collective-permute-start | bytes 98312 | tf_op jit(solution)/shard_map/ppermute | solution.py:648
  4.7 1.8 %collective-permute-start = (f32[64,128]{1,0:T(8,128)S(1)}, f32[64,128]{1,0:T(8,128)S(1)}, u32[]{:S(2)}, u32[]{:S(2)}) collective-permute-start(f32[64,128]{1,0:T(8,128)S(1)} %get-tuple-element.30.zp), channel_id=1, source_target_pairs={{0,1},{1,0},{2,3},{3,2},{4,5},{5,4},{6,7},{7,6},{8,9},{9,8},{10,11... | collective-permute-start | bytes 98312 | tf_op jit(solution)/shard_map/ppermute | solution.py:648
  6.6 5.9 %collective-permute-start.2 = (f32[136,128]{1,0:T(8,128)S(1)}, f32[136,128]{1,0:T(8,128)S(1)}, u32[]{:S(2)}, u32[]{:S(2)}) collective-permute-start(f32[136,128]{1,0:T(8,128)S(1)} %get-tuple-element.35), channel_id=1, source_target_pairs={{0,4},{1,5},{2,6},{3,7},{4,0},{5,1},{6,2},{7,3},{8,12},{9,13},{10,... | collective-permute-start | bytes 208904 | tf_op jit(solution)/shard_map/ppermute | solution.py:648
  9.1 5.2 %collective-permute-start.3 = (f32[136,128]{1,0:T(8,128)S(1)}, f32[136,128]{1,0:T(8,128)S(1)}, u32[]{:S(2)}, u32[]{:S(2)}) collective-permute-start(f32[136,128]{1,0:T(8,128)S(1)} %get-tuple-element.36), channel_id=1, source_target_pairs={{0,12},{1,13},{2,14},{3,15},{4,8},{5,9},{6,10},{7,11},{8,4},{9,5},... | collective-permute-start | bytes 208904 | tf_op jit(solution)/shard_map/ppermute | solution.py:648
  14.4 10.1 %collective-permute-start.4 = (f32[312,128]{1,0:T(8,128)S(1)}, f32[312,128]{1,0:T(8,128)S(1)}, u32[]{:S(2)}, u32[]{:S(2)}) collective-permute-start(f32[312,128]{1,0:T(8,128)S(1)} %get-tuple-element.42), channel_id=1, source_target_pairs={{0,16},{1,17},{2,18},{3,19},{4,20},{5,21},{6,22},{7,23},{8,24},{9,... | collective-permute-start | bytes 479240 | tf_op jit(solution)/shard_map/ppermute | solution.py:648

commit v7 on v6

--- a/solution.py
+++ b/solution.py
@@ -64,18 +64,43 @@
     return (word & bits) == bits
 
 
-def ring_store(ref, lead, value):
-    n = value.shape[0]
-    ref[(*lead, slice(8, 8 + n), slice(None))] = value
-    ref[(*lead, slice(0, 8), slice(None))] = value[n - 8 :]
-
-
-def ring_load(ref, lead, step):
+ALL, OWN, RIM = "all", "own", "rim"
+
+
+def ring_store(ref, lead, value, part=ALL):
+    def put(first, rows):
+        ref[(*lead, slice(first, first + rows.shape[0]), slice(None))] = rows
+
+    if part == RIM:
+        put(8, value[16:])
+        put(ref.shape[-2] - 24, value[:16])
+        put(0, value[8:16])
+    else:
+        put(8, value)
+        if part == ALL:
+            put(0, value[-8:])
+
+
+def ring_load(ref, lead, step, part=ALL):
     n = ref.shape[-2] - 16
-    if step <= 0:
-        return ref[(*lead, slice(8 + step, 8 + step + n), slice(None))]
-    own = ref[(*lead, slice(8 + step, n + step), slice(None))]
-    return jnp.concatenate([own, ref[(*lead, slice(step, 8 + step), slice(None))]], axis=0)
+
+    def get(first, last):
+        return ref[(*lead, slice(first + step, last + step), slice(None))]
+
+    if part == OWN:
+        return get(8, n)
+    if part == RIM:
+        spans = [(n - 8, n), (0, 16)] if step > 0 else [(n - 8, n + 8), (8, 16)]
+    else:
+        spans = [(8, n), (0, 8)] if step > 0 else [(8, n + 8)]
+    return jnp.concatenate([get(*span) for span in spans], axis=0)
+
+
+def cut(value, part):
+    if part == ALL:
+        return value
+    n = value.shape[0] - 8
+    return value[:n] if part == OWN else jnp.concatenate([value[n - 8 :], value[:8]], axis=0)
 
 
 def pack_kernel(cx, cy, u_in, vf_in, mask_in, code_in, zp, u, vf, c, mask, code, sems):
@@ -191,7 +216,7 @@
     return jnp.where(codes, EDGE, 0.0)
 
 
-def y_merge_kernel(cx, cy, two_x, r_a, r_b, zh, *refs):
+def y_merge_kernel(cx, cy, two_x, ended, r_a, r_b, zh, *refs):
     copies = 2 if two_x else 1
     mains, (y_lo, y_hi), xs = refs[:copies], refs[copies : copies + 2], refs[copies + 2 :]
     bx, by, bz = place()
@@ -260,7 +285,7 @@
 
 
 def spread_counts(r, planes, slot):
-    mid = up = down = jnp.zeros((r.rows, 128), jnp.int32)
+    mid = up = down = jnp.zeros(r.lane.shape, jnp.int32)
     for word, bits in planes:
         v = 1 + ((word & YU) << 6) + ((word & YD) << 4)
         if bits is not None:
@@ -269,78 +294,101 @@
         up = up + jnp.where((word & XU) != 0, v, 0)
         down = down + jnp.where((word & XD) != 0, v, 0)
     total = mid + roll(up, 2) + roll(down, -2)
-    ring_store(r.tmp_i, (slot,), total)
-    before, after = ring_load(r.tmp_i, (slot,), -1), ring_load(r.tmp_i, (slot,), 1)
+    ring_store(r.tmp_i, (slot,), total, r.part)
+    before, after = (ring_load(r.tmp_i, (slot,), step, r.part) for step in (-1, 1))
     return (total & 255) + ((before >> 8) & 255) + ((after >> 16) & 255)
 
 
 def z_counts(r):
-    outer1, outer2, inner1, inner2 = (decode(r.zf[f].astype(jnp.int32)) for f in (C1, C2, NF + C1, NF + C2))
-    r.ow[...], r.iw[...] = outer1, inner1
+    rows = slice(0, r.lane.shape[0])
+    outer1, outer2, inner1, inner2 = (decode(r.zf[f, rows].astype(jnp.int32)) for f in (C1, C2, NF + C1, NF + C2))
+    r.ow[rows], r.iw[rows] = outer1, inner1
     planes = ((outer1, None), (outer2, r.inward), (inner1, r.outward)), ((inner1, None), (outer1, r.inward), (inner2, r.outward))
     for first, out, plane in zip((0, NF), (r.zw, r.zi), planes):
         inverse = 1.0 / spread_counts(r, plane, first // NF).astype(jnp.float32)
-        weight = r.zf[first + VF] * inverse
-        out[0] = weight
+        weight = r.zf[first + VF, rows] * inverse
+        out[0, rows] = weight
         for f in range(NFIELD):
-            out[f + 1] = weight * r.zf[first + f]
-    r.ci[...] = inverse
-
-
-def weigh(r, group):
-    rows = r.rows
-    edge_lane = (r.lane == 0) | (r.lane == 127)
+            out[f + 1, rows] = weight * r.zf[first + f, rows]
+    r.ci[rows] = inverse
+
+
+def sum_x(mid, left, right):
+    total = (mid & LOW) + jnp.where((left & XU) != 0, left & LOW, 0)
+    return total + jnp.where((right & XD) != 0, right & LOW, 0)
+
+
+def weigh(r, group, part):
+    n = r.cy
+    lane = lanes_of(({ALL: n + 8, OWN: n, RIM: 24}[part], 128))
+    edge_lane = (lane == 0) | (lane == 127)
     totals = []
-    for slot, (layer, _) in enumerate(group, 2):
-        mid, left, right = (r.cw[layer + d, 8 : 8 + rows, :] for d in (0, -1, 1))
-        total = (mid & LOW) + jnp.where((left & XU) != 0, left & LOW, 0)
-        ring_store(r.tmp_i, (slot,), total + jnp.where((right & XD) != 0, right & LOW, 0))
-    for slot, (layer, _) in enumerate(group, 2):
-        total, before, after = (ring_load(r.tmp_i, (slot,), step) for step in (0, -1, 1))
+    for layer, _ in group:
+        if part == RIM:
+            total = sum_x(*(r.cw[layer + d, 8 + n : 16 + n, :] for d in (0, -1, 1)))
+            r.xt[layer, 8 + n : 16 + n, :] = total
+            r.xt[layer, 0:8, :] = total
+        else:
+            ring_store(r.xt, (layer,), sum_x(*(ring_load(r.cw, (layer + d,), 0, part) for d in (0, -1, 1))), part)
+    for layer, _ in group:
+        total, before, after = (ring_load(r.xt, (layer,), step, part) for step in (0, -1, 1))
         total = (total & 0x333) + ((before >> 2) & 0x333) + ((after >> 12) & 0x333)
-        totals.append((total, roll(total, 1), roll(total, -1), roll(r.ci[...], -2 * layer)))
+        totals.append((total, roll(total, 1), roll(total, -1), roll(cut(r.ci[...], part), -2 * layer)))
     for (layer, field), (total, below, above, edge) in zip(group, totals):
         count = (total & 15) + ((below >> 4) & 15) + ((above >> 8) & 15)
         inverse = jnp.where(edge_lane, edge, 1.0 / count.astype(jnp.float32))
-        r.rc[layer] = inverse[: r.cy]
-        ring_store(r.h0, (0, layer), field(VF) * inverse)
+        if part == RIM:
+            r.rc[layer, n - 8 :], r.rc[layer, 0:8] = inverse[:8], inverse[16:]
+        else:
+            r.rc[layer] = inverse[:n]
+        ring_store(r.h0, (0, layer), field(VF, part) * inverse, part)
     for layer, field in group:
-        weight = ring_load(r.h0, (0, layer), 0)
+        weight = ring_load(r.h0, (0, layer), 0, part)
         for f in range(NFIELD + 1):
             w = weight
             if f:
-                w = weight * field(f - 1)
-                ring_store(r.h0, (f, layer), w)
-            ring_store(r.hm, (f, layer), w + roll(w, 1))
-            ring_store(r.hp, (f, layer), w + roll(w, -1))
-
-
-def own_field(r, x, f):
+                w = weight * field(f - 1, part)
+                ring_store(r.h0, (f, layer), w, part)
+            ring_store(r.hm, (f, layer), w + roll(w, 1), part)
+            ring_store(r.hp, (f, layer), w + roll(w, -1), part)
+
+
+def own_field(r, x, f, part):
     base = (f * r.cx + x if f < NFIELD else x) * r.cy
     ref = r.u if f < NFIELD else r.vf
-    if not isinstance(base, int):
-        base = pl.multiple_of(base, 8)
-    return jnp.concatenate([ref[pl.ds(base, r.cy), :], r.ht[f, x + 2]], axis=0)
-
-
-def z_averages(r):
+
+    def rows(first, count):
+        start = base + first
+        return ref[pl.ds(start if isinstance(start, int) else pl.multiple_of(start, 8), count), :]
+
+    if part == OWN:
+        return rows(0, r.cy)
+    if part == RIM:
+        return jnp.concatenate([rows(r.cy - 8, 8), r.ht[f, x + 2], rows(0, 8)], axis=0)
+    return jnp.concatenate([rows(0, r.cy), r.ht[f, x + 2]], axis=0)
+
+
+def z_averages(r, deposit=True):
     tmp = r.tmp_f
 
     def pick(word, up, down, values):
         mid, plus, minus = values
         return mid + jnp.where((word & up) != 0, plus, jnp.where((word & down) != 0, minus, 0.0))
 
+    rows = slice(0, r.lane.shape[0])
     sums, inner_sums = [], []
     for f in range(NFIELD + 1):
-        both = r.zw[f] + r.zi[f]
+        both = r.zw[f, rows] + r.zi[f, rows]
         for i, value in enumerate((both, roll(both, -2), roll(both, 2))):
-            ring_store(tmp, (3 * f + i,), value)
-        around = [[ring_load(tmp, (3 * f + i,), step) for step in (0, 1, -1)] for i in range(3)]
-        for word, out in ((r.ow[...], sums), (r.iw[...], inner_sums)):
+            ring_store(tmp, (3 * f + i,), value, r.part)
+        around = [[ring_load(tmp, (3 * f + i,), step, r.part) for step in (0, 1, -1)] for i in range(3)]
+        for word, out in ((r.ow[rows], sums), (r.iw[rows], inner_sums))[1 - deposit :]:
             out.append(pick(word, XU, XD, [pick(word, YU, YD, line) for line in around]))
     inverse = 1.0 / inner_sums[0]
     for f in range(NFIELD):
-        r.ai[f] = inner_sums[f + 1] * inverse
+        r.ai[f, rows] = inner_sums[f + 1] * inverse
+    if not deposit:
+        return
     word = r.ow[...]
     inverse = 1.0 / sums[0]
     first = 3 * NFIELD + 3
@@ -356,11 +404,11 @@
         r.dz[f] = totals[0] + roll(totals[1], 2) + roll(totals[2], -2)
 
 
-def average(r, layer):
-    rows = r.rows
+def average(r, layer, rows_of=None):
+    rows = r.cy + 8
     tiles = rows // 8
     lane = lanes_of((8, 128))
-    for t in range(tiles):
+    for t in range(tiles) if rows_of is None else rows_of:
         at = 8 + 8 * t
         word = r.cw[layer, at : at + 8, :]
         zu, zd = (word & ZU) != 0, (word & ZD) != 0
@@ -422,25 +470,23 @@
             out[pl.ds(pl.multiple_of((f * cx + x) * cy + 8 * t, 8), 8), :] = total * inverse
 
 
-def common(r):
-    r.rows = r.cy + 8
-    r.lane = lanes_of((r.rows, 128))
+def common(r, part):
+    r.part = part
+    r.lane = lanes_of((r.cy + (8 if part == ALL else 0), 128))
     even = (r.lane & 1) == 0
     r.inward = jnp.where(even, ZU, ZD)
     r.outward = jnp.where(even, ZD, ZU)
-    n = NF * r.cx
-    for g in range(4):
-        for i, row in enumerate((0, 1)):
-            r.hz[0, g, row : row + 1, :] = r.y_hi[n + 2 * g + i : n + 2 * g + i + 1, :]
-            r.hz[0, g, 7 - row : 8 - row, :] = r.y_lo[n + 2 * g + i : n + 2 * g + i + 1, :]
-
-    def own_z(g):
-        return jnp.concatenate([r.zh[g * r.cy : (g + 1) * r.cy, :], r.hz[0, g]], axis=0)
-
-    return own_z
-
-
-KEPT = ("cw", "zf", "h0", "hm", "hp", "rc", "av")
+
+
+def z_fields(r, rows, own):
+    for f in range(2 * NF):
+        value = z_halo(r, f, own)
+        if r.outside is not None:
+            value = jnp.where(r.outside[: value.shape[0]], EDGE if f % NF >= C1 else 0.0, value)
+        r.zf[f, rows] = value
+
+
+KEPT = ("cw", "zf", "xt", "h0", "hm", "hp", "rc", "av")
 SCRATCH = ("ht", "hz", "ow", "iw", "tmp_i", "tmp_f", "ci", "zw", "zi", "ai", "dz")
 
 
@@ -491,40 +537,61 @@
     lax.fori_loop(span[0], span[0] + span[1], body, 0)
 
 
-def inner_kernel(cx, cy, nbx, *refs):
-    names = ("u", "vf", "zh", "y_lo", "y_hi", "cw_in", *KEPT, "res", *SCRATCH)
+def set_outside(r, nbx, bx):
+    r.outside = x_lanes(r, bx > 0) if nbx == 2 else None
+
+
+def early_kernel(cx, cy, nbx, *refs):
+    names = ("u", "vf", "zh", "cw_in", *KEPT, "ended", *SCRATCH)
     r = types.SimpleNamespace(cx=cx, cy=cy, **dict(zip(names, refs)))
-    own_z = common(r)
+    common(r, OWN)
     bx, by, bz = place()
     todo = plan(cx, nbx, bx)
+    set_outside(r, nbx, bx)
+    z_fields(r, slice(0, cy), lambda g: r.zh[g * cy : (g + 1) * cy, :])
+    if nbx == 2:
+        edge = todo.at(0)
+        ring_store(r.cw, (edge,), jnp.ones((cy + 8, 128), jnp.int32))
+        for f in range(NFIELD + 1):
+            for h in (r.h0, r.hm, r.hp):
+                ring_store(h, (f, edge), jnp.zeros((cy + 8, 128), jnp.float32))
+    z_counts(r)
+    weigh(r, [(layer, functools.partial(own_field, r, layer - 2)) for layer in todo.inner_weigh], OWN)
+    z_averages(r, deposit=False)
+    each(todo.inner_average, lambda j: average(r, todo.at(j), range(1, cy // 8 - 1)))
+    r.ended[...] = r.ci[0:8]
+
+
+def inner_kernel(cx, cy, nbx, *refs):
+    kept_in = len(KEPT)
+    names = ("u", "vf", "y_lo", "y_hi")
+    rest = refs[len(names) + kept_in :]
+    r = types.SimpleNamespace(cx=cx, cy=cy, **dict(zip(names, refs)))
+    r.__dict__.update(zip((*KEPT, "res", *SCRATCH), rest))
+    common(r, ALL)
+    bx, by, bz = place()
+    todo = plan(cx, nbx, bx)
+    set_outside(r, nbx, bx)
     r.ht[...] = jnp.zeros(r.ht.shape, jnp.float32)
     for x in range(cx):
         y_rows(r, x)
-
-    for x in range(cx):
         set_halo_words(r, x + 2)
-    outside = x_lanes(r, bx > 0) if nbx == 2 else None
-    for f in range(2 * NF):
-        value = z_halo(r, f, own_z)
-        if nbx == 2:
-            value = jnp.where(outside, EDGE if f % NF >= C1 else 0.0, value)
-        r.zf[f] = value
-    if nbx == 2:
-        edge = todo.at(0)
-        ring_store(r.cw, (edge,), jnp.ones((r.rows, 128), jnp.int32))
-        for f in range(NFIELD + 1):
-            for h in (r.h0, r.hm, r.hp):
-                ring_store(h, (f, edge), jnp.zeros((r.rows, 128), jnp.float32))
+    n = NF * cx
+    for g in range(4):
+        for i, row in enumerate((0, 1)):
+            r.hz[g, row : row + 1, :] = r.y_hi[n + 2 * g + i : n + 2 * g + i + 1, :]
+            r.hz[g, 7 - row : 8 - row, :] = r.y_lo[n + 2 * g + i : n + 2 * g + i + 1, :]
+    z_fields(r, slice(cy, cy + 8), lambda g: r.hz[g])
     z_counts(r)
-    weigh(r, [(layer, functools.partial(own_field, r, layer - 2)) for layer in todo.inner_weigh])
+    weigh(r, [(layer, functools.partial(own_field, r, layer - 2)) for layer in todo.inner_weigh], RIM)
     z_averages(r)
-    each(todo.inner_average, lambda j: average(r, todo.at(j)))
+    each(todo.inner_average, lambda j: average(r, todo.at(j), (0, cy // 8 - 1, cy // 8)))
     each(todo.inner_spread, lambda j: redistribute(r, todo.at(j) - 2, r.res))
 
 
 def outer_kernel(cx, cy, nbx, *refs):
     kept_in = len(KEPT)
-    names = ("u", "vf", "zh", "y_lo", "y_hi", "res", "xa", "xb")
+    names = ("u", "vf", "y_lo", "y_hi", "res", "xa", "xb")
     ins = refs[: len(names)]
     rest = refs[len(names) + kept_in :]
     r = types.SimpleNamespace(cx=cx, cy=cy, **dict(zip(names, ins)))
@@ -543,7 +610,7 @@
         return copies
 
     copies = send(r.res, todo.inner_rows, 0)
-    common(r)
+    common(r, ALL)
     x_odd = bx % 2 == 1
 
     if nbx == 2:
@@ -589,23 +656,23 @@
             r.ht[C1, second, row2 : row2 + 1, :] = rim(NF + 1, EDGE)
         set_words(r, raw(C1), layer)
         set_words(r, raw(C2), second)
-        halo.append((layer, lambda f, raw=raw, layer=layer: jnp.concatenate([raw(f), r.ht[f, layer]], axis=0)))
+        halo.append((layer, lambda f, part, raw=raw, layer=layer: jnp.concatenate([raw(f), r.ht[f, layer]], axis=0)))
 
         for g in range(4):
             for i, row in enumerate((0, 1)):
                 lo, hi = edges + 2 * g + i, edges + 8 + 2 * g + i
-                r.hz[1, g, row : row + 1, :] = part(hi, 1)
-                r.hz[1, g, 7 - row : 8 - row, :] = part(lo, 1)
+                r.hz[g, row : row + 1, :] = part(hi, 1)
+                r.hz[g, 7 - row : 8 - row, :] = part(lo, 1)
         lanes = x_lanes(r, high)
         for f in range(2 * NF):
             g, k = f // 4, f % 4
             shift = 4 - 2 * cx * k + choose(high, 2 * cx, -2 * cx)
             tile = part(zrow + 8 * (g // 2), 8)
             tiles = [roll(tile, shift - 8 * t - 4 * (g % 2)) for t in range(cy // 8)]
-            value = jnp.concatenate([*tiles, roll(r.hz[1, g], shift)], axis=0)
+            value = jnp.concatenate([*tiles, roll(r.hz[g], shift)], axis=0)
             r.zf[f] = jnp.where(lanes, present_or(present, value, EDGE if f % NF >= C1 else 0.0), r.zf[f])
     z_counts(r)
-    weigh(r, [(layer, functools.partial(own_field, r, layer - 2)) for layer in todo.outer_weigh] + halo)
+    weigh(r, [(layer, functools.partial(own_field, r, layer - 2)) for layer in todo.outer_weigh] + halo, ALL)
     z_averages(r)
     for span in todo.outer_average:
         each(span, lambda j: average(r, todo.at(j)))
@@ -668,20 +735,10 @@
     zh, ya, yb = call(
         functools.partial(z_merge_kernel, cx, cy), [on_chip] * 5, [vmem(4 * cy), vmem(n + 8), vmem(n + 8)], name="z_merge"
     )(za, zb, zp, ya, yb)
-    yb = swap(yb, NBZ, NBY, True)
-    ya = swap(ya, NBZ, NBY, False)
-    y_lo, y_hi, *xs = call(
-        functools.partial(y_merge_kernel, cx, cy, two_x),
-        [on_chip] * (3 + copies),
-        [vmem(n + 8), vmem(n + 8)] + [vmem(NF * cy + 56)] * copies,
-        name="y_merge",
-    )(ya, yb, zh, *xs)
-    xs = [swap(x, NBY * NBZ, nbx, odd) for odd, x in enumerate(xs)]
-    xa, xb = xs if two_x else xs * 2
-
     kept = [
         vmem(layers, ring, dtype=i32),
         vmem(2 * NF, rows),
+        vmem(layers, ring, dtype=i32),
         vmem(NFIELD + 1, layers, ring),
         vmem(NFIELD + 1, layers, ring),
         vmem(NFIELD + 1, layers, ring),
@@ -690,10 +747,10 @@
     ]
     scratch = [
         vmem(C2, layers, 8),
-        vmem(2, 4, 8),
+        vmem(4, 8),
         vmem(rows, dtype=i32),
         vmem(rows, dtype=i32),
-        vmem(layers, ring, dtype=i32),
+        vmem(2, ring, dtype=i32),
         vmem(9 * NFIELD + 3, ring),
         vmem(rows),
         vmem(NFIELD + 1, rows),
@@ -701,16 +758,36 @@
         vmem(NFIELD, rows),
         vmem(NFIELD, rows),
     ]
+    yb = swap(yb, NBZ, NBY, True)
+    ya = swap(ya, NBZ, NBY, False)
+    *state, ended = call(
+        functools.partial(early_kernel, cx, cy, nbx),
+        [on_chip] * 4,
+        kept + [vmem(8)],
+        scratch,
+        "early",
+        flops=1 << 24,
+        input_output_aliases={3: 0},
+    )(u, vf, zh, cw)
+    y_lo, y_hi, *xs = call(
+        functools.partial(y_merge_kernel, cx, cy, two_x),
+        [on_chip] * (4 + copies),
+        [vmem(n + 8), vmem(n + 8)] + [vmem(NF * cy + 56)] * copies,
+        name="y_merge",
+    )(ended, ya, yb, zh, *xs)
+    xs = [swap(x, NBY * NBZ, nbx, odd) for odd, x in enumerate(xs)]
+    xa, xb = xs if two_x else xs * 2
+
     *state, res = call(
         functools.partial(inner_kernel, cx, cy, nbx),
-        [on_chip] * 6,
+        [on_chip] * (4 + len(kept)),
         kept + [vmem(NFIELD * cells)],
         scratch,
         "inner",
         flops=1 << 26,
-        input_output_aliases={5: 0},
-    )(u, vf, zh, y_lo, y_hi, cw)
-    first = 8
+        input_output_aliases={4 + i: i for i in range(len(kept))},
+    )(u, vf, y_lo, y_hi, *state)
+    first = 7
     out, *_ = call(
         functools.partial(outer_kernel, cx, cy, nbx),
         [on_chip] * (first + len(kept)),
@@ -719,7 +796,7 @@
         "outer",
         flops=1 << 25,
         input_output_aliases={first + i: 1 + i for i in range(len(kept))},
-    )(u, vf, zh, y_lo, y_hi, res, xa, xb, *state)
+    )(u, vf, y_lo, y_hi, res, xa, xb, *state)
     return out.reshape(conserved.shape)
 
 

time: 27.5 us -> 26.8 us (0.975)
  waiting for transfers between devices: 4.45 us -> 1.96 us
  Pallas kernels: 13.1 us -> 14.9 us
    ppermute x5, waiting for transfers between devices: 4.45 us -> 1.96 us  [swap(): return lax.ppermute(value, AXIS, pairing(stride, extent, devices, odd))]
    pallas_call x2 -> x3, Pallas kernels: 7.49 us -> 9.19 us  [the longest x1 6.12 us: per_device(): call(functools.partial(inner_kernel, cx, cy, nbx), [on_chip] * (4 + len(k...]
  transfers between devices with their start and end apart: 5 -> 5, of which waited for: 3 -> 3; matrix products, arithmetic and copies ran while one was open for 0% -> 0% of each run, Pallas kernels for 28% -> 35%
where the time goes in v7:
time: 26.8 us; the launch traced here: 26.7 us
  Pallas kernels  14.9 us (56%)
  starting transfers between devices  9.82 us (37%)
  waiting for transfers between devices  1.96 us (7%)
    ppermute x5, starting transfers between devices, swap(): return lax.ppermute(value, AXIS, pairing(stride, extent, devices, odd))  9.82 us
    pallas_call x1, Pallas kernels, per_device(): call(functools.partial(inner_kernel, cx, cy, nbx), [on_chip] * (4 + len(k...  6.12 us
    pallas_call x1, Pallas kernels, per_device(): call(functools.partial(outer_kernel, cx, cy, nbx), [on_chip] * (first + l...  2.99 us
    pallas_call x1, Pallas kernels, per_device(): call(functools.partial(early_kernel, cx, cy, nbx), [on_chip] * 4, kept +...  2.99 us
    pallas_call x1, Pallas kernels, per_device(): call(functools.partial(pack_kernel, cx, cy), [far] * 4, [vmem(2 * cy), vm...  2.24 us
    ppermute x5, waiting for transfers between devices, swap(): return lax.ppermute(value, AXIS, pairing(stride, extent, devices, odd))  1.96 us
  transfers between devices with their start and end apart: 5, of which 3 were waited for; matrix products, arithmetic and copies ran while one was open for 0% of the time, Pallas kernels for 35%

profile of v7, /device:TPU:0, one launch (start us, length us, event | category | flops | bytes accessed | tf_op | source)
XLA Modules:
  0.0 26.7 jit_solution(17314090881811743541)
XLA Ops:
  0.0 2.2 %pack.1 = (f32[64,128]{1,0:T(8,128)S(1)}, f32[2560,128]{1,0:T(8,128)S(1)}, f32[512,128]{1,0:T(8,128)S(1)}, f32[512,128]{1,0:T(8,128)S(1)}) custom-call(f32[2560,128]{1,0:T(8,128)} %bitcast.5, f32[512,128]{1,0:T(8,128)} %bitcast.6, s32[512,128]{1,0:T(8,128)} %bitcast.7, s32[512,128]{1,0:T(8,128)} %bitcast.8), custom_call_target="tpu_custom_call" | custom-call | tf_op jit(solution)/shard_map/pack/pallas_call | solution.py:719
  2.2 2.5 %collective-permute-start.1 = (f32[64,128]{1,0:T(8,128)S(1)}, f32[64,128]{1,0:T(8,128)S(1)}, u32[]{:S(2)}, u32[]{:S(2)}) collective-permute-start(f32[64,128]{1,0:T(8,128)S(1)} %get-tuple-element.40.zp), channel_id=1, source_target_pairs={{0,3},{1,2},{2,1},{3,0},{4,7},{5,6},{6,5},{7,4},{8,11},{9,10},{10,... | collective-permute-start | bytes 98312 | tf_op jit(solution)/shard_map/ppermute | solution.py:715
  4.7 0.7 %collective-permute-start = (f32[64,128]{1,0:T(8,128)S(1)}, f32[64,128]{1,0:T(8,128)S(1)}, u32[]{:S(2)}, u32[]{:S(2)}) collective-permute-start(f32[64,128]{1,0:T(8,128)S(1)} %get-tuple-element.40.zp), channel_id=1, source_target_pairs={{0,1},{1,0},{2,3},{3,2},{4,5},{5,4},{6,7},{7,6},{8,9},{9,8},{10,11... | collective-permute-start | bytes 98312 | tf_op jit(solution)/shard_map/ppermute | solution.py:715
  5.4 0.3 %faces.1 = (s32[20,56,128]{2,1,0:T(8,128)S(1)}, f32[128,128]{1,0:T(8,128)S(1)}, f32[128,128]{1,0:T(8,128)S(1)}, f32[256,128]{1,0:T(8,128)S(1)}) custom-call(f32[2560,128]{1,0:T(8,128)S(1)} %get-tuple-element.38.u.refs_0_, f32[512,128]{1,0:T(8,128)S(1)} %get-tuple-element.39.vf.refs_1_, f32[512,128]{1,0:T(8,128)S(1)} %get-tuple-element.41.c), custom_call_target="tpu_custom_call" | custom-call | flops 1048576 | tf_op jit(solution)/shard_map/faces/pallas_call | solution.py:728
  5.7 0.8 %collective-permute-done.1.r_b = f32[64,128]{1,0:T(8,128)S(1)} collective-permute-done((f32[64,128]{1,0:T(8,128)S(1)}, f32[64,128]{1,0:T(8,128)S(1)}, u32[]{:S(2)}, u32[]{:S(2)}) %collective-permute-start.1) | collective-permute-done | bytes 32800 | tf_op jit(solution)/shard_map/ppermute | solution.py:715
  6.5 0.0 collective-permute-done.r_a
  6.5 0.1 z_merge.1
  6.6 2.5 %collective-permute-start.2 = (f32[136,128]{1,0:T(8,128)S(1)}, f32[136,128]{1,0:T(8,128)S(1)}, u32[]{:S(2)}, u32[]{:S(2)}) collective-permute-start(f32[136,128]{1,0:T(8,128)S(1)} %get-tuple-element.47), channel_id=1, source_target_pairs={{0,4},{1,5},{2,6},{3,7},{4,0},{5,1},{6,2},{7,3},{8,12},{9,13},{10,... | collective-permute-start | bytes 208904 | tf_op jit(solution)/shard_map/ppermute | solution.py:715
  9.1 1.5 %collective-permute-start.3 = (f32[136,128]{1,0:T(8,128)S(1)}, f32[136,128]{1,0:T(8,128)S(1)}, u32[]{:S(2)}, u32[]{:S(2)}) collective-permute-start(f32[136,128]{1,0:T(8,128)S(1)} %get-tuple-element.48), channel_id=1, source_target_pairs={{0,12},{1,13},{2,14},{3,15},{4,8},{5,9},{6,10},{7,11},{8,4},{9,5},... | collective-permute-start | bytes 208904 | tf_op jit(solution)/shard_map/ppermute | solution.py:715
  10.6 3.0 %early.1 = (s32[20,56,128]{2,1,0:T(8,128)S(1)}, f32[16,40,128]{2,1,0:T(8,128)S(1)}, s32[20,56,128]{2,1,0:T(8,128)S(1)}, f32[6,20,56,128]{3,2,1,0:T(8,128)S(1)}, ...) custom-call(f32[2560,128]{1,0:T(8,128)S(1)} %get-tuple-element.38.u., ...), custom_call_target="tpu_custom_call", output_to_operand_aliasing={{0}: (3, {})} | custom-call | flops 16777216 | tf_op jit(solution)/shard_map/early/pallas_call | solution.py:763
  13.6 0.0 collective-permute-done.2.r_a
  13.6 0.7 %collective-permute-done.3.r_b = f32[136,128]{1,0:T(8,128)S(1)} collective-permute-done((f32[136,128]{1,0:T(8,128)S(1)}, f32[136,128]{1,0:T(8,128)S(1)}, u32[]{:S(2)}, u32[]{:S(2)}) %collective-permute-start.3) | collective-permute-done | bytes 69664 | tf_op jit(solution)/shard_map/ppermute | solution.py:715
  14.3 0.1 y_merge.1
  14.4 2.6 %collective-permute-start.4 = (f32[312,128]{1,0:T(8,128)S(1)}, f32[312,128]{1,0:T(8,128)S(1)}, u32[]{:S(2)}, u32[]{:S(2)}) collective-permute-start(f32[312,128]{1,0:T(8,128)S(1)} %get-tuple-element.61), channel_id=1, source_target_pairs={{0,16},{1,17},{2,18},{3,19},{4,20},{5,21},{6,22},{7,23},{8,24},{9,... | collective-permute-start | bytes 479240 | tf_op jit(solution)/shard_map/ppermute | solution.py:715
  17.1 6.1 %inner.1 = (s32[20,56,128]{2,1,0:T(8,128)S(1)}, f32[16,40,128]{2,1,0:T(8,128)S(1)}, s32[20,56,128]{2,1,0:T(8,128)S(1)}, f32[6,20,56,128]{3,2,1,0:T(8,128)S(1)}, ...) custom-call(f32[2560,128]{1,0:T(8,128)S(1)} %get-tuple-element.38.u., ...), custom_call_target="tpu_custom_call", output_to_operand_aliasing={{0}: (4, {}), {1}: (5, {}), {2}: (6, {}), {3}: (7, {}), {4}... | custom-call | flops 67108864 | tf_op jit(solution)/shard_map/inner/pallas_call | solution.py:781
  23.2 0.5 %collective-permute-done.4.refs_5_.refs_6_ = f32[312,128]{1,0:T(8,128)S(1)} collective-permute-done((f32[312,128]{1,0:T(8,128)S(1)}, f32[312,128]{1,0:T(8,128)S(1)}, u32[]{:S(2)}, u32[]{:S(2)}) %collective-permute-start.4) | collective-permute-done | bytes 159776 | tf_op jit(solution)/shard_map/ppermute | solution.py:715
  23.7 3.0 %outer.1 = (f32[2560,128]{1,0:T(8,128)}, s32[20,56,128]{2,1,0:T(8,128)S(1)}, f32[16,40,128]{2,1,0:T(8,128)S(1)}, s32[20,56,128]{2,1,0:T(8,128)S(1)}, f32[6,20,56...) custom-call(f32[2560,128]{1,0:T(8,128)S(1)} %get-tuple-element.38.u., ...), custom_call_target="tpu_custom_call", output_to_operand_aliasing={{1}: (7, {}), {2}: (8, {}), {3}: (9, {}), {4}: (10, {}), {5... | custom-call | flops 33554432 | tf_op jit(solution)/shard_map/outer/pallas_call | solution.py:791
Async XLA Ops:
  2.2 4.3 %collective-permute-start.1 = (f32[64,128]{1,0:T(8,128)S(1)}, f32[64,128]{1,0:T(8,128)S(1)}, u32[]{:S(2)}, u32[]{:S(2)}) collective-permute-start(f32[64,128]{1,0:T(8,128)S(1)} %get-tuple-element.40.zp), channel_id=1, source_target_pairs={{0,3},{1,2},{2,1},{3,0},{4,7},{5,6},{6,5},{7,4},{8,11},{9,10},{10,... | collective-permute-start | bytes 98312 | tf_op jit(solution)/shard_map/ppermute | solution.py:715
  4.7 1.8 %collective-permute-start = (f32[64,128]{1,0:T(8,128)S(1)}, f32[64,128]{1,0:T(8,128)S(1)}, u32[]{:S(2)}, u32[]{:S(2)}) collective-permute-start(f32[64,128]{1,0:T(8,128)S(1)} %get-tuple-element.40.zp), channel_id=1, source_target_pairs={{0,1},{1,0},{2,3},{3,2},{4,5},{5,4},{6,7},{7,6},{8,9},{9,8},{10,11... | collective-permute-start | bytes 98312 | tf_op jit(solution)/shard_map/ppermute | solution.py:715
  6.6 7.0 %collective-permute-start.2 = (f32[136,128]{1,0:T(8,128)S(1)}, f32[136,128]{1,0:T(8,128)S(1)}, u32[]{:S(2)}, u32[]{:S(2)}) collective-permute-start(f32[136,128]{1,0:T(8,128)S(1)} %get-tuple-element.47), channel_id=1, source_target_pairs={{0,4},{1,5},{2,6},{3,7},{4,0},{5,1},{6,2},{7,3},{8,12},{9,13},{10,... | collective-permute-start | bytes 208904 | tf_op jit(solution)/shard_map/ppermute | solution.py:715
  9.1 5.2 %collective-permute-start.3 = (f32[136,128]{1,0:T(8,128)S(1)}, f32[136,128]{1,0:T(8,128)S(1)}, u32[]{:S(2)}, u32[]{:S(2)}) collective-permute-start(f32[136,128]{1,0:T(8,128)S(1)} %get-tuple-element.48), channel_id=1, source_target_pairs={{0,12},{1,13},{2,14},{3,15},{4,8},{5,9},{6,10},{7,11},{8,4},{9,5},... | collective-permute-start | bytes 208904 | tf_op jit(solution)/shard_map/ppermute | solution.py:715
  14.4 9.3 %collective-permute-start.4 = (f32[312,128]{1,0:T(8,128)S(1)}, f32[312,128]{1,0:T(8,128)S(1)}, u32[]{:S(2)}, u32[]{:S(2)}) collective-permute-start(f32[312,128]{1,0:T(8,128)S(1)} %get-tuple-element.61), channel_id=1, source_target_pairs={{0,16},{1,17},{2,18},{3,19},{4,20},{5,21},{6,22},{7,23},{8,24},{9,... | collective-permute-start | bytes 479240 | tf_op jit(solution)/shard_map/ppermute | solution.py:715

commit v8 on v7

--- a/solution.py
+++ b/solution.py
@@ -242,9 +242,9 @@
                     tile = jnp.where((spot >= start) & (spot < start + 4), roll(zh[row : row + 8, :], start), tile)
             out[at : at + 8, :] = tile
             at += 8
-        for y in (y_lo, y_hi):
-            out[at : at + 8, :] = y[n : n + 8, :]
-            at += 8
+        low, up = y_lo[n : n + 8, :], y_hi[n : n + 8, :]
+        out[at : at + 8, :] = jnp.where(spot < 4, low, roll(up, 4))
+        at += 8
         for y in (y_lo, y_hi):
             for f in range(NF):
                 out[at : at + 1, :] = y[pl.ds(f * cx + rim, 1), :]
@@ -506,7 +506,6 @@
             outer_average=[(cx - 1, 3)],
             outer_spread=[(cx - 2, 3)],
             inner_rows=(jnp.where(high, 0, 3), cx - 3),
-            outer_rows=[(jnp.where(high, cx - 3, 0), 3)],
         )
     return types.SimpleNamespace(
         at=lambda j: j + 1,
@@ -517,7 +516,6 @@
         outer_average=[(0, 3), (cx - 1, 3)],
         outer_spread=[(1, 3), (cx - 2, 3)],
         inner_rows=(3, cx - 6),
-        outer_rows=[(0, 3), (cx - 3, 3)],
     )
 
 
@@ -600,16 +598,19 @@
     bx, by, bz = place()
     todo = plan(cx, nbx, bx)
 
-    def send(src, rows, base):
-        copies = []
+    def copy(src, first, count, f, semaphore):
+        start = pl.multiple_of(f * size + first * cy, 8)
+        part = pl.ds(start, count * cy)
+        return pltpu.make_async_copy(src.at[part, :], r.out.at[part, :], r.sems.at[semaphore])
+
+    each((0, NFIELD), lambda f: copy(r.res, *todo.inner_rows, f, f).start())
+
+    def finish_layer(j, first, turn):
+        x = todo.at(j) - 2
+        redistribute(r, x, r.rim)
         for f in range(NFIELD):
-            part = pl.ds(pl.multiple_of(f * size + rows[0] * cy, 8), rows[1] * cy)
-            copies.append(pltpu.make_async_copy(src.at[part, :], r.out.at[part, :], r.sems.at[base + f]))
-        for copy in copies:
-            copy.start()
-        return copies
-
-    copies = send(r.res, todo.inner_rows, 0)
+            copy(r.rim, x, 1, f, (turn + j - first) * NFIELD + f).start()
+
     common(r, ALL)
     x_odd = bx % 2 == 1
 
@@ -643,7 +644,7 @@
             return present_or(present, part(f * cy, cy), EDGE if f >= C1 else 0.0)
 
         for y, row1, row2 in ((0, 7, 6), (1, 0, 1)):
-            base = edges + 16 + 10 * y
+            base = edges + 8 + 10 * y
 
             def rim(i, edge, base=base, present=present, part=part):
                 return present_or(present, part(base + i, 1), edge)
@@ -658,11 +659,13 @@
         set_words(r, raw(C2), second)
         halo.append((layer, lambda f, part, raw=raw, layer=layer: jnp.concatenate([raw(f), r.ht[f, layer]], axis=0)))
 
+        edge_rows = part(edges, 8)
+        upper_rows = roll(edge_rows, -4)
         for g in range(4):
             for i, row in enumerate((0, 1)):
-                lo, hi = edges + 2 * g + i, edges + 8 + 2 * g + i
-                r.hz[g, row : row + 1, :] = part(hi, 1)
-                r.hz[g, 7 - row : 8 - row, :] = part(lo, 1)
+                at = 2 * g + i
+                r.hz[g, row : row + 1, :] = upper_rows[at : at + 1]
+                r.hz[g, 7 - row : 8 - row, :] = edge_rows[at : at + 1]
         lanes = x_lanes(r, high)
         for f in range(2 * NF):
             g, k = f // 4, f % 4
@@ -676,11 +679,18 @@
     z_averages(r)
     for span in todo.outer_average:
         each(span, lambda j: average(r, todo.at(j)))
-    for i, (span, rows) in enumerate(zip(todo.outer_spread, todo.outer_rows)):
-        each(span, lambda j: redistribute(r, todo.at(j) - 2, r.rim))
-        copies += send(r.rim, rows, (1 + i) * NFIELD)
-    for copy in copies:
-        copy.wait()
+    turn = 1
+    for first, count in todo.outer_spread:
+        each((first, count), lambda j: finish_layer(j, first, turn))
+        turn += count
+    turn = 1
+    for first, count in todo.outer_spread:
+        for j in range(first, first + count):
+            for f in range(NFIELD):
+                copy(r.rim, todo.at(j) - 2, 1, f, turn * NFIELD + f).wait()
+            turn += 1
+    for f in range(NFIELD):
+        copy(r.res, *todo.inner_rows, f, f).wait()
 
 
 def call(kernel, ins, outs, scratch=(), name=None, grant=8, flops=0, **kwargs):
@@ -772,7 +782,7 @@
     y_lo, y_hi, *xs = call(
         functools.partial(y_merge_kernel, cx, cy, two_x),
         [on_chip] * (4 + copies),
-        [vmem(n + 8), vmem(n + 8)] + [vmem(NF * cy + 56)] * copies,
+        [vmem(n + 8), vmem(n + 8)] + [vmem(NF * cy + 48)] * copies,
         name="y_merge",
     )(ended, ya, yb, zh, *xs)
     xs = [swap(x, NBY * NBZ, nbx, odd) for odd, x in enumerate(xs)]
@@ -792,7 +802,7 @@
         functools.partial(outer_kernel, cx, cy, nbx),
         [on_chip] * (first + len(kept)),
         [pltpu.HBM((NFIELD * cells, cz), f32)] + kept,
-        scratch + [vmem(NFIELD * cells), pltpu.SemaphoreType.DMA((3 * NFIELD,))],
+        scratch + [vmem(NFIELD * cells), pltpu.SemaphoreType.DMA((7 * NFIELD,))],
         "outer",
         flops=1 << 25,
         input_output_aliases={first + i: 1 + i for i in range(len(kept))},

time: 26.8 us -> 26.4 us (0.985)
  Pallas kernels: 14.9 us -> 14.2 us
    pallas_call x1, Pallas kernels: 2.99 us -> 2.66 us  [per_device(): call(functools.partial(early_kernel, cx, cy, nbx), [on_chip] * 4, kept +...]
    pallas_call x1, Pallas kernels: 6.12 us -> 5.83 us  [per_device(): call(functools.partial(inner_kernel, cx, cy, nbx), [on_chip] * (4 + len(k...]
  transfers between devices with their start and end apart: 5 -> 5, of which waited for: 3 -> 3; matrix products, arithmetic and copies ran while one was open for 0% -> 0% of each run, Pallas kernels for 35% -> 34%
where the time goes in v8:
time: 26.4 us; the launch traced here: 26.2 us
  Pallas kernels  14.2 us (54%)
  starting transfers between devices  9.82 us (37%)
  waiting for transfers between devices  2.19 us (8%)
    ppermute x5, starting transfers between devices, swap(): return lax.ppermute(value, AXIS, pairing(stride, extent, devices, odd))  9.82 us
    pallas_call x1, Pallas kernels, per_device(): call(functools.partial(inner_kernel, cx, cy, nbx), [on_chip] * (4 + len(k...  5.83 us
    pallas_call x1, Pallas kernels, per_device(): call(functools.partial(outer_kernel, cx, cy, nbx), [on_chip] * (first + l...  2.89 us
    pallas_call x1, Pallas kernels, per_device(): call(functools.partial(early_kernel, cx, cy, nbx), [on_chip] * 4, kept +...  2.66 us
    pallas_call x1, Pallas kernels, per_device(): call(functools.partial(pack_kernel, cx, cy), [far] * 4, [vmem(2 * cy), vm...  2.24 us
    ppermute x5, waiting for transfers between devices, swap(): return lax.ppermute(value, AXIS, pairing(stride, extent, devices, odd))  2.19 us
  transfers between devices with their start and end apart: 5, of which 3 were waited for; matrix products, arithmetic and copies ran while one was open for 0% of the time, Pallas kernels for 34%

profile of v8, /device:TPU:0, one launch (start us, length us, event | category | flops | bytes accessed | tf_op | source)
XLA Modules:
  0.0 26.2 jit_solution(10032487726370323371)
XLA Ops:
  0.0 2.2 %pack.1 = (f32[64,128]{1,0:T(8,128)S(1)}, f32[2560,128]{1,0:T(8,128)S(1)}, f32[512,128]{1,0:T(8,128)S(1)}, f32[512,128]{1,0:T(8,128)S(1)}) custom-call(f32[2560,128]{1,0:T(8,128)} %bitcast.5, f32[512,128]{1,0:T(8,128)} %bitcast.6, s32[512,128]{1,0:T(8,128)} %bitcast.7, s32[512,128]{1,0:T(8,128)} %bitcast.8), custom_call_target="tpu_custom_call" | custom-call | tf_op jit(solution)/shard_map/pack/pallas_call | solution.py:729
  2.2 2.5 %collective-permute-start.1 = (f32[64,128]{1,0:T(8,128)S(1)}, f32[64,128]{1,0:T(8,128)S(1)}, u32[]{:S(2)}, u32[]{:S(2)}) collective-permute-start(f32[64,128]{1,0:T(8,128)S(1)} %get-tuple-element.40.zp), channel_id=1, source_target_pairs={{0,3},{1,2},{2,1},{3,0},{4,7},{5,6},{6,5},{7,4},{8,11},{9,10},{10,... | collective-permute-start | bytes 98312 | tf_op jit(solution)/shard_map/ppermute | solution.py:725
  4.7 0.7 %collective-permute-start = (f32[64,128]{1,0:T(8,128)S(1)}, f32[64,128]{1,0:T(8,128)S(1)}, u32[]{:S(2)}, u32[]{:S(2)}) collective-permute-start(f32[64,128]{1,0:T(8,128)S(1)} %get-tuple-element.40.zp), channel_id=1, source_target_pairs={{0,1},{1,0},{2,3},{3,2},{4,5},{5,4},{6,7},{7,6},{8,9},{9,8},{10,11... | collective-permute-start | bytes 98312 | tf_op jit(solution)/shard_map/ppermute | solution.py:725
  5.4 0.3 %faces.1 = (s32[20,56,128]{2,1,0:T(8,128)S(1)}, f32[128,128]{1,0:T(8,128)S(1)}, f32[128,128]{1,0:T(8,128)S(1)}, f32[256,128]{1,0:T(8,128)S(1)}) custom-call(f32[2560,128]{1,0:T(8,128)S(1)} %get-tuple-element.38.u.refs_0_, f32[512,128]{1,0:T(8,128)S(1)} %get-tuple-element.39.vf.refs_1_, f32[512,128]{1,0:T(8,128)S(1)} %get-tuple-element.41.c), custom_call_target="tpu_custom_call" | custom-call | flops 1048576 | tf_op jit(solution)/shard_map/faces/pallas_call | solution.py:738
  5.7 0.8 %collective-permute-done.1.r_b = f32[64,128]{1,0:T(8,128)S(1)} collective-permute-done((f32[64,128]{1,0:T(8,128)S(1)}, f32[64,128]{1,0:T(8,128)S(1)}, u32[]{:S(2)}, u32[]{:S(2)}) %collective-permute-start.1) | collective-permute-done | bytes 32800 | tf_op jit(solution)/shard_map/ppermute | solution.py:725
  6.5 0.0 collective-permute-done.r_a
  6.5 0.1 z_merge.1
  6.6 2.5 %collective-permute-start.2 = (f32[136,128]{1,0:T(8,128)S(1)}, f32[136,128]{1,0:T(8,128)S(1)}, u32[]{:S(2)}, u32[]{:S(2)}) collective-permute-start(f32[136,128]{1,0:T(8,128)S(1)} %get-tuple-element.47), channel_id=1, source_target_pairs={{0,4},{1,5},{2,6},{3,7},{4,0},{5,1},{6,2},{7,3},{8,12},{9,13},{10,... | collective-permute-start | bytes 208904 | tf_op jit(solution)/shard_map/ppermute | solution.py:725
  9.1 1.5 %collective-permute-start.3 = (f32[136,128]{1,0:T(8,128)S(1)}, f32[136,128]{1,0:T(8,128)S(1)}, u32[]{:S(2)}, u32[]{:S(2)}) collective-permute-start(f32[136,128]{1,0:T(8,128)S(1)} %get-tuple-element.48), channel_id=1, source_target_pairs={{0,12},{1,13},{2,14},{3,15},{4,8},{5,9},{6,10},{7,11},{8,4},{9,5},... | collective-permute-start | bytes 208904 | tf_op jit(solution)/shard_map/ppermute | solution.py:725
  10.6 2.7 %early.1 = (s32[20,56,128]{2,1,0:T(8,128)S(1)}, f32[16,40,128]{2,1,0:T(8,128)S(1)}, s32[20,56,128]{2,1,0:T(8,128)S(1)}, f32[6,20,56,128]{3,2,1,0:T(8,128)S(1)}, ...) custom-call(f32[2560,128]{1,0:T(8,128)S(1)} %get-tuple-element.38.u., ...), custom_call_target="tpu_custom_call", output_to_operand_aliasing={{0}: (3, {})} | custom-call | flops 16777216 | tf_op jit(solution)/shard_map/early/pallas_call | solution.py:773
  13.3 0.0 collective-permute-done.2.r_a
  13.3 1.0 %collective-permute-done.3.r_b = f32[136,128]{1,0:T(8,128)S(1)} collective-permute-done((f32[136,128]{1,0:T(8,128)S(1)}, f32[136,128]{1,0:T(8,128)S(1)}, u32[]{:S(2)}, u32[]{:S(2)}) %collective-permute-start.3) | collective-permute-done | bytes 69664 | tf_op jit(solution)/shard_map/ppermute | solution.py:725
  14.3 0.1 y_merge.1
  14.4 2.6 %collective-permute-start.4 = (f32[304,128]{1,0:T(8,128)S(1)}, f32[304,128]{1,0:T(8,128)S(1)}, u32[]{:S(2)}, u32[]{:S(2)}) collective-permute-start(f32[304,128]{1,0:T(8,128)S(1)} %get-tuple-element.61), channel_id=1, source_target_pairs={{0,16},{1,17},{2,18},{3,19},{4,20},{5,21},{6,22},{7,23},{8,24},{9,... | collective-permute-start | bytes 466952 | tf_op jit(solution)/shard_map/ppermute | solution.py:725
  17.1 5.8 %inner.1 = (s32[20,56,128]{2,1,0:T(8,128)S(1)}, f32[16,40,128]{2,1,0:T(8,128)S(1)}, s32[20,56,128]{2,1,0:T(8,128)S(1)}, f32[6,20,56,128]{3,2,1,0:T(8,128)S(1)}, ...) custom-call(f32[2560,128]{1,0:T(8,128)S(1)} %get-tuple-element.38.u., ...), custom_call_target="tpu_custom_call", output_to_operand_aliasing={{0}: (4, {}), {1}: (5, {}), {2}: (6, {}), {3}: (7, {}), {4}... | custom-call | flops 67108864 | tf_op jit(solution)/shard_map/inner/pallas_call | solution.py:791
  22.9 0.4 %collective-permute-done.4.refs_5_.refs_6_ = f32[304,128]{1,0:T(8,128)S(1)} collective-permute-done((f32[304,128]{1,0:T(8,128)S(1)}, f32[304,128]{1,0:T(8,128)S(1)}, u32[]{:S(2)}, u32[]{:S(2)}) %collective-permute-start.4) | collective-permute-done | bytes 155680 | tf_op jit(solution)/shard_map/ppermute | solution.py:725
  23.3 2.9 %outer.1 = (f32[2560,128]{1,0:T(8,128)}, s32[20,56,128]{2,1,0:T(8,128)S(1)}, f32[16,40,128]{2,1,0:T(8,128)S(1)}, s32[20,56,128]{2,1,0:T(8,128)S(1)}, f32[6,20,56...) custom-call(f32[2560,128]{1,0:T(8,128)S(1)} %get-tuple-element.38.u., ...), custom_call_target="tpu_custom_call", output_to_operand_aliasing={{1}: (7, {}), {2}: (8, {}), {3}: (9, {}), {4}: (10, {}), {5... | custom-call | flops 33554432 | tf_op jit(solution)/shard_map/outer/pallas_call | solution.py:801
Async XLA Ops:
  2.2 4.3 %collective-permute-start.1 = (f32[64,128]{1,0:T(8,128)S(1)}, f32[64,128]{1,0:T(8,128)S(1)}, u32[]{:S(2)}, u32[]{:S(2)}) collective-permute-start(f32[64,128]{1,0:T(8,128)S(1)} %get-tuple-element.40.zp), channel_id=1, source_target_pairs={{0,3},{1,2},{2,1},{3,0},{4,7},{5,6},{6,5},{7,4},{8,11},{9,10},{10,... | collective-permute-start | bytes 98312 | tf_op jit(solution)/shard_map/ppermute | solution.py:725
  4.7 1.8 %collective-permute-start = (f32[64,128]{1,0:T(8,128)S(1)}, f32[64,128]{1,0:T(8,128)S(1)}, u32[]{:S(2)}, u32[]{:S(2)}) collective-permute-start(f32[64,128]{1,0:T(8,128)S(1)} %get-tuple-element.40.zp), channel_id=1, source_target_pairs={{0,1},{1,0},{2,3},{3,2},{4,5},{5,4},{6,7},{7,6},{8,9},{9,8},{10,11... | collective-permute-start | bytes 98312 | tf_op jit(solution)/shard_map/ppermute | solution.py:725
  6.6 6.7 %collective-permute-start.2 = (f32[136,128]{1,0:T(8,128)S(1)}, f32[136,128]{1,0:T(8,128)S(1)}, u32[]{:S(2)}, u32[]{:S(2)}) collective-permute-start(f32[136,128]{1,0:T(8,128)S(1)} %get-tuple-element.47), channel_id=1, source_target_pairs={{0,4},{1,5},{2,6},{3,7},{4,0},{5,1},{6,2},{7,3},{8,12},{9,13},{10,... | collective-permute-start | bytes 208904 | tf_op jit(solution)/shard_map/ppermute | solution.py:725
  9.1 5.2 %collective-permute-start.3 = (f32[136,128]{1,0:T(8,128)S(1)}, f32[136,128]{1,0:T(8,128)S(1)}, u32[]{:S(2)}, u32[]{:S(2)}) collective-permute-start(f32[136,128]{1,0:T(8,128)S(1)} %get-tuple-element.48), channel_id=1, source_target_pairs={{0,12},{1,13},{2,14},{3,15},{4,8},{5,9},{6,10},{7,11},{8,4},{9,5},... | collective-permute-start | bytes 208904 | tf_op jit(solution)/shard_map/ppermute | solution.py:725
  14.4 8.9 %collective-permute-start.4 = (f32[304,128]{1,0:T(8,128)S(1)}, f32[304,128]{1,0:T(8,128)S(1)}, u32[]{:S(2)}, u32[]{:S(2)}) collective-permute-start(f32[304,128]{1,0:T(8,128)S(1)} %get-tuple-element.61), channel_id=1, source_target_pairs={{0,16},{1,17},{2,18},{3,19},{4,20},{5,21},{6,22},{7,23},{8,24},{9,... | collective-permute-start | bytes 466952 | tf_op jit(solution)/shard_map/ppermute | solution.py:725

commit v9 on v8

--- a/solution.py
+++ b/solution.py
@@ -103,7 +103,7 @@
     return value[:n] if part == OWN else jnp.concatenate([value[n - 8 :], value[:8]], axis=0)
 
 
-def pack_kernel(cx, cy, u_in, vf_in, mask_in, code_in, zp, u, vf, c, mask, code, sems):
+def pack_kernel(cx, cy, u_in, vf_in, mask_in, code_in, zp, z_a, z_b, u, vf, c, mask, code, sems):
     copies = [
         pltpu.make_async_copy(mask_in, mask, sems.at[0]),
         pltpu.make_async_copy(code_in, code, sems.at[1]),
@@ -139,6 +139,13 @@
                     part = jnp.where(low_lane, roll(c[rows, :], 2 * m - 1), roll(c[rows, :], 2 * m + 1))
                 acc = jnp.where(slot == m, part, acc)
         zp[g * cy : (g + 1) * cy, :] = acc
+        if g:
+            second = acc
+    high = jnp.where(low_lane, roll(second, 1), acc)
+    low = jnp.where(low_lane, acc, roll(second, -1))
+    odd = place()[2] % 2 == 1
+    z_a[...] = jnp.where(odd, low, high)
+    z_b[...] = jnp.where(odd, high, low)
 
 
 def faces_kernel(cx, cy, two_x, u, vf, c, cw, y_a, y_b, *xs):
@@ -186,13 +193,13 @@
     lane = lanes_of((cy, 128))
     low_lane = (lane & 1) == 0
     codes = (lane >= 63) & (lane <= 126)
+    a, b = r_a[...], r_b[...]
+    below, above = jnp.where(odd, a, b), jnp.where(odd, b, a)
     for g in range(2):
-        rows = slice(g * cy, (g + 1) * cy)
-        a, b = r_a[rows, :], r_b[rows, :]
         edge = jnp.where(codes, EDGE, 0.0) if g else jnp.zeros((cy, 128), jnp.float32)
-        low = jnp.where(bz > 0, roll(jnp.where(odd, a, b), 1), edge)
-        high = jnp.where(bz < NBZ - 1, roll(jnp.where(odd, b, a), -1), edge)
-        zh[rows, :] = jnp.where(low_lane, low, high)
+        low = jnp.where(bz > 0, below if g else roll(below, 1), edge)
+        high = jnp.where(bz < NBZ - 1, above if g else roll(above, -1), edge)
+        zh[g * cy : (g + 1) * cy, :] = jnp.where(low_lane, low, high)
     zh[2 * cy :, :] = zp[...]
     n = NF * cx
 
@@ -467,7 +474,7 @@
             halo = roll(r.dz[f, 8 * t : 8 * t + 8, :], back)
             total = base[f] + jnp.where(first_lane, halo, roll(up[f], 1))
             total = total + jnp.where(last_lane, halo, roll(down[f], -1))
-            out[pl.ds(pl.multiple_of((f * cx + x) * cy + 8 * t, 8), 8), :] = total * inverse
+            out[f, pl.ds(pl.multiple_of(x * cy + 8 * t, 8), 8), :] = total * inverse
 
 
 def common(r, part):
@@ -594,22 +601,19 @@
     rest = refs[len(names) + kept_in :]
     r = types.SimpleNamespace(cx=cx, cy=cy, **dict(zip(names, ins)))
     r.__dict__.update(zip(("out", *KEPT, *SCRATCH, "rim", "sems"), rest))
-    size = cx * cy
     bx, by, bz = place()
     todo = plan(cx, nbx, bx)
 
-    def copy(src, first, count, f, semaphore):
-        start = pl.multiple_of(f * size + first * cy, 8)
-        part = pl.ds(start, count * cy)
-        return pltpu.make_async_copy(src.at[part, :], r.out.at[part, :], r.sems.at[semaphore])
-
-    each((0, NFIELD), lambda f: copy(r.res, *todo.inner_rows, f, f).start())
+    def copy(src, first, count, semaphore):
+        part = pl.ds(pl.multiple_of(first * cy, 8), count * cy)
+        return pltpu.make_async_copy(src.at[:, part, :], r.out.at[:, part, :], r.sems.at[semaphore])
+
+    each((0, 2), lambda i: pl.when(i == 0)(lambda: copy(r.res, *todo.inner_rows, 0).start()))
 
     def finish_layer(j, first, turn):
         x = todo.at(j) - 2
         redistribute(r, x, r.rim)
-        for f in range(NFIELD):
-            copy(r.rim, x, 1, f, (turn + j - first) * NFIELD + f).start()
+        copy(r.rim, x, 1, turn + j - first).start()
 
     common(r, ALL)
     x_odd = bx % 2 == 1
@@ -686,11 +690,9 @@
     turn = 1
     for first, count in todo.outer_spread:
         for j in range(first, first + count):
-            for f in range(NFIELD):
-                copy(r.rim, todo.at(j) - 2, 1, f, turn * NFIELD + f).wait()
+            copy(r.rim, todo.at(j) - 2, 1, turn).wait()
             turn += 1
-    for f in range(NFIELD):
-        copy(r.res, *todo.inner_rows, f, f).wait()
+    copy(r.res, *todo.inner_rows, 0).wait()
 
 
 def call(kernel, ins, outs, scratch=(), name=None, grant=8, flops=0, **kwargs):
@@ -726,14 +728,14 @@
 
     n = NF * cx
     copies = 2 if two_x else 1
-    zp, u, vf, c = call(
+    zp, za, zb, u, vf, c = call(
         functools.partial(pack_kernel, cx, cy),
         [far] * 4,
-        [vmem(2 * cy), vmem(NFIELD * cells), vmem(cells), vmem(cells)],
+        [vmem(2 * cy), vmem(cy), vmem(cy), vmem(NFIELD * cells), vmem(cells), vmem(cells)],
         [vmem(cells, dtype=i32), vmem(cells, dtype=i32), pltpu.SemaphoreType.DMA((3 + NFIELD,))],
         "pack",
     )(*(pltpu.with_memory_space_constraint(a, pltpu.HBM) for a in (u, vf, mask, code)))
-    za, zb = swap(zp, 1, NBZ, False), swap(zp, 1, NBZ, True)
+    za, zb = swap(za, 1, NBZ, False), swap(zb, 1, NBZ, True)
     rows, ring, layers = cy + 8, cy + 24, cx + 4
     cw, ya, yb, *xs = call(
         functools.partial(faces_kernel, cx, cy, two_x),
@@ -791,7 +793,7 @@
     *state, res = call(
         functools.partial(inner_kernel, cx, cy, nbx),
         [on_chip] * (4 + len(kept)),
-        kept + [vmem(NFIELD * cells)],
+        kept + [vmem(NFIELD, cells)],
         scratch,
         "inner",
         flops=1 << 26,
@@ -801,8 +803,8 @@
     out, *_ = call(
         functools.partial(outer_kernel, cx, cy, nbx),
         [on_chip] * (first + len(kept)),
-        [pltpu.HBM((NFIELD * cells, cz), f32)] + kept,
-        scratch + [vmem(NFIELD * cells), pltpu.SemaphoreType.DMA((7 * NFIELD,))],
+        [pltpu.HBM((NFIELD, cells, cz), f32)] + kept,
+        scratch + [vmem(NFIELD, cells), pltpu.SemaphoreType.DMA((7,))],
         "outer",
         flops=1 << 25,
         input_output_aliases={first + i: 1 + i for i in range(len(kept))},

time: 26.4 us -> 26 us (0.985)
  starting transfers between devices: 9.82 us -> 9.07 us
  waiting for transfers between devices: 2.19 us -> 2.81 us
    ppermute x5, starting transfers between devices: 9.82 us -> 9.07 us  [swap(): return lax.ppermute(value, AXIS, pairing(stride, extent, devices, odd))]
    ppermute x5, waiting for transfers between devices: 2.19 us -> 2.81 us  [swap(): return lax.ppermute(value, AXIS, pairing(stride, extent, devices, odd))]
where the time goes in v9:
time: 26 us; the launch traced here: 25.9 us
  Pallas kernels  14 us (54%)
  starting transfers between devices  9.07 us (35%)
  waiting for transfers between devices  2.81 us (11%)
    ppermute x5, starting transfers between devices, swap(): return lax.ppermute(value, AXIS, pairing(stride, extent, devices, odd))  9.07 us
    pallas_call x1, Pallas kernels, per_device(): call(functools.partial(inner_kernel, cx, cy, nbx), [on_chip] * (4 + len(k...  5.86 us
    ppermute x5, waiting for transfers between devices, swap(): return lax.ppermute(value, AXIS, pairing(stride, extent, devices, odd))  2.81 us
    pallas_call x1, Pallas kernels, per_device(): call(functools.partial(early_kernel, cx, cy, nbx), [on_chip] * 4, kept +...  2.66 us
    pallas_call x1, Pallas kernels, per_device(): call(functools.partial(outer_kernel, cx, cy, nbx), [on_chip] * (first + l...  2.65 us
    pallas_call x1, Pallas kernels, per_device(): call(functools.partial(pack_kernel, cx, cy), [far] * 4, [vmem(2 * cy), vm...  2.25 us
  transfers between devices with their start and end apart: 5, of which 3 were waited for; matrix products, arithmetic and copies ran while one was open for 0% of the time, Pallas kernels for 34%

profile of v9, /device:TPU:0, one launch (start us, length us, event | category | flops | bytes accessed | tf_op | source)
XLA Modules:
  0.0 25.9 jit_solution(16946482932741409552)
XLA Ops:
  0.0 2.2 %pack.1 = (f32[64,128]{1,0:T(8,128)S(1)}, f32[32,128]{1,0:T(8,128)S(1)}, f32[32,128]{1,0:T(8,128)S(1)}, f32[2560,128]{1,0:T(8,128)S(1)}, f32[512,128]{1,0:T(8,128)S(1)}, /*index=5*/f32[512,128]{1,0:T(8,128)S(1)}) custom-call(f32[2560,128]{1,0:T(8,128)} %bitcast.5, f32[512,128]{1,0:T(8,128)} %bitcast.6, s32[512,128]{1,0:T(8,128)} %bitcast.7, s32[512,128]{1,0:T(8,128)} %bitcast.8), custom_call_target="tpu_custom_call" | custom-call | tf_op jit(solution)/shard_map/pack/pallas_call | solution.py:731
  2.3 0.6 %collective-permute-start = (f32[32,128]{1,0:T(8,128)S(1)}, f32[32,128]{1,0:T(8,128)S(1)}, u32[]{:S(2)}, u32[]{:S(2)}) collective-permute-start(f32[32,128]{1,0:T(8,128)S(1)} %get-tuple-element.42), channel_id=1, source_target_pairs={{0,1},{1,0},{2,3},{3,2},{4,5},{5,4},{6,7},{7,6},{8,9},{9,8},{10,11... | collective-permute-start | bytes 49160 | tf_op jit(solution)/shard_map/ppermute | solution.py:727
  2.8 2.6 %collective-permute-start.1 = (f32[32,128]{1,0:T(8,128)S(1)}, f32[32,128]{1,0:T(8,128)S(1)}, u32[]{:S(2)}, u32[]{:S(2)}) collective-permute-start(f32[32,128]{1,0:T(8,128)S(1)} %get-tuple-element.43), channel_id=1, source_target_pairs={{0,3},{1,2},{2,1},{3,0},{4,7},{5,6},{6,5},{7,4},{8,11},{9,10},{10,... | collective-permute-start | bytes 49160 | tf_op jit(solution)/shard_map/ppermute | solution.py:727
  5.4 0.3 %faces.1 = (s32[20,56,128]{2,1,0:T(8,128)S(1)}, f32[128,128]{1,0:T(8,128)S(1)}, f32[128,128]{1,0:T(8,128)S(1)}, f32[256,128]{1,0:T(8,128)S(1)}) custom-call(f32[2560,128]{1,0:T(8,128)S(1)} %get-tuple-element.40.u.refs_0_, f32[512,128]{1,0:T(8,128)S(1)} %get-tuple-element.41.vf.refs_1_, f32[512,128]{1,0:T(8,128)S(1)} %get-tuple-element.45.c), custom_call_target="tpu_custom_call" | custom-call | flops 1048576 | tf_op jit(solution)/shard_map/faces/pallas_call | solution.py:740
  5.8 0.0 collective-permute-done.r_a
  5.8 1.1 %collective-permute-done.1.r_b = f32[32,128]{1,0:T(8,128)S(1)} collective-permute-done((f32[32,128]{1,0:T(8,128)S(1)}, f32[32,128]{1,0:T(8,128)S(1)}, u32[]{:S(2)}, u32[]{:S(2)}) %collective-permute-start.1) | collective-permute-done | bytes 16416 | tf_op jit(solution)/shard_map/ppermute | solution.py:727
  6.8 0.1 z_merge.1
  6.9 1.8 %collective-permute-start.2 = (f32[136,128]{1,0:T(8,128)S(1)}, f32[136,128]{1,0:T(8,128)S(1)}, u32[]{:S(2)}, u32[]{:S(2)}) collective-permute-start(f32[136,128]{1,0:T(8,128)S(1)} %get-tuple-element.51), channel_id=1, source_target_pairs={{0,4},{1,5},{2,6},{3,7},{4,0},{5,1},{6,2},{7,3},{8,12},{9,13},{10,... | collective-permute-start | bytes 208904 | tf_op jit(solution)/shard_map/ppermute | solution.py:727
  8.7 1.5 %collective-permute-start.3 = (f32[136,128]{1,0:T(8,128)S(1)}, f32[136,128]{1,0:T(8,128)S(1)}, u32[]{:S(2)}, u32[]{:S(2)}) collective-permute-start(f32[136,128]{1,0:T(8,128)S(1)} %get-tuple-element.52), channel_id=1, source_target_pairs={{0,12},{1,13},{2,14},{3,15},{4,8},{5,9},{6,10},{7,11},{8,4},{9,5},... | collective-permute-start | bytes 208904 | tf_op jit(solution)/shard_map/ppermute | solution.py:727
  10.2 2.7 %early.1 = (s32[20,56,128]{2,1,0:T(8,128)S(1)}, f32[16,40,128]{2,1,0:T(8,128)S(1)}, s32[20,56,128]{2,1,0:T(8,128)S(1)}, f32[6,20,56,128]{3,2,1,0:T(8,128)S(1)}, ...) custom-call(f32[2560,128]{1,0:T(8,128)S(1)} %get-tuple-element.40.u., ...), custom_call_target="tpu_custom_call", output_to_operand_aliasing={{0}: (3, {})} | custom-call | flops 16777216 | tf_op jit(solution)/shard_map/early/pallas_call | solution.py:775
  12.9 0.0 collective-permute-done.2.r_a
  12.9 1.0 %collective-permute-done.3.r_b = f32[136,128]{1,0:T(8,128)S(1)} collective-permute-done((f32[136,128]{1,0:T(8,128)S(1)}, f32[136,128]{1,0:T(8,128)S(1)}, u32[]{:S(2)}, u32[]{:S(2)}) %collective-permute-start.3) | collective-permute-done | bytes 69664 | tf_op jit(solution)/shard_map/ppermute | solution.py:727
  13.9 0.1 y_merge.1
  14.0 2.6 %collective-permute-start.4 = (f32[304,128]{1,0:T(8,128)S(1)}, f32[304,128]{1,0:T(8,128)S(1)}, u32[]{:S(2)}, u32[]{:S(2)}) collective-permute-start(f32[304,128]{1,0:T(8,128)S(1)} %get-tuple-element.65), channel_id=1, source_target_pairs={{0,16},{1,17},{2,18},{3,19},{4,20},{5,21},{6,22},{7,23},{8,24},{9,... | collective-permute-start | bytes 466952 | tf_op jit(solution)/shard_map/ppermute | solution.py:727
  16.7 5.9 %inner.1 = (s32[20,56,128]{2,1,0:T(8,128)S(1)}, f32[16,40,128]{2,1,0:T(8,128)S(1)}, s32[20,56,128]{2,1,0:T(8,128)S(1)}, f32[6,20,56,128]{3,2,1,0:T(8,128)S(1)}, ...) custom-call(f32[2560,128]{1,0:T(8,128)S(1)} %get-tuple-element.40.u., ...), custom_call_target="tpu_custom_call", output_to_operand_aliasing={{0}: (4, {}), {1}: (5, {}), {2}: (6, {}), {3}: (7, {}), {4}... | custom-call | flops 67108864 | tf_op jit(solution)/shard_map/inner/pallas_call | solution.py:793
  22.5 0.7 %collective-permute-done.4.refs_5_.refs_6_ = f32[304,128]{1,0:T(8,128)S(1)} collective-permute-done((f32[304,128]{1,0:T(8,128)S(1)}, f32[304,128]{1,0:T(8,128)S(1)}, u32[]{:S(2)}, u32[]{:S(2)}) %collective-permute-start.4) | collective-permute-done | bytes 155680 | tf_op jit(solution)/shard_map/ppermute | solution.py:727
  23.2 2.7 %outer.1 = (f32[5,512,128]{2,1,0:T(8,128)}, s32[20,56,128]{2,1,0:T(8,128)S(1)}, f32[16,40,128]{2,1,0:T(8,128)S(1)}, s32[20,56,128]{2,1,0:T(8,128)S(1)}, f32[6,20...) custom-call(f32[2560,128]{1,0:T(8,128)S(1)} %get-tuple-element.40.u., ...), custom_call_target="tpu_custom_call", output_to_operand_aliasing={{1}: (7, {}), {2}: (8, {}), {3}: (9, {}), {4}: (10, {}), {5... | custom-call | flops 33554432 | tf_op jit(solution)/shard_map/outer/pallas_call | solution.py:803
Async XLA Ops:
  2.3 3.5 %collective-permute-start = (f32[32,128]{1,0:T(8,128)S(1)}, f32[32,128]{1,0:T(8,128)S(1)}, u32[]{:S(2)}, u32[]{:S(2)}) collective-permute-start(f32[32,128]{1,0:T(8,128)S(1)} %get-tuple-element.42), channel_id=1, source_target_pairs={{0,1},{1,0},{2,3},{3,2},{4,5},{5,4},{6,7},{7,6},{8,9},{9,8},{10,11... | collective-permute-start | bytes 49160 | tf_op jit(solution)/shard_map/ppermute | solution.py:727
  2.8 4.0 %collective-permute-start.1 = (f32[32,128]{1,0:T(8,128)S(1)}, f32[32,128]{1,0:T(8,128)S(1)}, u32[]{:S(2)}, u32[]{:S(2)}) collective-permute-start(f32[32,128]{1,0:T(8,128)S(1)} %get-tuple-element.43), channel_id=1, source_target_pairs={{0,3},{1,2},{2,1},{3,0},{4,7},{5,6},{6,5},{7,4},{8,11},{9,10},{10,... | collective-permute-start | bytes 49160 | tf_op jit(solution)/shard_map/ppermute | solution.py:727
  6.9 6.0 %collective-permute-start.2 = (f32[136,128]{1,0:T(8,128)S(1)}, f32[136,128]{1,0:T(8,128)S(1)}, u32[]{:S(2)}, u32[]{:S(2)}) collective-permute-start(f32[136,128]{1,0:T(8,128)S(1)} %get-tuple-element.51), channel_id=1, source_target_pairs={{0,4},{1,5},{2,6},{3,7},{4,0},{5,1},{6,2},{7,3},{8,12},{9,13},{10,... | collective-permute-start | bytes 208904 | tf_op jit(solution)/shard_map/ppermute | solution.py:727
  8.7 5.2 %collective-permute-start.3 = (f32[136,128]{1,0:T(8,128)S(1)}, f32[136,128]{1,0:T(8,128)S(1)}, u32[]{:S(2)}, u32[]{:S(2)}) collective-permute-start(f32[136,128]{1,0:T(8,128)S(1)} %get-tuple-element.52), channel_id=1, source_target_pairs={{0,12},{1,13},{2,14},{3,15},{4,8},{5,9},{6,10},{7,11},{8,4},{9,5},... | collective-permute-start | bytes 208904 | tf_op jit(solution)/shard_map/ppermute | solution.py:727
  14.0 9.2 %collective-permute-start.4 = (f32[304,128]{1,0:T(8,128)S(1)}, f32[304,128]{1,0:T(8,128)S(1)}, u32[]{:S(2)}, u32[]{:S(2)}) collective-permute-start(f32[304,128]{1,0:T(8,128)S(1)} %get-tuple-element.65), channel_id=1, source_target_pairs={{0,16},{1,17},{2,18},{3,19},{4,20},{5,21},{6,22},{7,23},{8,24},{9,... | collective-permute-start | bytes 466952 | tf_op jit(solution)/shard_map/ppermute | solution.py:727

commit v10 on v9

--- a/solution.py
+++ b/solution.py
@@ -7,6 +7,7 @@
 from jax.experimental import pallas as pl
 from jax.experimental.pallas import tpu as pltpu
 from jax.sharding import PartitionSpec as P
+
 
 NBY = 4
 NBZ = 4
@@ -112,7 +113,7 @@
     for f in range(NFIELD):
         rows = pl.ds(f * cx * cy, cx * cy)
         copies.append(pltpu.make_async_copy(u_in.at[rows, :], u.at[rows, :], sems.at[3 + f]))
-    for copy in copies:
+    for copy in copies[:3] + copies[:2:-1]:
         copy.start()
     lane = lanes_of((cy, 128))
     slot = ((lane + 1) & 127) >> 1
@@ -149,7 +150,7 @@
 
 
 def faces_kernel(cx, cy, two_x, u, vf, c, cw, y_a, y_b, *xs):
-    bx, by, bz = place()
+    bx, by, _ = place()
     for x in range(cx):
         cw[x + 2, 8 : 8 + cy, :] = decode(c[x * cy : (x + 1) * cy, :].astype(jnp.int32))
 
@@ -188,7 +189,7 @@
 
 
 def z_merge_kernel(cx, cy, r_a, r_b, zp, ya_in, yb_in, zh, y_a, y_b):
-    bx, by, bz = place()
+    _, by, bz = place()
     odd = bz % 2 == 1
     lane = lanes_of((cy, 128))
     low_lane = (lane & 1) == 0
@@ -226,7 +227,7 @@
 def y_merge_kernel(cx, cy, two_x, ended, r_a, r_b, zh, *refs):
     copies = 2 if two_x else 1
     mains, (y_lo, y_hi), xs = refs[:copies], refs[copies : copies + 2], refs[copies + 2 :]
-    bx, by, bz = place()
+    bx, by, _ = place()
     odd = by % 2 == 1
     edge = z_edge_rows(cx)
     a, b = r_a[...], r_b[...]
@@ -444,7 +445,7 @@
 
 
 def redistribute(r, x, out):
-    cx, cy = r.cx, r.cy
+    cy = r.cy
     layer = x + 2
     back = -2 * layer
     lane = lanes_of((8, 128))
@@ -550,7 +551,7 @@
     names = ("u", "vf", "zh", "cw_in", *KEPT, "ended", *SCRATCH)
     r = types.SimpleNamespace(cx=cx, cy=cy, **dict(zip(names, refs)))
     common(r, OWN)
-    bx, by, bz = place()
+    bx, _, _ = place()
     todo = plan(cx, nbx, bx)
     set_outside(r, nbx, bx)
     z_fields(r, slice(0, cy), lambda g: r.zh[g * cy : (g + 1) * cy, :])
@@ -574,7 +575,7 @@
     r = types.SimpleNamespace(cx=cx, cy=cy, **dict(zip(names, refs)))
     r.__dict__.update(zip((*KEPT, "res", *SCRATCH), rest))
     common(r, ALL)
-    bx, by, bz = place()
+    bx, _, _ = place()
     todo = plan(cx, nbx, bx)
     set_outside(r, nbx, bx)
     r.ht[...] = jnp.zeros(r.ht.shape, jnp.float32)
@@ -601,7 +602,7 @@
     rest = refs[len(names) + kept_in :]
     r = types.SimpleNamespace(cx=cx, cy=cy, **dict(zip(names, ins)))
     r.__dict__.update(zip(("out", *KEPT, *SCRATCH, "rim", "sems"), rest))
-    bx, by, bz = place()
+    bx, _, _ = place()
     todo = plan(cx, nbx, bx)
 
     def copy(src, first, count, semaphore):
@@ -695,14 +696,13 @@
     copy(r.res, *todo.inner_rows, 0).wait()
 
 
-def call(kernel, ins, outs, scratch=(), name=None, grant=8, flops=0, **kwargs):
+def call(kernel, ins, outs, scratch=(), grant=8, flops=0, **kwargs):
     return pl.pallas_call(
         kernel,
         in_specs=ins,
         out_specs=tuple(pl.BlockSpec(memory_space=o.memory_space) for o in outs),
         out_shape=tuple(outs),
         scratch_shapes=scratch,
-        name=name,
         cost_estimate=pl.CostEstimate(flops=flops, transcendentals=0, bytes_accessed=0),
         compiler_params=pltpu.CompilerParams(vmem_limit_bytes=grant << 20),
         **kwargs,
@@ -733,7 +733,6 @@
         [far] * 4,
         [vmem(2 * cy), vmem(cy), vmem(cy), vmem(NFIELD * cells), vmem(cells), vmem(cells)],
         [vmem(cells, dtype=i32), vmem(cells, dtype=i32), pltpu.SemaphoreType.DMA((3 + NFIELD,))],
-        "pack",
     )(*(pltpu.with_memory_space_constraint(a, pltpu.HBM) for a in (u, vf, mask, code)))
     za, zb = swap(za, 1, NBZ, False), swap(zb, 1, NBZ, True)
     rows, ring, layers = cy + 8, cy + 24, cx + 4
@@ -741,11 +740,10 @@
         functools.partial(faces_kernel, cx, cy, two_x),
         [on_chip] * 3,
         [vmem(layers, ring, dtype=i32), vmem(n), vmem(n)] + [vmem(NF * cy)] * copies,
-        name="faces",
         flops=1 << 20,
     )(u, vf, c)
     zh, ya, yb = call(
-        functools.partial(z_merge_kernel, cx, cy), [on_chip] * 5, [vmem(4 * cy), vmem(n + 8), vmem(n + 8)], name="z_merge"
+        functools.partial(z_merge_kernel, cx, cy), [on_chip] * 5, [vmem(4 * cy), vmem(n + 8), vmem(n + 8)]
     )(za, zb, zp, ya, yb)
     kept = [
         vmem(layers, ring, dtype=i32),
@@ -777,7 +775,6 @@
         [on_chip] * 4,
         kept + [vmem(8)],
         scratch,
-        "early",
         flops=1 << 24,
         input_output_aliases={3: 0},
     )(u, vf, zh, cw)
@@ -785,7 +782,6 @@
         functools.partial(y_merge_kernel, cx, cy, two_x),
         [on_chip] * (4 + copies),
         [vmem(n + 8), vmem(n + 8)] + [vmem(NF * cy + 48)] * copies,
-        name="y_merge",
     )(ended, ya, yb, zh, *xs)
     xs = [swap(x, NBY * NBZ, nbx, odd) for odd, x in enumerate(xs)]
     xa, xb = xs if two_x else xs * 2
@@ -795,7 +791,6 @@
         [on_chip] * (4 + len(kept)),
         kept + [vmem(NFIELD, cells)],
         scratch,
-        "inner",
         flops=1 << 26,
         input_output_aliases={4 + i: i for i in range(len(kept))},
     )(u, vf, y_lo, y_hi, *state)
@@ -805,7 +800,6 @@
         [on_chip] * (first + len(kept)),
         [pltpu.HBM((NFIELD, cells, cz), f32)] + kept,
         scratch + [vmem(NFIELD, cells), pltpu.SemaphoreType.DMA((7,))],
-        "outer",
         flops=1 << 25,
         input_output_aliases={first + i: 1 + i for i in range(len(kept))},
     )(u, vf, y_lo, y_hi, res, xa, xb, *state)

time: 26 us -> 26 us (level)
  no operation moved by 1% of the time
where the time goes in v10:
time: 26 us; the launch traced here: 25.8 us
  Pallas kernels  13.9 us (53%)
  starting transfers between devices  9.07 us (35%)
  waiting for transfers between devices  2.81 us (11%)
    ppermute x5, starting transfers between devices, swap(): return lax.ppermute(value, AXIS, pairing(stride, extent, devices, odd))  9.07 us
    pallas_call x1, Pallas kernels, per_device(): call(functools.partial(inner_kernel, cx, cy, nbx), [on_chip] * (4 + len(k...  5.86 us
    ppermute x5, waiting for transfers between devices, swap(): return lax.ppermute(value, AXIS, pairing(stride, extent, devices, odd))  2.81 us
    pallas_call x1, Pallas kernels, per_device(): call(functools.partial(early_kernel, cx, cy, nbx), [on_chip] * 4, kept +...  2.66 us
    pallas_call x1, Pallas kernels, per_device(): call(functools.partial(outer_kernel, cx, cy, nbx), [on_chip] * (first + l...  2.65 us
    pallas_call x1, Pallas kernels, per_device(): call(functools.partial(pack_kernel, cx, cy), [far] * 4, [vmem(2 * cy), vm...  2.18 us
  transfers between devices with their start and end apart: 5, of which 3 were waited for; matrix products, arithmetic and copies ran while one was open for 0% of the time, Pallas kernels for 34%

profile of v10, /device:TPU:0, one launch (start us, length us, event | category | flops | bytes accessed | tf_op | source)
XLA Modules:
  0.0 25.8 jit_solution(2641035786672528361)
XLA Ops:
  0.0 2.2 %shard_map.46 = (f32[64,128]{1,0:T(8,128)S(1)}, f32[32,128]{1,0:T(8,128)S(1)}, f32[32,128]{1,0:T(8,128)S(1)}, f32[2560,128]{1,0:T(8,128)S(1)}, f32[512,128]{1,0:T(8,128)S(1)}, /*index=5*/f32[512,128]{1,0:T(8,128)S(1)}) custom-call(f32[2560,128]{1,0:T(8,128)} %bitcast.5, f32[512,128]{1,0:T(8,128)} %bitcast.6, s32[512,128]{1,0:T(8,128)} %bitcast.7, ...), custom_call_target="tpu_custom_call" | custom-call | tf_op jit(solution)/shard_map/pallas_call | solution.py:731
  2.2 0.6 %collective-permute-start = (f32[32,128]{1,0:T(8,128)S(1)}, f32[32,128]{1,0:T(8,128)S(1)}, u32[]{:S(2)}, u32[]{:S(2)}) collective-permute-start(f32[32,128]{1,0:T(8,128)S(1)} %get-tuple-element.42), channel_id=1, source_target_pairs={{0,1},{1,0},{2,3},{3,2},{4,5},{5,4},{6,7},{7,6},{8,9},{9,8},{10,11... | collective-permute-start | bytes 49160 | tf_op jit(solution)/shard_map/ppermute | solution.py:727
  2.7 2.6 %collective-permute-start.1 = (f32[32,128]{1,0:T(8,128)S(1)}, f32[32,128]{1,0:T(8,128)S(1)}, u32[]{:S(2)}, u32[]{:S(2)}) collective-permute-start(f32[32,128]{1,0:T(8,128)S(1)} %get-tuple-element.43), channel_id=1, source_target_pairs={{0,3},{1,2},{2,1},{3,0},{4,7},{5,6},{6,5},{7,4},{8,11},{9,10},{10,... | collective-permute-start | bytes 49160 | tf_op jit(solution)/shard_map/ppermute | solution.py:727
  5.3 0.3 %shard_map.47 = (s32[20,56,128]{2,1,0:T(8,128)S(1)}, f32[128,128]{1,0:T(8,128)S(1)}, f32[128,128]{1,0:T(8,128)S(1)}, f32[256,128]{1,0:T(8,128)S(1)}) custom-call(f32[2560,128]{1,0:T(8,128)S(1)} %get-tuple-element.40.u.refs_0_, f32[512,128]{1,0:T(8,128)S(1)} %get-tuple-element.41.vf.refs_1_, f32[512,128]{1,0:T(8,128)S(1)} %get-tuple-element.45.c), custom_call_target="tpu_custom_call" | custom-call | flops 1048576 | tf_op jit(solution)/shard_map/pallas_call | solution.py:739
  5.7 0.0 collective-permute-done.r_a
  5.7 1.1 %collective-permute-done.1.r_b = f32[32,128]{1,0:T(8,128)S(1)} collective-permute-done((f32[32,128]{1,0:T(8,128)S(1)}, f32[32,128]{1,0:T(8,128)S(1)}, u32[]{:S(2)}, u32[]{:S(2)}) %collective-permute-start.1) | collective-permute-done | bytes 16416 | tf_op jit(solution)/shard_map/ppermute | solution.py:727
  6.8 0.1 shard_map.48
  6.9 1.8 %collective-permute-start.2 = (f32[136,128]{1,0:T(8,128)S(1)}, f32[136,128]{1,0:T(8,128)S(1)}, u32[]{:S(2)}, u32[]{:S(2)}) collective-permute-start(f32[136,128]{1,0:T(8,128)S(1)} %get-tuple-element.51), channel_id=1, source_target_pairs={{0,4},{1,5},{2,6},{3,7},{4,0},{5,1},{6,2},{7,3},{8,12},{9,13},{10,... | collective-permute-start | bytes 208904 | tf_op jit(solution)/shard_map/ppermute | solution.py:727
  8.6 1.5 %collective-permute-start.3 = (f32[136,128]{1,0:T(8,128)S(1)}, f32[136,128]{1,0:T(8,128)S(1)}, u32[]{:S(2)}, u32[]{:S(2)}) collective-permute-start(f32[136,128]{1,0:T(8,128)S(1)} %get-tuple-element.52), channel_id=1, source_target_pairs={{0,12},{1,13},{2,14},{3,15},{4,8},{5,9},{6,10},{7,11},{8,4},{9,5},... | collective-permute-start | bytes 208904 | tf_op jit(solution)/shard_map/ppermute | solution.py:727
  10.2 2.7 %shard_map.49 = (s32[20,56,128]{2,1,0:T(8,128)S(1)}, f32[16,40,128]{2,1,0:T(8,128)S(1)}, s32[20,56,128]{2,1,0:T(8,128)S(1)}, f32[6,20,56,128]{3,2,1,0:T(8,128)S(...) custom-call(f32[2560,128]{1,0:T(8,128)S(1)} %get-tuple-element.40.u., ...), custom_call_target="tpu_custom_call", output_to_operand_aliasing={{0}: (3, {})} | custom-call | flops 16777216 | tf_op jit(solution)/shard_map/pallas_call | solution.py:773
  12.8 0.0 collective-permute-done.2.r_a
  12.8 1.0 %collective-permute-done.3.r_b = f32[136,128]{1,0:T(8,128)S(1)} collective-permute-done((f32[136,128]{1,0:T(8,128)S(1)}, f32[136,128]{1,0:T(8,128)S(1)}, u32[]{:S(2)}, u32[]{:S(2)}) %collective-permute-start.3) | collective-permute-done | bytes 69664 | tf_op jit(solution)/shard_map/ppermute | solution.py:727
  13.9 0.1 shard_map.50
  14.0 2.6 %collective-permute-start.4 = (f32[304,128]{1,0:T(8,128)S(1)}, f32[304,128]{1,0:T(8,128)S(1)}, u32[]{:S(2)}, u32[]{:S(2)}) collective-permute-start(f32[304,128]{1,0:T(8,128)S(1)} %get-tuple-element.65), channel_id=1, source_target_pairs={{0,16},{1,17},{2,18},{3,19},{4,20},{5,21},{6,22},{7,23},{8,24},{9,... | collective-permute-start | bytes 466952 | tf_op jit(solution)/shard_map/ppermute | solution.py:727
  16.6 5.9 %shard_map.51 = (s32[20,56,128]{2,1,0:T(8,128)S(1)}, f32[16,40,128]{2,1,0:T(8,128)S(1)}, s32[20,56,128]{2,1,0:T(8,128)S(1)}, f32[6,20,56,128]{3,2,1,0:T(8,128)S(...) custom-call(f32[2560,128]{1,0:T(8,128)S(1)} %get-tuple-element.40.u., ...), custom_call_target="tpu_custom_call", output_to_operand_aliasing={{0}: (4, {}), {1}: (5, {}), {2}: (6, {}), {3}: (7, {}), {4}... | custom-call | flops 67108864 | tf_op jit(solution)/shard_map/pallas_call | solution.py:789
  22.5 0.7 %collective-permute-done.4.refs_5_.refs_6_ = f32[304,128]{1,0:T(8,128)S(1)} collective-permute-done((f32[304,128]{1,0:T(8,128)S(1)}, f32[304,128]{1,0:T(8,128)S(1)}, u32[]{:S(2)}, u32[]{:S(2)}) %collective-permute-start.4) | collective-permute-done | bytes 155680 | tf_op jit(solution)/shard_map/ppermute | solution.py:727
  23.2 2.7 %shard_map.52 = (f32[5,512,128]{2,1,0:T(8,128)}, s32[20,56,128]{2,1,0:T(8,128)S(1)}, f32[16,40,128]{2,1,0:T(8,128)S(1)}, s32[20,56,128]{2,1,0:T(8,128)S(1)}, f32...) custom-call(f32[2560,128]{1,0:T(8,128)S(1)} %get-tuple-element.40.u., ...), custom_call_target="tpu_custom_call", output_to_operand_aliasing={{1}: (7, {}), {2}: (8, {}), {3}: (9, {}), {4}: (10, {}), {5... | custom-call | flops 33554432 | tf_op jit(solution)/shard_map/pallas_call | solution.py:798
Async XLA Ops:
  2.2 3.5 %collective-permute-start = (f32[32,128]{1,0:T(8,128)S(1)}, f32[32,128]{1,0:T(8,128)S(1)}, u32[]{:S(2)}, u32[]{:S(2)}) collective-permute-start(f32[32,128]{1,0:T(8,128)S(1)} %get-tuple-element.42), channel_id=1, source_target_pairs={{0,1},{1,0},{2,3},{3,2},{4,5},{5,4},{6,7},{7,6},{8,9},{9,8},{10,11... | collective-permute-start | bytes 49160 | tf_op jit(solution)/shard_map/ppermute | solution.py:727
  2.7 4.0 %collective-permute-start.1 = (f32[32,128]{1,0:T(8,128)S(1)}, f32[32,128]{1,0:T(8,128)S(1)}, u32[]{:S(2)}, u32[]{:S(2)}) collective-permute-start(f32[32,128]{1,0:T(8,128)S(1)} %get-tuple-element.43), channel_id=1, source_target_pairs={{0,3},{1,2},{2,1},{3,0},{4,7},{5,6},{6,5},{7,4},{8,11},{9,10},{10,... | collective-permute-start | bytes 49160 | tf_op jit(solution)/shard_map/ppermute | solution.py:727
  6.9 6.0 %collective-permute-start.2 = (f32[136,128]{1,0:T(8,128)S(1)}, f32[136,128]{1,0:T(8,128)S(1)}, u32[]{:S(2)}, u32[]{:S(2)}) collective-permute-start(f32[136,128]{1,0:T(8,128)S(1)} %get-tuple-element.51), channel_id=1, source_target_pairs={{0,4},{1,5},{2,6},{3,7},{4,0},{5,1},{6,2},{7,3},{8,12},{9,13},{10,... | collective-permute-start | bytes 208904 | tf_op jit(solution)/shard_map/ppermute | solution.py:727
  8.6 5.2 %collective-permute-start.3 = (f32[136,128]{1,0:T(8,128)S(1)}, f32[136,128]{1,0:T(8,128)S(1)}, u32[]{:S(2)}, u32[]{:S(2)}) collective-permute-start(f32[136,128]{1,0:T(8,128)S(1)} %get-tuple-element.52), channel_id=1, source_target_pairs={{0,12},{1,13},{2,14},{3,15},{4,8},{5,9},{6,10},{7,11},{8,4},{9,5},... | collective-permute-start | bytes 208904 | tf_op jit(solution)/shard_map/ppermute | solution.py:727
  14.0 9.2 %collective-permute-start.4 = (f32[304,128]{1,0:T(8,128)S(1)}, f32[304,128]{1,0:T(8,128)S(1)}, u32[]{:S(2)}, u32[]{:S(2)}) collective-permute-start(f32[304,128]{1,0:T(8,128)S(1)} %get-tuple-element.65), channel_id=1, source_target_pairs={{0,16},{1,17},{2,18},{3,19},{4,20},{5,21},{6,22},{7,23},{8,24},{9,... | collective-permute-start | bytes 466952 | tf_op jit(solution)/shard_map/ppermute | solution.py:727
